TPU v7x, 128 devices: a whole 4x4x4 slice. The times are simulated.
128 devices in a mesh: subj: 4 (over y_lo, core), vox: 32 (over z, x, y_hi).
Axes of the slice: x: 4, y: 4 (y_hi: 2, y_lo: 2; y = y_hi * 2 + y_lo), z: 4, core: 2. Of those that a mesh axis runs over, the one named last changes fastest.
Arguments:
- series: bfloat16 [16, 256, 16384], P('subj', None, 'vox'), may hold values from -6 to 6
- offsets: int32 [16, 12], replicated, may hold values from 0 to 240
- selected: int32 [64], replicated, may hold values from 0 to 16383, as said below
Outputs:
- kernel: float32 [64, 192, 192], P('vox', 'subj')
Inputs may be any that keep to these rules, and one draw needn't show every extreme that they name: `offsets`: each epoch lies inside its subject's run; epochs may intersect. `selected`: the ids are distinct.
All inputs are finite; a program needn't handle non-finite values.
Results may differ from a plain program's by a relative error of at most 0.00035.
Values may be sent and summed in bfloat16 or wider, within the bound.
No kernel may reach another device: no remote copies, remote signals or barrier semaphores. Data moves between devices by JAX's collectives and lax.ppermute only.
A program may use at most 128 MiB of HBM per device.

v0:
```python
import jax
import jax.numpy as jnp
from jax import lax
from jax.experimental import pallas as pl
from jax.experimental.pallas import tpu as pltpu
from jax.sharding import PartitionSpec as P

TR = 16
EP = 12
GR = 4
SL = 4
SB = GR * SL
KL = 16
VOX = 16384
F32 = jnp.float32
BF16 = jnp.bfloat16
LINK = jnp.float16
series_floor = 1.0
spread_floor = 0.05
shrink_factor = 0.9


def iota(shape, dim):
    return lax.broadcasted_iota(jnp.int32, shape, dim)


def dot(a, b):
    return jnp.dot(a, b, preferred_element_type=F32)


def dot_nt(a, b):
    return lax.dot_general(a, b, (((1,), (1,)), ((), ())), preferred_element_type=F32)


def split(x):
    hi = x.astype(BF16)
    return hi, (x - hi.astype(F32)).astype(BF16)


def window_kernel(off_ref, sel_ref, series_ref, e_ref, t_ref, w_ref):
    j = lax.axis_index("subj")
    i = lax.axis_index("vox")
    width = series_ref.shape[2]
    lead = iota((TR, series_ref.shape[1]), 1) - iota((TR, series_ref.shape[1]), 0)
    for s in range(SL):
        for e in range(EP):
            chosen = lead == off_ref[j * SL + s, e]
            w_ref[e * TR : (e + 1) * TR, :] = jnp.where(chosen, 1.0, 0.0).astype(BF16)
        rows = dot(w_ref[...], series_ref[s]).astype(BF16)
        for e in range(EP):
            e_ref[e, s * TR : (s + 1) * TR, :] = rows[e * TR : (e + 1) * TR]
    row = iota((GR * KL, 128), 0)
    column = jnp.zeros((GR * KL, 128), jnp.int32)
    for r in range(GR):
        for k in range(KL):
            owner = (k // 4) * 8 + (j ^ r) * 2 + (k // 2) % 2
            column = jnp.where(row == r * KL + k, sel_ref[2 * owner + k % 2] - i * width, column)
    lane = iota((GR * KL, 128), 1)
    picker = jnp.concatenate(
        [jnp.where(column == lane + c, 1.0, 0.0).astype(BF16) for c in range(0, width, 128)], axis=1
    )
    t_ref[...] = dot_nt(picker, e_ref[...].reshape(EP * SL * TR, width)).astype(BF16)


def take_windows(series, offsets, selected):
    width = series.shape[2]
    return pl.pallas_call(
        window_kernel,
        out_shape=(
            jax.ShapeDtypeStruct((EP, SL * TR, width), BF16),
            jax.ShapeDtypeStruct((GR * KL, EP * SL * TR), BF16),
        ),
        in_specs=[
            pl.BlockSpec(memory_space=pltpu.SMEM),
            pl.BlockSpec(memory_space=pltpu.SMEM),
            pl.BlockSpec(memory_space=pltpu.VMEM),
        ],
        out_specs=(pl.BlockSpec(memory_space=pltpu.VMEM), pl.BlockSpec(memory_space=pltpu.VMEM)),
        scratch_shapes=[pltpu.VMEM((EP * TR, series.shape[1]), BF16)],
        name="windows",
    )(offsets, selected, series)


def kernel_kernel(e0, e1, e2, e3, s0, s1, s2, s3, o_ref, lh_ref, ll_ref, c_ref, n_ref, z_ref, g_ref):
    j = lax.axis_index("subj")
    epochs = (e0, e1, e2, e3)
    slabs = (s0, s1, s2, s3)
    width = e0.shape[2]
    deep = SB * TR
    chunk = SL * TR
    same = (iota((deep, deep), 0) // TR == iota((deep, deep), 1) // TR).astype(F32).astype(BF16)
    place = iota((SB, deep), 1)
    home = ((place // TR) % SL) * GR + ((place // chunk) ^ j)
    mine = iota((SB, deep), 0) == home
    gather = jnp.where(mine, 1.0, 0.0).astype(BF16)

    slab = jnp.concatenate(
        [
            jnp.concatenate([s[:, e * chunk : (e + 1) * chunk] for s in slabs], axis=1)
            for e in range(EP)
        ],
        axis=0,
    )
    centred = slab.astype(F32) - dot(slab, same) * (1.0 / TR)
    high, low = split(centred * centred)
    power = dot(high, same) + dot(low, same)
    slab_std = centred * (lax.rsqrt(power + series_floor) * shrink_factor)

    for e in range(EP):
        x = jnp.concatenate([p[e] for p in epochs], axis=0)
        xf = x.astype(F32)
        high, low = split(xf * xf)
        total = dot(gather, x)
        square = dot(gather, high) + dot(gather, low)
        n_ref[e] = lax.rsqrt(square - total * total * (1.0 / TR) + series_floor)
        for k in range(KL):
            line = jnp.where(mine, slab_std[e * KL + k : e * KL + k + 1, :], 0.0)
            lh, ll = split(line)
            lh_ref[k * SB : (k + 1) * SB, :] = lh
            ll_ref[k * SB : (k + 1) * SB, :] = ll
        c_ref[e] = dot(lh_ref[...], x) + dot(ll_ref[...], x)

    def pair(q, carry):
        for h in range(2):
            start = pl.multiple_of((q * 2 + h) * SB, SB)
            for c in range(0, width, 128):
                fisher = []
                for e in range(EP):
                    shrunk = c_ref[e, pl.ds(start, SB), c : c + 128] * n_ref[e, :, c : c + 128]
                    fisher.append(jnp.log(1.0 + shrunk) - jnp.log(1.0 - shrunk))
                mean = sum(fisher[1:], fisher[0]) * (1.0 / EP)
                fisher = [f - mean for f in fisher]
                spread = fisher[0] * fisher[0]
                for f in fisher[1:]:
                    spread = spread + f * f
                scale = lax.rsqrt(spread * (1.0 / EP) + 4.0 * spread_floor)
                for e in range(EP):
                    z_ref[h, e * SB : (e + 1) * SB, c : c + 128] = (fisher[e] * scale).astype(BF16)
            product = dot_nt(z_ref[h], z_ref[h])
            g_ref[h] = product[:, 0:128]
            g_ref[2, :, h * 64 : (h + 1) * 64] = product[:, 128 : EP * SB]
        base = (q // 2) * 8 + q % 2
        for r in range(GR):
            lines = pl.ds(r, EP * SL, stride=GR)
            both = jnp.concatenate([g_ref[n, lines, :] for n in range(3)], axis=0)
            o_ref[base + 2 * r] = both.astype(o_ref.dtype)
        return carry

    lax.fori_loop(0, KL // 2, pair, 0)


def partial_kernels(epochs, slabs, devices, dtype):
    width = epochs[0].shape[2]
    return pl.pallas_call(
        kernel_kernel,
        out_shape=jax.ShapeDtypeStruct((devices, 3 * EP * SL, 128), dtype),
        in_specs=[pl.BlockSpec(memory_space=pltpu.VMEM)] * (2 * GR),
        out_specs=pl.BlockSpec(memory_space=pltpu.VMEM),
        scratch_shapes=[
            pltpu.VMEM((KL * SB, SB * TR), BF16),
            pltpu.VMEM((KL * SB, SB * TR), BF16),
            pltpu.VMEM((EP, KL * SB, width), F32),
            pltpu.VMEM((EP, SB, width), F32),
            pltpu.VMEM((2, EP * SB, width), BF16),
            pltpu.VMEM((3, EP * SB, 128), F32),
        ],
        name="partial_kernels",
    )(*epochs, *slabs)


def order_kernel(y_ref, o_ref):
    rows = EP * SL
    cols = EP * SB
    source = iota((cols, cols), 0)
    target = (source % GR) * rows + ((source // GR) % SL) * EP + source // SB
    column = jnp.where(iota((cols, cols), 1) == target, 1.0, 0.0).astype(F32)
    source = iota((rows, rows), 1)
    line = jnp.where(iota((rows, rows), 0) == (source % SL) * EP + source // SL, 1.0, 0.0).astype(F32)
    exact = dict(precision=lax.Precision.HIGHEST, preferred_element_type=F32)
    for h in range(2):
        left = y_ref[h * rows : (h + 1) * rows, :]
        right = y_ref[2 * rows : 3 * rows, h * 64 : (h + 1) * 64]
        whole = jnp.concatenate([left, right], axis=1)
        o_ref[h] = jnp.dot(line, jnp.dot(whole, column, **exact), **exact) * (1.0 / VOX)


def in_order(tile):
    return pl.pallas_call(
        order_kernel,
        out_shape=jax.ShapeDtypeStruct((2, EP * SL, EP * SB), F32),
        in_specs=[pl.BlockSpec(memory_space=pltpu.VMEM)],
        out_specs=pl.BlockSpec(memory_space=pltpu.VMEM),
        name="in_order",
    )(tile)


def ring(step, size, stride, devices):
    def moved(n):
        place = (n // stride) % size
        return n + ((place + step) % size - place) * stride

    return [(n, moved(n)) for n in range(devices)]


def swapped(x, r):
    return lax.ppermute(x, "subj", [(n, n ^ r) for n in range(GR)])


def summed(x, size, stride, devices):
    parts = [lax.ppermute(x, "vox", ring(n, size, stride, devices)) for n in range(1, size)]
    return sum(parts, x)


def body(series, offsets, selected):
    devices = lax.axis_size("vox")
    own, picked = take_windows(series, offsets, selected)
    across = swapped(own, 2)
    beside = swapped(own, 1)
    beyond = swapped(across, 1)
    slab = summed(picked, 4, 8, devices)
    slab = summed(slab, 4, 2, devices)
    slab = summed(slab, 2, 1, devices)
    parts = [slab[r * KL : (r + 1) * KL] for r in range(GR)]
    parts = [parts[0]] + [swapped(parts[r], r) for r in range(1, GR)]
    tiles = partial_kernels((own, beside, across, beyond), parts, devices, F32)
    tiles = lax.all_to_all(tiles.astype(LINK), "vox", split_axis=0, concat_axis=0, tiled=True)
    tile = jnp.sum(tiles.astype(F32), axis=0)
    turn = [
        (j * devices + z * 8 + x * 2 + y, x * devices + z * 8 + j * 2 + y)
        for j in range(GR)
        for z in range(4)
        for x in range(4)
        for y in range(2)
    ]
    return in_order(lax.ppermute(tile, ("subj", "vox"), turn))


def solution(mesh):
    placed = (P("subj", None, "vox"), P(), P())
    return jax.shard_map(
        body, mesh=mesh, in_specs=placed, out_specs=P("vox", "subj", None), check_vma=False
    )
```

profile of v0, /device:TPU:8, one launch (start us, length us, event | category | flops | bytes accessed | tf_op | source)
XLA Modules:
  0.0 100.9 jit_solution(1174542104489335098)
XLA Ops:
  0.0 2.6 %windows.1 = (bf16[12,64,512]{2,1,0:T(8,128)(2,1)}, bf16[64,768]{1,0:T(8,128)(2,1)}) custom-call(s32[16,12]{1,0:T(8,128)} %off_ref.1, s32[64]{0:T(128)} %sel_ref.1, bf16[4,256,512]{2,1,0:T(8,128)(2,1)} %series_ref.1), custom_call_target="tpu_custom_call" | custom-call | tf_op jit(solution)/shard_map/windows/pallas_call | solution.py:67
  2.6 0.3 collective-permute-start.1
  2.9 4.1 %collective-permute-start.5 = (bf16[64,768]{1,0:T(8,128)(2,1)}, bf16[64,768]{1,0:T(8,128)(2,1)S(1)}, u32[]{:S(2)}, u32[]{:S(2)}) collective-permute-start(bf16[64,768]{1,0:T(8,128)(2,1)} %get-tuple-element.8), channel_id=1, source_target_pairs={{0,24},{1,25},{2,26},{3,27},{4,28},{5,29},{6,30},{7,31},{8,0},{9,1... | collective-permute-start | bytes 294920 | tf_op jit(solution)/shard_map/ppermute | solution.py:210
  7.1 0.0 collective-permute-start.4
  7.1 1.3 %collective-permute-start.3 = (bf16[64,768]{1,0:T(8,128)(2,1)}, bf16[64,768]{1,0:T(8,128)(2,1)S(1)}, u32[]{:S(2)}, u32[]{:S(2)}) collective-permute-start(bf16[64,768]{1,0:T(8,128)(2,1)} %get-tuple-element.8), channel_id=1, source_target_pairs={{0,8},{1,9},{2,10},{3,11},{4,12},{5,13},{6,14},{7,15},{8,16},{9,17... | collective-permute-start | bytes 294920 | tf_op jit(solution)/shard_map/ppermute | solution.py:210
  8.3 13.7 %collective-permute-done.1.e2 = bf16[12,64,512]{2,1,0:T(8,128)(2,1)S(1)} collective-permute-done((bf16[12,64,512]{2,1,0:T(8,128)(2,1)}, bf16[12,64,512]{2,1,0:T(8,128)(2,1)S(1)}, u32[]{:S(2)}, u32[]{:S(2)}) %collective-permute-start.1) | collective-permute-done | bytes 786464 | tf_op jit(solution)/shard_map/ppermute | solution.py:206
  22.1 1.0 %add_add_fusion.1 = bf16[64,768]{1,0:T(8,128)(2,1)S(1)} fusion(bf16[64,768]{1,0:T(8,128)(2,1)S(1)} %collective-permute-done.5, bf16[64,768]{1,0:T(8,128)(2,1)S(1)} %collective-permute-done.4, bf16[64,768]{1,0:T(8,128)(2,1)} %get-tuple-element.8, bf16[64,768]{1,0:T(8,128)(2,1)S(1)} %collective-permute-done.3), kind=kLoop, calls=%fused_computation.2 | loop fusion | flops 147456 | bytes 491520 | tf_op jit(solution)/shard_map/add | solution.py:211
  23.1 2.8 %collective-permute-start.8 = (bf16[64,768]{1,0:T(8,128)(2,1)S(1)}, bf16[64,768]{1,0:T(8,128)(2,1)S(1)}, u32[]{:S(2)}, u32[]{:S(2)}) collective-permute-start(bf16[64,768]{1,0:T(8,128)(2,1)S(1)} %add_add_fusion.1), channel_id=1, source_target_pairs={{0,6},{1,7},{2,0},{3,1},{4,2},{5,3},{6,4},{7,5},{8,14},{9,15},{10,... | collective-permute-start | bytes 294920 | tf_op jit(solution)/shard_map/ppermute | solution.py:210
  26.0 0.8 collective-permute-start.7
  26.7 0.9 collective-permute-start.6
  27.6 3.1 %collective-permute-done.8 = bf16[64,768]{1,0:T(8,128)(2,1)S(1)} collective-permute-done((bf16[64,768]{1,0:T(8,128)(2,1)S(1)}, bf16[64,768]{1,0:T(8,128)(2,1)S(1)}, u32[]{:S(2)}, u32[]{:S(2)}) %collective-permute-start.8) | collective-permute-done | bytes 98336 | tf_op jit(solution)/shard_map/ppermute | solution.py:210
  30.7 2.4 %collective-permute-done.7 = bf16[64,768]{1,0:T(8,128)(2,1)S(1)} collective-permute-done((bf16[64,768]{1,0:T(8,128)(2,1)S(1)}, bf16[64,768]{1,0:T(8,128)(2,1)S(1)}, u32[]{:S(2)}, u32[]{:S(2)}) %collective-permute-start.7) | collective-permute-done | bytes 98336 | tf_op jit(solution)/shard_map/ppermute | solution.py:210
  33.1 1.3 %collective-permute-done.6 = bf16[64,768]{1,0:T(8,128)(2,1)S(1)} collective-permute-done((bf16[64,768]{1,0:T(8,128)(2,1)S(1)}, bf16[64,768]{1,0:T(8,128)(2,1)S(1)}, u32[]{:S(2)}, u32[]{:S(2)}) %collective-permute-start.6) | collective-permute-done | bytes 98336 | tf_op jit(solution)/shard_map/ppermute | solution.py:210
  34.4 2.4 %collective-permute-start.9 = (bf16[64,768]{1,0:T(8,128)(2,1)S(1)}, bf16[64,768]{1,0:T(8,128)(2,1)S(1)}, u32[]{:S(2)}, u32[]{:S(2)}) collective-permute-start(bf16[64,768]{1,0:T(8,128)(2,1)S(1)} %add_add_fusion), channel_id=1, source_target_pairs={{0,1},{1,0},{2,3},{3,2},{4,5},{5,4},{6,7},{7,6},{8,9},{9,8},{10,11... | collective-permute-start | bytes 294920 | tf_op jit(solution)/shard_map/ppermute | solution.py:210
  36.8 3.9 %collective-permute-done.9 = bf16[64,768]{1,0:T(8,128)(2,1)S(1)} collective-permute-done((bf16[64,768]{1,0:T(8,128)(2,1)S(1)}, bf16[64,768]{1,0:T(8,128)(2,1)S(1)}, u32[]{:S(2)}, u32[]{:S(2)}) %collective-permute-start.9) | collective-permute-done | bytes 98336 | tf_op jit(solution)/shard_map/ppermute | solution.py:210
  40.7 0.6 fusion
  41.3 0.8 collective-permute-start.11
  42.1 1.1 %collective-permute-start.10 = (bf16[16,768]{1,0:T(8,128)(2,1)S(1)}, bf16[16,768]{1,0:T(8,128)(2,1)S(1)}, u32[]{:S(2)}, u32[]{:S(2)}) collective-permute-start(bf16[16,768]{1,0:T(8,128)(2,1)S(1)} %get-tuple-element.11), channel_id=1, source_target_pairs={{0,32},{32,0},{64,96},{96,64},{1,33},{33,1},{65,97},{97,65},{2,34}... | collective-permute-start | bytes 73736 | tf_op jit(solution)/shard_map/ppermute | solution.py:206
  43.2 1.4 %collective-permute-done.12.s3 = bf16[16,768]{1,0:T(8,128)(2,1)S(1)} collective-permute-done((bf16[16,768]{1,0:T(8,128)(2,1)S(1)}, bf16[16,768]{1,0:T(8,128)(2,1)S(1)}, u32[]{:S(2)}, u32[]{:S(2)}) %collective-permute-start.12) | collective-permute-done | bytes 24608 | tf_op jit(solution)/shard_map/ppermute | solution.py:206
  44.6 0.6 collective-permute-done.11.s2
  45.2 0.6 copy-done.5
  45.8 0.0 copy-done.6
  45.8 0.3 copy-done.1
  46.1 0.3 copy-done.2
  46.4 12.4 %partial_kernels.1 = f32[32,144,128]{2,1,0:T(8,128)} custom-call(bf16[12,64,512]{2,1,0:T(8,128)(2,1)} %get-tuple-element.7.e0, bf16[12,64,512]{2,1,0:T(8,128)(2,1)} %copy-done.1, bf16[12,64,512]{2,1,0:T(8,128)(2,1)} %copy-done, bf16[12,64,512]{2,1,0:T(8,128)(2,1)} %copy-done.2, bf16[16,768]{1,0:T(8,128)(2,1)} %get-tuple-element.12.s0, ...), custom_call_target="tpu_custom_call" | custom-call | tf_op jit(solution)/shard_map/partial_kernels/pallas_call | solution.py:154
  58.8 1.8 %convert_element_type.6 = f16[32,144,128]{2,1,0:T(8,128)(2,1)S(1)} convert(f32[32,144,128]{2,1,0:T(8,128)} %partial_kernels.1) | non-fusion elementwise | flops 589824 | bytes 3538944 | tf_op jit(solution)/shard_map/convert_element_type | solution.py:226
  60.7 28.4 %all_to_all.5 = f16[32,144,128]{2,1,0:T(8,128)(2,1)S(1)} all-to-all(f16[32,144,128]{2,1,0:T(8,128)(2,1)S(1)} %convert_element_type.6), channel_id=1, replica_groups=mesh['subj'=4,'vox'=32] {'vox'}, dimensions={0} | all-to-all | bytes 2359296 | tf_op jit(solution)/shard_map/all_to_all | solution.py:226
  89.1 0.2 convert_reduce_fusion
  89.3 4.1 %collective-permute-start.13 = (f32[144,128]{1,0:T(8,128)S(1)}, f32[144,128]{1,0:T(8,128)S(1)}, u32[]{:S(2)}, u32[]{:S(2)}) collective-permute-start(f32[144,128]{1,0:T(8,128)S(1)} %convert_reduce_fusion), channel_id=1, source_target_pairs={{0,0},{1,1},{2,32},{3,33},{4,64},{5,65},{6,96},{7,97},{8,8},{9,9},... | collective-permute-start | bytes 221192 | tf_op jit(solution)/shard_map/ppermute | solution.py:235
  93.4 4.5 %collective-permute-done.13.y_ref = f32[144,128]{1,0:T(8,128)S(1)} collective-permute-done((f32[144,128]{1,0:T(8,128)S(1)}, f32[144,128]{1,0:T(8,128)S(1)}, u32[]{:S(2)}, u32[]{:S(2)}) %collective-permute-start.13) | collective-permute-done | bytes 73760 | tf_op jit(solution)/shard_map/ppermute | solution.py:235
  97.9 0.6 copy-done.3
  98.5 2.4 %in_order.1 = f32[2,48,192]{2,1,0:T(8,128)} custom-call(f32[144,128]{1,0:T(8,128)} %copy-done.3), custom_call_target="tpu_custom_call" | custom-call | tf_op jit(solution)/shard_map/in_order/pallas_call | solution.py:188
  (20 shorter events, 0.1 us)
Async XLA Ops:
  2.6 19.5 %collective-permute-start.1 = (bf16[12,64,512]{2,1,0:T(8,128)(2,1)}, bf16[12,64,512]{2,1,0:T(8,128)(2,1)S(1)}, u32[]{:S(2)}, u32[]{:S(2)}) collective-permute-start(bf16[12,64,512]{2,1,0:T(8,128)(2,1)} %get-tuple-element.7.e0), channel_id=1, source_target_pairs={{0,64},{32,96},{64,0},{96,32},{1,65},{33,97},{65,1},{97,33},{2,66}... | collective-permute-start | bytes 2359304 | tf_op jit(solution)/shard_map/ppermute | solution.py:206
  2.9 19.2 %collective-permute-start.5 = (bf16[64,768]{1,0:T(8,128)(2,1)}, bf16[64,768]{1,0:T(8,128)(2,1)S(1)}, u32[]{:S(2)}, u32[]{:S(2)}) collective-permute-start(bf16[64,768]{1,0:T(8,128)(2,1)} %get-tuple-element.8), channel_id=1, source_target_pairs={{0,24},{1,25},{2,26},{3,27},{4,28},{5,29},{6,30},{7,31},{8,0},{9,1... | collective-permute-start | bytes 294920 | tf_op jit(solution)/shard_map/ppermute | solution.py:210
  7.1 15.0 %collective-permute-start.4 = (bf16[64,768]{1,0:T(8,128)(2,1)}, bf16[64,768]{1,0:T(8,128)(2,1)S(1)}, u32[]{:S(2)}, u32[]{:S(2)}) collective-permute-start(bf16[64,768]{1,0:T(8,128)(2,1)} %get-tuple-element.8), channel_id=1, source_target_pairs={{0,16},{1,17},{2,18},{3,19},{4,20},{5,21},{6,22},{7,23},{8,24},{9,... | collective-permute-start | bytes 294920 | tf_op jit(solution)/shard_map/ppermute | solution.py:210
  7.1 15.0 %collective-permute-start.3 = (bf16[64,768]{1,0:T(8,128)(2,1)}, bf16[64,768]{1,0:T(8,128)(2,1)S(1)}, u32[]{:S(2)}, u32[]{:S(2)}) collective-permute-start(bf16[64,768]{1,0:T(8,128)(2,1)} %get-tuple-element.8), channel_id=1, source_target_pairs={{0,8},{1,9},{2,10},{3,11},{4,12},{5,13},{6,14},{7,15},{8,16},{9,17... | collective-permute-start | bytes 294920 | tf_op jit(solution)/shard_map/ppermute | solution.py:210
  8.3 36.9 %collective-permute-start = (bf16[12,64,512]{2,1,0:T(8,128)(2,1)}, bf16[12,64,512]{2,1,0:T(8,128)(2,1)S(1)}, u32[]{:S(2)}, u32[]{:S(2)}) collective-permute-start(bf16[12,64,512]{2,1,0:T(8,128)(2,1)} %get-tuple-element.7.e0), channel_id=1, source_target_pairs={{0,32},{32,0},{64,96},{96,64},{1,33},{33,1},{65,97},{97,65},{2,34}... | collective-permute-start | bytes 2359304 | tf_op jit(solution)/shard_map/ppermute | solution.py:206
  22.1 23.2 %copy-start = (bf16[12,64,512]{2,1,0:T(8,128)(2,1)}, bf16[12,64,512]{2,1,0:T(8,128)(2,1)S(1)}, u32[]{:S(2)}) copy-start(bf16[12,64,512]{2,1,0:T(8,128)(2,1)S(1)} %collective-permute-done.1.e2) | copy-start | bytes 2359300
  22.1 23.1 %collective-permute-start.2 = (bf16[12,64,512]{2,1,0:T(8,128)(2,1)S(1)}, bf16[12,64,512]{2,1,0:T(8,128)(2,1)S(1)}, u32[]{:S(2)}, u32[]{:S(2)}) collective-permute-start(bf16[12,64,512]{2,1,0:T(8,128)(2,1)S(1)} %collective-permute-done.1.e2), channel_id=1, source_target_pairs={{0,32},{32,0},{64,96},{96,64},{1,33},{33,1},{65,97},{97,65},{2,34}... | collective-permute-start | bytes 2359304 | tf_op jit(solution)/shard_map/ppermute | solution.py:206
  23.1 7.6 %collective-permute-start.8 = (bf16[64,768]{1,0:T(8,128)(2,1)S(1)}, bf16[64,768]{1,0:T(8,128)(2,1)S(1)}, u32[]{:S(2)}, u32[]{:S(2)}) collective-permute-start(bf16[64,768]{1,0:T(8,128)(2,1)S(1)} %add_add_fusion.1), channel_id=1, source_target_pairs={{0,6},{1,7},{2,0},{3,1},{4,2},{5,3},{6,4},{7,5},{8,14},{9,15},{10,... | collective-permute-start | bytes 294920 | tf_op jit(solution)/shard_map/ppermute | solution.py:210
  26.0 7.2 %collective-permute-start.7 = (bf16[64,768]{1,0:T(8,128)(2,1)S(1)}, bf16[64,768]{1,0:T(8,128)(2,1)S(1)}, u32[]{:S(2)}, u32[]{:S(2)}) collective-permute-start(bf16[64,768]{1,0:T(8,128)(2,1)S(1)} %add_add_fusion.1), channel_id=1, source_target_pairs={{0,4},{1,5},{2,6},{3,7},{4,0},{5,1},{6,2},{7,3},{8,12},{9,13},{10,... | collective-permute-start | bytes 294920 | tf_op jit(solution)/shard_map/ppermute | solution.py:210
  26.7 7.6 %collective-permute-start.6 = (bf16[64,768]{1,0:T(8,128)(2,1)S(1)}, bf16[64,768]{1,0:T(8,128)(2,1)S(1)}, u32[]{:S(2)}, u32[]{:S(2)}) collective-permute-start(bf16[64,768]{1,0:T(8,128)(2,1)S(1)} %add_add_fusion.1), channel_id=1, source_target_pairs={{0,2},{1,3},{2,4},{3,5},{4,6},{5,7},{6,0},{7,1},{8,10},{9,11},{10,... | collective-permute-start | bytes 294920 | tf_op jit(solution)/shard_map/ppermute | solution.py:210
  34.4 6.3 %collective-permute-start.9 = (bf16[64,768]{1,0:T(8,128)(2,1)S(1)}, bf16[64,768]{1,0:T(8,128)(2,1)S(1)}, u32[]{:S(2)}, u32[]{:S(2)}) collective-permute-start(bf16[64,768]{1,0:T(8,128)(2,1)S(1)} %add_add_fusion), channel_id=1, source_target_pairs={{0,1},{1,0},{2,3},{3,2},{4,5},{5,4},{6,7},{7,6},{8,9},{9,8},{10,11... | collective-permute-start | bytes 294920 | tf_op jit(solution)/shard_map/ppermute | solution.py:210
  41.3 3.3 %collective-permute-start.12 = (bf16[16,768]{1,0:T(8,128)(2,1)S(1)}, bf16[16,768]{1,0:T(8,128)(2,1)S(1)}, u32[]{:S(2)}, u32[]{:S(2)}) collective-permute-start(bf16[16,768]{1,0:T(8,128)(2,1)S(1)} %get-tuple-element.9), channel_id=1, source_target_pairs={{0,96},{32,64},{64,32},{96,0},{1,97},{33,65},{65,33},{97,1},{2,98}... | collective-permute-start | bytes 73736 | tf_op jit(solution)/shard_map/ppermute | solution.py:206
  41.3 3.8 %collective-permute-start.11 = (bf16[16,768]{1,0:T(8,128)(2,1)S(1)}, bf16[16,768]{1,0:T(8,128)(2,1)S(1)}, u32[]{:S(2)}, u32[]{:S(2)}) collective-permute-start(bf16[16,768]{1,0:T(8,128)(2,1)S(1)} %get-tuple-element.10), channel_id=1, source_target_pairs={{0,64},{32,96},{64,0},{96,32},{1,65},{33,97},{65,1},{97,33},{2,66}... | collective-permute-start | bytes 73736 | tf_op jit(solution)/shard_map/ppermute | solution.py:206
  42.1 3.0 %collective-permute-start.10 = (bf16[16,768]{1,0:T(8,128)(2,1)S(1)}, bf16[16,768]{1,0:T(8,128)(2,1)S(1)}, u32[]{:S(2)}, u32[]{:S(2)}) collective-permute-start(bf16[16,768]{1,0:T(8,128)(2,1)S(1)} %get-tuple-element.11), channel_id=1, source_target_pairs={{0,32},{32,0},{64,96},{96,64},{1,33},{33,1},{65,97},{97,65},{2,34}... | collective-permute-start | bytes 73736 | tf_op jit(solution)/shard_map/ppermute | solution.py:206
  44.6 0.6 copy-start.4
  45.2 0.6 copy-start.5
  45.2 0.6 copy-start.6
  45.2 0.9 copy-start.1
  45.2 1.2 %copy-start.2 = (bf16[12,64,512]{2,1,0:T(8,128)(2,1)}, bf16[12,64,512]{2,1,0:T(8,128)(2,1)S(1)}, u32[]{:S(2)}) copy-start(bf16[12,64,512]{2,1,0:T(8,128)(2,1)S(1)} %collective-permute-done.2.e3) | copy-start | bytes 2359300
  89.3 8.6 %collective-permute-start.13 = (f32[144,128]{1,0:T(8,128)S(1)}, f32[144,128]{1,0:T(8,128)S(1)}, u32[]{:S(2)}, u32[]{:S(2)}) collective-permute-start(f32[144,128]{1,0:T(8,128)S(1)} %convert_reduce_fusion), channel_id=1, source_target_pairs={{0,0},{1,1},{2,32},{3,33},{4,64},{5,65},{6,96},{7,97},{8,8},{9,9},... | collective-permute-start | bytes 221192 | tf_op jit(solution)/shard_map/ppermute | solution.py:235
  97.9 0.6 copy-start.3
where the time goes:
time: 101 us
  waiting for transfers between devices  30.9 us (31%)
  blocking collectives  28.4 us (28%)
  starting transfers between devices  18.6 us (18%)
  Pallas kernels  17.4 us (17%)
  other arithmetic  3.06 us (3%)
  local copies, waits for them, and re-layouts  2.41 us (2%)
    all_to_all x1, blocking collectives, body(): lax.all_to_all(tiles.astype(LINK), 'vox', split_axis=0, concat_axis=0, ti...  28.4 us
    ppermute x6, waiting for transfers between devices, swapped(): return lax.ppermute(x, 'subj', [(n, n ^ r) for n in range(GR)])  15.7 us
    pallas_call x1, Pallas kernels, partial_kernels(): pl.pallas_call(kernel_kernel, out_shape=jax.ShapeDtypeStruct((devices, 3...  12.4 us
    ppermute x7, starting transfers between devices, summed(): lax.ppermute(x, 'vox', ring(n, size, stride, devices))  12.3 us
    ppermute x7, waiting for transfers between devices, summed(): lax.ppermute(x, 'vox', ring(n, size, stride, devices))  10.7 us
    ppermute x1, waiting for transfers between devices, body(): return in_order(lax.ppermute(tile, ('subj', 'vox'), turn))  4.52 us
    ppermute x1, starting transfers between devices, body(): return in_order(lax.ppermute(tile, ('subj', 'vox'), turn))  4.12 us
    pallas_call x1, Pallas kernels, take_windows(): pl.pallas_call(window_kernel, out_shape=(jax.ShapeDtypeStruct((EP, SL * T...  2.56 us
  transfers between devices with their start and end apart: 14, of which 8 were waited for; matrix products, arithmetic and copies ran while one was open for 2% of the time, Pallas kernels for 0%

commit v1 on v0

--- a/solution.py
+++ b/solution.py
@@ -4,6 +4,7 @@
 from jax.experimental import pallas as pl
 from jax.experimental.pallas import tpu as pltpu
 from jax.sharding import PartitionSpec as P
+
 
 TR = 16
 EP = 12
@@ -81,7 +82,38 @@
     )(offsets, selected, series)
 
 
-def kernel_kernel(e0, e1, e2, e3, s0, s1, s2, s3, o_ref, lh_ref, ll_ref, c_ref, n_ref, z_ref, g_ref):
+def meeting(j, first, count):
+    shape = (SB, count * SL * TR)
+    place = iota(shape, 1)
+    home = ((place // TR) % SL) * GR + ((place // (SL * TR) + first) ^ j)
+    return iota(shape, 0) == home
+
+
+def norm_kernel(first, e0, e1, n_ref):
+    j = lax.axis_index("subj")
+    gather = jnp.where(meeting(j, first, 2), 1.0, 0.0).astype(BF16)
+    for e in range(EP):
+        x = jnp.concatenate([e0[e], e1[e]], axis=0)
+        xf = x.astype(F32)
+        high, low = split(xf * xf)
+        total = dot(gather, x)
+        square = dot(gather, high) + dot(gather, low)
+        n_ref[e] = square - total * total * (1.0 / TR)
+
+
+def norms(e0, e1, first):
+    return pl.pallas_call(
+        lambda *refs: norm_kernel(first, *refs),
+        out_shape=jax.ShapeDtypeStruct((EP, SB, e0.shape[2]), F32),
+        in_specs=[pl.BlockSpec(memory_space=pltpu.VMEM)] * 2,
+        out_specs=pl.BlockSpec(memory_space=pltpu.VMEM),
+        name="norms",
+    )(e0, e1)
+
+
+def kernel_kernel(
+    e0, e1, e2, e3, s0, s1, s2, s3, na, nb, o_ref, lh_ref, ll_ref, c_ref, n_ref, z_ref, g_ref
+):
     j = lax.axis_index("subj")
     epochs = (e0, e1, e2, e3)
     slabs = (s0, s1, s2, s3)
@@ -89,10 +121,7 @@
     deep = SB * TR
     chunk = SL * TR
     same = (iota((deep, deep), 0) // TR == iota((deep, deep), 1) // TR).astype(F32).astype(BF16)
-    place = iota((SB, deep), 1)
-    home = ((place // TR) % SL) * GR + ((place // chunk) ^ j)
-    mine = iota((SB, deep), 0) == home
-    gather = jnp.where(mine, 1.0, 0.0).astype(BF16)
+    mine = meeting(j, 0, GR)
 
     slab = jnp.concatenate(
         [
@@ -108,11 +137,7 @@
 
     for e in range(EP):
         x = jnp.concatenate([p[e] for p in epochs], axis=0)
-        xf = x.astype(F32)
-        high, low = split(xf * xf)
-        total = dot(gather, x)
-        square = dot(gather, high) + dot(gather, low)
-        n_ref[e] = lax.rsqrt(square - total * total * (1.0 / TR) + series_floor)
+        n_ref[e] = lax.rsqrt(na[e] + nb[e] + series_floor)
         for k in range(KL):
             line = jnp.where(mine, slab_std[e * KL + k : e * KL + k + 1, :], 0.0)
             lh, ll = split(line)
@@ -127,7 +152,7 @@
                 fisher = []
                 for e in range(EP):
                     shrunk = c_ref[e, pl.ds(start, SB), c : c + 128] * n_ref[e, :, c : c + 128]
-                    fisher.append(jnp.log(1.0 + shrunk) - jnp.log(1.0 - shrunk))
+                    fisher.append(jnp.log((1.0 + shrunk) / (1.0 - shrunk)))
                 mean = sum(fisher[1:], fisher[0]) * (1.0 / EP)
                 fisher = [f - mean for f in fisher]
                 spread = fisher[0] * fisher[0]
@@ -149,12 +174,12 @@
     lax.fori_loop(0, KL // 2, pair, 0)
 
 
-def partial_kernels(epochs, slabs, devices, dtype):
+def partial_kernels(epochs, slabs, powers, devices, dtype):
     width = epochs[0].shape[2]
     return pl.pallas_call(
         kernel_kernel,
         out_shape=jax.ShapeDtypeStruct((devices, 3 * EP * SL, 128), dtype),
-        in_specs=[pl.BlockSpec(memory_space=pltpu.VMEM)] * (2 * GR),
+        in_specs=[pl.BlockSpec(memory_space=pltpu.VMEM)] * (2 * GR + 2),
         out_specs=pl.BlockSpec(memory_space=pltpu.VMEM),
         scratch_shapes=[
             pltpu.VMEM((KL * SB, SB * TR), BF16),
@@ -165,7 +190,7 @@
             pltpu.VMEM((3, EP * SB, 128), F32),
         ],
         name="partial_kernels",
-    )(*epochs, *slabs)
+    )(*epochs, *slabs, *powers)
 
 
 def order_kernel(y_ref, o_ref):
@@ -173,15 +198,17 @@
     cols = EP * SB
     source = iota((cols, cols), 0)
     target = (source % GR) * rows + ((source // GR) % SL) * EP + source // SB
-    column = jnp.where(iota((cols, cols), 1) == target, 1.0, 0.0).astype(F32)
-    source = iota((rows, rows), 1)
-    line = jnp.where(iota((rows, rows), 0) == (source % SL) * EP + source // SL, 1.0, 0.0).astype(F32)
-    exact = dict(precision=lax.Precision.HIGHEST, preferred_element_type=F32)
+    column = jnp.where(iota((cols, cols), 1) == target, 1.0, 0.0).astype(BF16)
     for h in range(2):
-        left = y_ref[h * rows : (h + 1) * rows, :]
-        right = y_ref[2 * rows : 3 * rows, h * 64 : (h + 1) * 64]
-        whole = jnp.concatenate([left, right], axis=1)
-        o_ref[h] = jnp.dot(line, jnp.dot(whole, column, **exact), **exact) * (1.0 / VOX)
+        lines = []
+        for s in range(SL):
+            left = y_ref[pl.ds(h * rows + s, EP, stride=SL), :]
+            right = y_ref[pl.ds(2 * rows + s, EP, stride=SL), :]
+            lines.append(jnp.concatenate([left, right[:, h * 64 : (h + 1) * 64]], axis=1))
+        whole = jnp.concatenate(lines, axis=0)
+        high, _ = split(whole)
+        middle, low = split(whole - high.astype(F32))
+        o_ref[h] = (dot(high, column) + dot(middle, column) + dot(low, column)) * (1.0 / VOX)
 
 
 def in_order(tile):
@@ -216,13 +243,15 @@
     own, picked = take_windows(series, offsets, selected)
     across = swapped(own, 2)
     beside = swapped(own, 1)
-    beyond = swapped(across, 1)
+    near = norms(own, beside, 0)
     slab = summed(picked, 4, 8, devices)
     slab = summed(slab, 4, 2, devices)
     slab = summed(slab, 2, 1, devices)
+    beyond = swapped(across, 1)
+    far = norms(across, beyond, 2)
     parts = [slab[r * KL : (r + 1) * KL] for r in range(GR)]
     parts = [parts[0]] + [swapped(parts[r], r) for r in range(1, GR)]
-    tiles = partial_kernels((own, beside, across, beyond), parts, devices, F32)
+    tiles = partial_kernels((own, beside, across, beyond), parts, (near, far), devices, F32)
     tiles = lax.all_to_all(tiles.astype(LINK), "vox", split_axis=0, concat_axis=0, tiled=True)
     tile = jnp.sum(tiles.astype(F32), axis=0)
     turn = [

time: 101 us -> 104 us (1.030)
  Pallas kernels: 17.4 us -> 21.3 us
  waiting for transfers between devices: 30.9 us -> 29 us
  local copies, waits for them, and re-layouts: 2.41 us -> 3.63 us
    pallas_call x0 -> x2, Pallas kernels: none -> 5.77 us  [norms(): pl.pallas_call(lambda *refs: norm_kernel(first, *refs), out_shape=jax.Sha...]
    ppermute x6, waiting for transfers between devices: 15.7 us -> 13.8 us  [swapped(): return lax.ppermute(x, 'subj', [(n, n ^ r) for n in range(GR)])]
    pallas_call x1, Pallas kernels: 12.4 us -> 11.2 us  [partial_kernels(): pl.pallas_call(kernel_kernel, out_shape=jax.ShapeDtypeStruct((devices, 3...]
    unnamed x14, local copies, waits for them, and re-layouts: 1.8 us -> 3.02 us
  transfers between devices with their start and end apart: 14 -> 14, of which waited for: 8 -> 6; matrix products, arithmetic and copies ran while one was open for 2% -> 2% of each run, Pallas kernels for 0% -> 6%
where the time goes in v1:
time: 104 us
  waiting for transfers between devices  29 us (28%)
  blocking collectives  28.3 us (27%)
  Pallas kernels  21.3 us (20%)
  starting transfers between devices  18.5 us (18%)
  local copies, waits for them, and re-layouts  3.63 us (3%)
  other arithmetic  3.06 us (3%)
    all_to_all x1, blocking collectives, body(): lax.all_to_all(tiles.astype(LINK), 'vox', split_axis=0, concat_axis=0, ti...  28.3 us
    ppermute x6, waiting for transfers between devices, swapped(): return lax.ppermute(x, 'subj', [(n, n ^ r) for n in range(GR)])  13.8 us
    ppermute x7, starting transfers between devices, summed(): lax.ppermute(x, 'vox', ring(n, size, stride, devices))  12.3 us
    pallas_call x1, Pallas kernels, partial_kernels(): pl.pallas_call(kernel_kernel, out_shape=jax.ShapeDtypeStruct((devices, 3...  11.2 us
    ppermute x7, waiting for transfers between devices, summed(): lax.ppermute(x, 'vox', ring(n, size, stride, devices))  10.7 us
    pallas_call x2, Pallas kernels, norms(): pl.pallas_call(lambda *refs: norm_kernel(first, *refs), out_shape=jax.Sha...  5.77 us
    ppermute x1, waiting for transfers between devices, body(): return in_order(lax.ppermute(tile, ('subj', 'vox'), turn))  4.62 us
    ppermute x1, starting transfers between devices, body(): return in_order(lax.ppermute(tile, ('subj', 'vox'), turn))  4.03 us
  transfers between devices with their start and end apart: 14, of which 6 were waited for; matrix products, arithmetic and copies ran while one was open for 2% of the time, Pallas kernels for 6%

profile of v1, /device:TPU:8, one launch (start us, length us, event | category | flops | bytes accessed | tf_op | source)
XLA Modules:
  0.0 103.9 jit_solution(8051898973284963547)
XLA Ops:
  0.0 2.6 %windows.1 = (bf16[12,64,512]{2,1,0:T(8,128)(2,1)}, bf16[64,768]{1,0:T(8,128)(2,1)}) custom-call(s32[16,12]{1,0:T(8,128)} %off_ref.1, s32[64]{0:T(128)} %sel_ref.1, bf16[4,256,512]{2,1,0:T(8,128)(2,1)} %series_ref.1), custom_call_target="tpu_custom_call" | custom-call | tf_op jit(solution)/shard_map/windows/pallas_call | solution.py:68
  2.6 0.3 collective-permute-start.1
  2.9 4.1 %collective-permute-start.5 = (bf16[64,768]{1,0:T(8,128)(2,1)}, bf16[64,768]{1,0:T(8,128)(2,1)S(1)}, u32[]{:S(2)}, u32[]{:S(2)}) collective-permute-start(bf16[64,768]{1,0:T(8,128)(2,1)} %get-tuple-element.8), channel_id=1, source_target_pairs={{0,24},{1,25},{2,26},{3,27},{4,28},{5,29},{6,30},{7,31},{8,0},{9,1... | collective-permute-start | bytes 294920 | tf_op jit(solution)/shard_map/ppermute | solution.py:237
  7.1 1.3 %collective-permute-start.3 = (bf16[64,768]{1,0:T(8,128)(2,1)}, bf16[64,768]{1,0:T(8,128)(2,1)S(1)}, u32[]{:S(2)}, u32[]{:S(2)}) collective-permute-start(bf16[64,768]{1,0:T(8,128)(2,1)} %get-tuple-element.8), channel_id=1, source_target_pairs={{0,8},{1,9},{2,10},{3,11},{4,12},{5,13},{6,14},{7,15},{8,16},{9,17... | collective-permute-start | bytes 294920 | tf_op jit(solution)/shard_map/ppermute | solution.py:237
  8.3 13.7 %collective-permute-done.1.refs_0_.e2 = bf16[12,64,512]{2,1,0:T(8,128)(2,1)S(1)} collective-permute-done((bf16[12,64,512]{2,1,0:T(8,128)(2,1)}, bf16[12,64,512]{2,1,0:T(8,128)(2,1)S(1)}, u32[]{:S(2)}, u32[]{:S(2)}) %collective-permute-start.1) | collective-permute-done | bytes 786464 | tf_op jit(solution)/shard_map/ppermute | solution.py:233
  22.1 1.0 add_add_fusion.1
  23.1 2.8 %collective-permute-start.8 = (bf16[64,768]{1,0:T(8,128)(2,1)S(1)}, bf16[64,768]{1,0:T(8,128)(2,1)S(1)}, u32[]{:S(2)}, u32[]{:S(2)}) collective-permute-start(bf16[64,768]{1,0:T(8,128)(2,1)S(1)} %add_add_fusion.1), channel_id=1, source_target_pairs={{0,6},{1,7},{2,0},{3,1},{4,2},{5,3},{6,4},{7,5},{8,14},{9,15},{10,... | collective-permute-start | bytes 294920 | tf_op jit(solution)/shard_map/ppermute | solution.py:237
  26.0 0.8 collective-permute-start.7
  26.7 0.9 collective-permute-start.6
  27.6 3.1 %collective-permute-done.8 = bf16[64,768]{1,0:T(8,128)(2,1)S(1)} collective-permute-done((bf16[64,768]{1,0:T(8,128)(2,1)S(1)}, bf16[64,768]{1,0:T(8,128)(2,1)S(1)}, u32[]{:S(2)}, u32[]{:S(2)}) %collective-permute-start.8) | collective-permute-done | bytes 98336 | tf_op jit(solution)/shard_map/ppermute | solution.py:237
  30.7 2.4 %collective-permute-done.7 = bf16[64,768]{1,0:T(8,128)(2,1)S(1)} collective-permute-done((bf16[64,768]{1,0:T(8,128)(2,1)S(1)}, bf16[64,768]{1,0:T(8,128)(2,1)S(1)}, u32[]{:S(2)}, u32[]{:S(2)}) %collective-permute-start.7) | collective-permute-done | bytes 98336 | tf_op jit(solution)/shard_map/ppermute | solution.py:237
  33.1 1.3 %collective-permute-done.6 = bf16[64,768]{1,0:T(8,128)(2,1)S(1)} collective-permute-done((bf16[64,768]{1,0:T(8,128)(2,1)S(1)}, bf16[64,768]{1,0:T(8,128)(2,1)S(1)}, u32[]{:S(2)}, u32[]{:S(2)}) %collective-permute-start.6) | collective-permute-done | bytes 98336 | tf_op jit(solution)/shard_map/ppermute | solution.py:237
  34.4 2.4 %collective-permute-start.9 = (bf16[64,768]{1,0:T(8,128)(2,1)S(1)}, bf16[64,768]{1,0:T(8,128)(2,1)S(1)}, u32[]{:S(2)}, u32[]{:S(2)}) collective-permute-start(bf16[64,768]{1,0:T(8,128)(2,1)S(1)} %add_add_fusion), channel_id=1, source_target_pairs={{0,1},{1,0},{2,3},{3,2},{4,5},{5,4},{6,7},{7,6},{8,9},{9,8},{10,11... | collective-permute-start | bytes 294920 | tf_op jit(solution)/shard_map/ppermute | solution.py:237
  36.8 3.9 %collective-permute-done.9 = bf16[64,768]{1,0:T(8,128)(2,1)S(1)} collective-permute-done((bf16[64,768]{1,0:T(8,128)(2,1)S(1)}, bf16[64,768]{1,0:T(8,128)(2,1)S(1)}, u32[]{:S(2)}, u32[]{:S(2)}) %collective-permute-start.9) | collective-permute-done | bytes 98336 | tf_op jit(solution)/shard_map/ppermute | solution.py:237
  40.7 0.6 fusion
  41.3 0.8 collective-permute-start.11
  42.1 1.1 %collective-permute-start.10 = (bf16[16,768]{1,0:T(8,128)(2,1)S(1)}, bf16[16,768]{1,0:T(8,128)(2,1)S(1)}, u32[]{:S(2)}, u32[]{:S(2)}) collective-permute-start(bf16[16,768]{1,0:T(8,128)(2,1)S(1)} %get-tuple-element.11), channel_id=1, source_target_pairs={{0,32},{32,0},{64,96},{96,64},{1,33},{33,1},{65,97},{97,65},{2,34}... | collective-permute-start | bytes 73736 | tf_op jit(solution)/shard_map/ppermute | solution.py:233
  43.2 0.9 copy-done.1
  44.1 2.9 %norms.2.na = f32[12,16,512]{2,1,0:T(8,128)} custom-call(bf16[12,64,512]{2,1,0:T(8,128)(2,1)} %get-tuple-element.7.refs_0_.e0, bf16[12,64,512]{2,1,0:T(8,128)(2,1)} %copy-done.1), custom_call_target="tpu_custom_call" | custom-call | tf_op jit(solution)/shard_map/norms/pallas_call | solution.py:105
  47.0 0.9 copy-done.2
  47.9 2.9 %norms.3.nb = f32[12,16,512]{2,1,0:T(8,128)} custom-call(bf16[12,64,512]{2,1,0:T(8,128)(2,1)} %copy-done, bf16[12,64,512]{2,1,0:T(8,128)(2,1)} %copy-done.2), custom_call_target="tpu_custom_call" | custom-call | tf_op jit(solution)/shard_map/norms/pallas_call | solution.py:105
  50.8 0.6 copy-done.4
  51.4 0.0 copy-done.5
  51.4 0.0 copy-done.6
  51.4 11.2 %partial_kernels.1 = f32[32,144,128]{2,1,0:T(8,128)} custom-call(bf16[12,64,512]{2,1,0:T(8,128)(2,1)} %get-tuple-element.7.refs_0_.e0, bf16[12,64,512]{2,1,0:T(8,128)(2,1)} %copy-done.1, bf16[12,64,512]{2,1,0:T(8,128)(2,1)} %copy-done, bf16[12,64,512]{2,1,0:T(8,128)(2,1)} %copy-done.2, bf16[16,768]{1,0:T(8,128)(2,1)} %get-tuple-element.12.s0, ...), custom_call_target="tpu_custom_call" | custom-call | tf_op jit(solution)/shard_map/partial_kernels/pallas_call | solution.py:179
  62.6 1.8 %convert_element_type.6 = f16[32,144,128]{2,1,0:T(8,128)(2,1)S(1)} convert(f32[32,144,128]{2,1,0:T(8,128)} %partial_kernels.1) | non-fusion elementwise | flops 589824 | bytes 3538944 | tf_op jit(solution)/shard_map/convert_element_type | solution.py:255
  64.4 28.3 %all_to_all.5 = f16[32,144,128]{2,1,0:T(8,128)(2,1)S(1)} all-to-all(f16[32,144,128]{2,1,0:T(8,128)(2,1)S(1)} %convert_element_type.6), channel_id=1, replica_groups=mesh['subj'=4,'vox'=32] {'vox'}, dimensions={0} | all-to-all | bytes 2359296 | tf_op jit(solution)/shard_map/all_to_all | solution.py:255
  92.7 0.2 convert_reduce_fusion
  92.9 4.0 %collective-permute-start.13 = (f32[144,128]{1,0:T(8,128)S(1)}, f32[144,128]{1,0:T(8,128)S(1)}, u32[]{:S(2)}, u32[]{:S(2)}) collective-permute-start(f32[144,128]{1,0:T(8,128)S(1)} %convert_reduce_fusion), channel_id=1, source_target_pairs={{0,0},{1,1},{2,32},{3,33},{4,64},{5,65},{6,96},{7,97},{8,8},{9,9},... | collective-permute-start | bytes 221192 | tf_op jit(solution)/shard_map/ppermute | solution.py:264
  96.9 4.6 %collective-permute-done.13.y_ref = f32[144,128]{1,0:T(8,128)S(1)} collective-permute-done((f32[144,128]{1,0:T(8,128)S(1)}, f32[144,128]{1,0:T(8,128)S(1)}, u32[]{:S(2)}, u32[]{:S(2)}) %collective-permute-start.13) | collective-permute-done | bytes 73760 | tf_op jit(solution)/shard_map/ppermute | solution.py:264
  101.5 0.6 copy-done.3
  102.1 1.8 %in_order.1 = f32[2,48,192]{2,1,0:T(8,128)} custom-call(f32[144,128]{1,0:T(8,128)} %copy-done.3), custom_call_target="tpu_custom_call" | custom-call | tf_op jit(solution)/shard_map/in_order/pallas_call | solution.py:215
  (22 shorter events, 0.1 us)
Async XLA Ops:
  2.6 19.5 %collective-permute-start.1 = (bf16[12,64,512]{2,1,0:T(8,128)(2,1)}, bf16[12,64,512]{2,1,0:T(8,128)(2,1)S(1)}, u32[]{:S(2)}, u32[]{:S(2)}) collective-permute-start(bf16[12,64,512]{2,1,0:T(8,128)(2,1)} %get-tuple-element.7.refs_0_.e0), channel_id=1, source_target_pairs={{0,64},{32,96},{64,0},{96,32},{1,65},{33,97},{65,1},{97,33},{2,66}... | collective-permute-start | bytes 2359304 | tf_op jit(solution)/shard_map/ppermute | solution.py:233
  2.9 19.2 %collective-permute-start.5 = (bf16[64,768]{1,0:T(8,128)(2,1)}, bf16[64,768]{1,0:T(8,128)(2,1)S(1)}, u32[]{:S(2)}, u32[]{:S(2)}) collective-permute-start(bf16[64,768]{1,0:T(8,128)(2,1)} %get-tuple-element.8), channel_id=1, source_target_pairs={{0,24},{1,25},{2,26},{3,27},{4,28},{5,29},{6,30},{7,31},{8,0},{9,1... | collective-permute-start | bytes 294920 | tf_op jit(solution)/shard_map/ppermute | solution.py:237
  7.1 15.0 %collective-permute-start.4 = (bf16[64,768]{1,0:T(8,128)(2,1)}, bf16[64,768]{1,0:T(8,128)(2,1)S(1)}, u32[]{:S(2)}, u32[]{:S(2)}) collective-permute-start(bf16[64,768]{1,0:T(8,128)(2,1)} %get-tuple-element.8), channel_id=1, source_target_pairs={{0,16},{1,17},{2,18},{3,19},{4,20},{5,21},{6,22},{7,23},{8,24},{9,... | collective-permute-start | bytes 294920 | tf_op jit(solution)/shard_map/ppermute | solution.py:237
  7.1 15.0 %collective-permute-start.3 = (bf16[64,768]{1,0:T(8,128)(2,1)}, bf16[64,768]{1,0:T(8,128)(2,1)S(1)}, u32[]{:S(2)}, u32[]{:S(2)}) collective-permute-start(bf16[64,768]{1,0:T(8,128)(2,1)} %get-tuple-element.8), channel_id=1, source_target_pairs={{0,8},{1,9},{2,10},{3,11},{4,12},{5,13},{6,14},{7,15},{8,16},{9,17... | collective-permute-start | bytes 294920 | tf_op jit(solution)/shard_map/ppermute | solution.py:237
  8.3 34.9 %collective-permute-start = (bf16[12,64,512]{2,1,0:T(8,128)(2,1)}, bf16[12,64,512]{2,1,0:T(8,128)(2,1)S(1)}, u32[]{:S(2)}, u32[]{:S(2)}) collective-permute-start(bf16[12,64,512]{2,1,0:T(8,128)(2,1)} %get-tuple-element.7.refs_0_.e0), channel_id=1, source_target_pairs={{0,32},{32,0},{64,96},{96,64},{1,33},{33,1},{65,97},{97,65},{2,34}... | collective-permute-start | bytes 2359304 | tf_op jit(solution)/shard_map/ppermute | solution.py:233
  22.1 24.9 %copy-start = (bf16[12,64,512]{2,1,0:T(8,128)(2,1)}, bf16[12,64,512]{2,1,0:T(8,128)(2,1)S(1)}, u32[]{:S(2)}) copy-start(bf16[12,64,512]{2,1,0:T(8,128)(2,1)S(1)} %collective-permute-done.1.refs_0_.e2) | copy-start | bytes 2359300
  22.1 24.9 %collective-permute-start.2 = (bf16[12,64,512]{2,1,0:T(8,128)(2,1)S(1)}, bf16[12,64,512]{2,1,0:T(8,128)(2,1)S(1)}, u32[]{:S(2)}, u32[]{:S(2)}) collective-permute-start(bf16[12,64,512]{2,1,0:T(8,128)(2,1)S(1)} %collective-permute-done.1.refs_0_.e2), channel_id=1, source_target_pairs={{0,32},{32,0},{64,96},{96,64},{1,33},{33,1},{65,97},{97,65},{2,34}... | collective-permute-start | bytes 2359304 | tf_op jit(solution)/shard_map/ppermute | solution.py:233
  23.1 7.6 %collective-permute-start.8 = (bf16[64,768]{1,0:T(8,128)(2,1)S(1)}, bf16[64,768]{1,0:T(8,128)(2,1)S(1)}, u32[]{:S(2)}, u32[]{:S(2)}) collective-permute-start(bf16[64,768]{1,0:T(8,128)(2,1)S(1)} %add_add_fusion.1), channel_id=1, source_target_pairs={{0,6},{1,7},{2,0},{3,1},{4,2},{5,3},{6,4},{7,5},{8,14},{9,15},{10,... | collective-permute-start | bytes 294920 | tf_op jit(solution)/shard_map/ppermute | solution.py:237
  26.0 7.2 %collective-permute-start.7 = (bf16[64,768]{1,0:T(8,128)(2,1)S(1)}, bf16[64,768]{1,0:T(8,128)(2,1)S(1)}, u32[]{:S(2)}, u32[]{:S(2)}) collective-permute-start(bf16[64,768]{1,0:T(8,128)(2,1)S(1)} %add_add_fusion.1), channel_id=1, source_target_pairs={{0,4},{1,5},{2,6},{3,7},{4,0},{5,1},{6,2},{7,3},{8,12},{9,13},{10,... | collective-permute-start | bytes 294920 | tf_op jit(solution)/shard_map/ppermute | solution.py:237
  26.7 7.6 %collective-permute-start.6 = (bf16[64,768]{1,0:T(8,128)(2,1)S(1)}, bf16[64,768]{1,0:T(8,128)(2,1)S(1)}, u32[]{:S(2)}, u32[]{:S(2)}) collective-permute-start(bf16[64,768]{1,0:T(8,128)(2,1)S(1)} %add_add_fusion.1), channel_id=1, source_target_pairs={{0,2},{1,3},{2,4},{3,5},{4,6},{5,7},{6,0},{7,1},{8,10},{9,11},{10,... | collective-permute-start | bytes 294920 | tf_op jit(solution)/shard_map/ppermute | solution.py:237
  34.4 6.3 %collective-permute-start.9 = (bf16[64,768]{1,0:T(8,128)(2,1)S(1)}, bf16[64,768]{1,0:T(8,128)(2,1)S(1)}, u32[]{:S(2)}, u32[]{:S(2)}) collective-permute-start(bf16[64,768]{1,0:T(8,128)(2,1)S(1)} %add_add_fusion), channel_id=1, source_target_pairs={{0,1},{1,0},{2,3},{3,2},{4,5},{5,4},{6,7},{7,6},{8,9},{9,8},{10,11... | collective-permute-start | bytes 294920 | tf_op jit(solution)/shard_map/ppermute | solution.py:237
  41.3 9.4 %collective-permute-start.12 = (bf16[16,768]{1,0:T(8,128)(2,1)S(1)}, bf16[16,768]{1,0:T(8,128)(2,1)S(1)}, u32[]{:S(2)}, u32[]{:S(2)}) collective-permute-start(bf16[16,768]{1,0:T(8,128)(2,1)S(1)} %get-tuple-element.9), channel_id=1, source_target_pairs={{0,96},{32,64},{64,32},{96,0},{1,97},{33,65},{65,33},{97,1},{2,98}... | collective-permute-start | bytes 73736 | tf_op jit(solution)/shard_map/ppermute | solution.py:233
  41.3 9.5 %collective-permute-start.11 = (bf16[16,768]{1,0:T(8,128)(2,1)S(1)}, bf16[16,768]{1,0:T(8,128)(2,1)S(1)}, u32[]{:S(2)}, u32[]{:S(2)}) collective-permute-start(bf16[16,768]{1,0:T(8,128)(2,1)S(1)} %get-tuple-element.10), channel_id=1, source_target_pairs={{0,64},{32,96},{64,0},{96,32},{1,65},{33,97},{65,1},{97,33},{2,66}... | collective-permute-start | bytes 73736 | tf_op jit(solution)/shard_map/ppermute | solution.py:233
  42.1 8.7 %collective-permute-start.10 = (bf16[16,768]{1,0:T(8,128)(2,1)S(1)}, bf16[16,768]{1,0:T(8,128)(2,1)S(1)}, u32[]{:S(2)}, u32[]{:S(2)}) collective-permute-start(bf16[16,768]{1,0:T(8,128)(2,1)S(1)} %get-tuple-element.11), channel_id=1, source_target_pairs={{0,32},{32,0},{64,96},{96,64},{1,33},{33,1},{65,97},{97,65},{2,34}... | collective-permute-start | bytes 73736 | tf_op jit(solution)/shard_map/ppermute | solution.py:233
  43.2 0.9 copy-start.1
  47.0 0.9 copy-start.2
  50.8 0.6 copy-start.4
  50.8 0.6 copy-start.5
  50.8 0.6 copy-start.6
  92.9 8.6 %collective-permute-start.13 = (f32[144,128]{1,0:T(8,128)S(1)}, f32[144,128]{1,0:T(8,128)S(1)}, u32[]{:S(2)}, u32[]{:S(2)}) collective-permute-start(f32[144,128]{1,0:T(8,128)S(1)} %convert_reduce_fusion), channel_id=1, source_target_pairs={{0,0},{1,1},{2,32},{3,33},{4,64},{5,65},{6,96},{7,97},{8,8},{9,9},... | collective-permute-start | bytes 221192 | tf_op jit(solution)/shard_map/ppermute | solution.py:264
  101.5 0.6 copy-start.3

commit v2 on v1

--- a/solution.py
+++ b/solution.py
@@ -19,6 +19,10 @@
 series_floor = 1.0
 spread_floor = 0.05
 shrink_factor = 0.9
+
+
+def near(x):
+    return pltpu.with_memory_space_constraint(x, pltpu.VMEM)
 
 
 def iota(shape, dim):
@@ -68,8 +72,8 @@
     return pl.pallas_call(
         window_kernel,
         out_shape=(
-            jax.ShapeDtypeStruct((EP, SL * TR, width), BF16),
-            jax.ShapeDtypeStruct((GR * KL, EP * SL * TR), BF16),
+            pltpu.VMEM((EP, SL * TR, width), BF16),
+            pltpu.VMEM((GR * KL, EP * SL * TR), BF16),
         ),
         in_specs=[
             pl.BlockSpec(memory_space=pltpu.SMEM),
@@ -78,6 +82,7 @@
         ],
         out_specs=(pl.BlockSpec(memory_space=pltpu.VMEM), pl.BlockSpec(memory_space=pltpu.VMEM)),
         scratch_shapes=[pltpu.VMEM((EP * TR, series.shape[1]), BF16)],
+        compiler_params=pltpu.CompilerParams(vmem_limit_bytes=8 << 20),
         name="windows",
     )(offsets, selected, series)
 
@@ -104,11 +109,12 @@
 def norms(e0, e1, first):
     return pl.pallas_call(
         lambda *refs: norm_kernel(first, *refs),
-        out_shape=jax.ShapeDtypeStruct((EP, SB, e0.shape[2]), F32),
+        out_shape=pltpu.VMEM((EP, SB, e0.shape[2]), F32),
         in_specs=[pl.BlockSpec(memory_space=pltpu.VMEM)] * 2,
         out_specs=pl.BlockSpec(memory_space=pltpu.VMEM),
+        compiler_params=pltpu.CompilerParams(vmem_limit_bytes=4 << 20),
         name="norms",
-    )(e0, e1)
+    )(near(e0), near(e1))
 
 
 def kernel_kernel(
@@ -178,7 +184,7 @@
     width = epochs[0].shape[2]
     return pl.pallas_call(
         kernel_kernel,
-        out_shape=jax.ShapeDtypeStruct((devices, 3 * EP * SL, 128), dtype),
+        out_shape=pltpu.VMEM((devices, 3 * EP * SL, 128), dtype),
         in_specs=[pl.BlockSpec(memory_space=pltpu.VMEM)] * (2 * GR + 2),
         out_specs=pl.BlockSpec(memory_space=pltpu.VMEM),
         scratch_shapes=[
@@ -189,8 +195,9 @@
             pltpu.VMEM((2, EP * SB, width), BF16),
             pltpu.VMEM((3, EP * SB, 128), F32),
         ],
+        compiler_params=pltpu.CompilerParams(vmem_limit_bytes=20 << 20),
         name="partial_kernels",
-    )(*epochs, *slabs, *powers)
+    )(*map(near, (*epochs, *slabs, *powers)))
 
 
 def order_kernel(y_ref, o_ref):
@@ -217,8 +224,9 @@
         out_shape=jax.ShapeDtypeStruct((2, EP * SL, EP * SB), F32),
         in_specs=[pl.BlockSpec(memory_space=pltpu.VMEM)],
         out_specs=pl.BlockSpec(memory_space=pltpu.VMEM),
+        compiler_params=pltpu.CompilerParams(vmem_limit_bytes=4 << 20),
         name="in_order",
-    )(tile)
+    )(near(tile))
 
 
 def ring(step, size, stride, devices):
@@ -243,15 +251,15 @@
     own, picked = take_windows(series, offsets, selected)
     across = swapped(own, 2)
     beside = swapped(own, 1)
-    near = norms(own, beside, 0)
+    first = norms(own, beside, 0)
     slab = summed(picked, 4, 8, devices)
     slab = summed(slab, 4, 2, devices)
     slab = summed(slab, 2, 1, devices)
     beyond = swapped(across, 1)
-    far = norms(across, beyond, 2)
+    second = norms(across, beyond, 2)
     parts = [slab[r * KL : (r + 1) * KL] for r in range(GR)]
     parts = [parts[0]] + [swapped(parts[r], r) for r in range(1, GR)]
-    tiles = partial_kernels((own, beside, across, beyond), parts, (near, far), devices, F32)
+    tiles = partial_kernels((own, beside, across, beyond), parts, (first, second), devices, F32)
     tiles = lax.all_to_all(tiles.astype(LINK), "vox", split_axis=0, concat_axis=0, tiled=True)
     tile = jnp.sum(tiles.astype(F32), axis=0)
     turn = [

time: 104 us -> 91 us (0.88)
  Pallas kernels: 21.3 us -> 11.3 us
  other arithmetic: 3.06 us -> 0.4 us
  local copies, waits for them, and re-layouts: 3.63 us -> 2.58 us
    pallas_call x4, Pallas kernels: 19.5 us -> 10.4 us  [the longest x1 7.58 us: partial_kernels(): pl.pallas_call(kernel_kernel, out_shape=pltpu.VMEM((devices, 3 * EP * SL,...]
    convert_element_type x1, other arithmetic: 1.82 us -> 0.16 us  [body(): tiles.astype(LINK)]
    unnamed x14 -> x6, local copies, waits for them, and re-layouts: 3.02 us -> 2.58 us
  transfers between devices with their start and end apart: 14 -> 14, of which waited for: 6 -> 7; matrix products, arithmetic and copies ran while one was open for 2% -> 0% of each run, Pallas kernels for 6% -> 2%
where the time goes in v2:
time: 91 us; the launch traced here: 90.8 us
  waiting for transfers between devices  29.3 us (32%)
  blocking collectives  28.2 us (31%)
  starting transfers between devices  18.9 us (21%)
  Pallas kernels  11.3 us (12%)
  local copies, waits for them, and re-layouts  2.58 us (3%)
    all_to_all x1, blocking collectives, body(): lax.all_to_all(tiles.astype(LINK), 'vox', split_axis=0, concat_axis=0, ti...  28.2 us
    ppermute x6, waiting for transfers between devices, swapped(): return lax.ppermute(x, 'subj', [(n, n ^ r) for n in range(GR)])  14.1 us
    ppermute x7, starting transfers between devices, summed(): lax.ppermute(x, 'vox', ring(n, size, stride, devices))  12.3 us
    ppermute x7, waiting for transfers between devices, summed(): lax.ppermute(x, 'vox', ring(n, size, stride, devices))  10.8 us
    pallas_call x1, Pallas kernels, partial_kernels(): pl.pallas_call(kernel_kernel, out_shape=pltpu.VMEM((devices, 3 * EP * SL,...  7.58 us
    ppermute x1, waiting for transfers between devices, body(): return in_order(lax.ppermute(tile, ('subj', 'vox'), turn))  4.42 us
    ppermute x1, starting transfers between devices, body(): return in_order(lax.ppermute(tile, ('subj', 'vox'), turn))  4.22 us
    unnamed x6, local copies, waits for them, and re-layouts  2.58 us
  transfers between devices with their start and end apart: 14, of which 7 were waited for; matrix products, arithmetic and copies ran while one was open for 0% of the time, Pallas kernels for 2%

profile of v2, /device:TPU:8, one launch (start us, length us, event | category | flops | bytes accessed | tf_op | source)
XLA Modules:
  0.0 90.8 jit_solution(5115131844136300767)
XLA Ops:
  0.0 1.2 %copy-done = bf16[4,256,512]{2,1,0:T(8,128)(2,1)S(1)} copy-done((bf16[4,256,512]{2,1,0:T(8,128)(2,1)S(1)}, bf16[4,256,512]{2,1,0:T(8,128)(2,1)}, u32[]{:S(2)}) %copy-start) | copy-done | bytes 1048600
  1.2 0.7 copy-done.1
  1.9 0.7 copy-done.2
  2.6 1.3 %windows.1 = (bf16[12,64,512]{2,1,0:T(8,128)(2,1)S(1)}, bf16[64,768]{1,0:T(8,128)(2,1)S(1)}) custom-call(s32[16,12]{1,0:T(8,128)S(1)} %copy-done.1, s32[64]{0:T(128)S(1)} %copy-done.2, bf16[4,256,512]{2,1,0:T(8,128)(2,1)S(1)} %copy-done), custom_call_target="tpu_custom_call" | custom-call | tf_op jit(solution)/shard_map/windows/pallas_call | solution.py:72
  3.9 0.4 collective-permute-start.1
  4.3 4.1 %collective-permute-start.5 = (bf16[64,768]{1,0:T(8,128)(2,1)S(1)}, bf16[64,768]{1,0:T(8,128)(2,1)S(1)}, u32[]{:S(2)}, u32[]{:S(2)}) collective-permute-start(bf16[64,768]{1,0:T(8,128)(2,1)S(1)} %get-tuple-element.8), channel_id=1, source_target_pairs={{0,24},{1,25},{2,26},{3,27},{4,28},{5,29},{6,30},{7,31},{8,0},{9,1... | collective-permute-start | bytes 294920 | tf_op jit(solution)/shard_map/ppermute | solution.py:245
  8.5 0.0 collective-permute-start.4
  8.5 1.3 %collective-permute-start.3 = (bf16[64,768]{1,0:T(8,128)(2,1)S(1)}, bf16[64,768]{1,0:T(8,128)(2,1)S(1)}, u32[]{:S(2)}, u32[]{:S(2)}) collective-permute-start(bf16[64,768]{1,0:T(8,128)(2,1)S(1)} %get-tuple-element.8), channel_id=1, source_target_pairs={{0,8},{1,9},{2,10},{3,11},{4,12},{5,13},{6,14},{7,15},{8,16},{9,17... | collective-permute-start | bytes 294920 | tf_op jit(solution)/shard_map/ppermute | solution.py:245
  9.8 0.0 collective-permute-start
  9.8 13.5 %collective-permute-done.1.refs_0_.e2 = bf16[12,64,512]{2,1,0:T(8,128)(2,1)S(1)} collective-permute-done((bf16[12,64,512]{2,1,0:T(8,128)(2,1)S(1)}, bf16[12,64,512]{2,1,0:T(8,128)(2,1)S(1)}, u32[]{:S(2)}, u32[]{:S(2)}) %collective-permute-start.1) | collective-permute-done | bytes 786464 | tf_op jit(solution)/shard_map/ppermute | solution.py:241
  23.3 0.0 collective-permute-done.3
  23.3 2.8 %collective-permute-start.8 = (bf16[64,768]{1,0:T(8,128)(2,1)S(1)}, bf16[64,768]{1,0:T(8,128)(2,1)S(1)}, u32[]{:S(2)}, u32[]{:S(2)}) collective-permute-start(bf16[64,768]{1,0:T(8,128)(2,1)S(1)} %add_add_fusion.1), channel_id=1, source_target_pairs={{0,6},{1,7},{2,0},{3,1},{4,2},{5,3},{6,4},{7,5},{8,14},{9,15},{10,... | collective-permute-start | bytes 294920 | tf_op jit(solution)/shard_map/ppermute | solution.py:245
  26.2 0.8 collective-permute-start.7
  27.0 0.9 collective-permute-start.6
  27.9 3.2 %collective-permute-done.8 = bf16[64,768]{1,0:T(8,128)(2,1)S(1)} collective-permute-done((bf16[64,768]{1,0:T(8,128)(2,1)S(1)}, bf16[64,768]{1,0:T(8,128)(2,1)S(1)}, u32[]{:S(2)}, u32[]{:S(2)}) %collective-permute-start.8) | collective-permute-done | bytes 98336 | tf_op jit(solution)/shard_map/ppermute | solution.py:245
  31.0 2.3 %collective-permute-done.7 = bf16[64,768]{1,0:T(8,128)(2,1)S(1)} collective-permute-done((bf16[64,768]{1,0:T(8,128)(2,1)S(1)}, bf16[64,768]{1,0:T(8,128)(2,1)S(1)}, u32[]{:S(2)}, u32[]{:S(2)}) %collective-permute-start.7) | collective-permute-done | bytes 98336 | tf_op jit(solution)/shard_map/ppermute | solution.py:245
  33.3 1.4 %collective-permute-done.6 = bf16[64,768]{1,0:T(8,128)(2,1)S(1)} collective-permute-done((bf16[64,768]{1,0:T(8,128)(2,1)S(1)}, bf16[64,768]{1,0:T(8,128)(2,1)S(1)}, u32[]{:S(2)}, u32[]{:S(2)}) %collective-permute-start.6) | collective-permute-done | bytes 98336 | tf_op jit(solution)/shard_map/ppermute | solution.py:245
  34.7 2.4 %collective-permute-start.9 = (bf16[64,768]{1,0:T(8,128)(2,1)S(1)}, bf16[64,768]{1,0:T(8,128)(2,1)S(1)}, u32[]{:S(2)}, u32[]{:S(2)}) collective-permute-start(bf16[64,768]{1,0:T(8,128)(2,1)S(1)} %add_add_fusion), channel_id=1, source_target_pairs={{0,1},{1,0},{2,3},{3,2},{4,5},{5,4},{6,7},{7,6},{8,9},{9,8},{10,11... | collective-permute-start | bytes 294920 | tf_op jit(solution)/shard_map/ppermute | solution.py:245
  37.1 3.9 %collective-permute-done.9 = bf16[64,768]{1,0:T(8,128)(2,1)S(1)} collective-permute-done((bf16[64,768]{1,0:T(8,128)(2,1)S(1)}, bf16[64,768]{1,0:T(8,128)(2,1)S(1)}, u32[]{:S(2)}, u32[]{:S(2)}) %collective-permute-start.9) | collective-permute-done | bytes 98336 | tf_op jit(solution)/shard_map/ppermute | solution.py:245
  41.1 0.1 collective-permute-start.12
  41.2 0.8 collective-permute-start.11
  42.0 1.1 %collective-permute-start.10 = (bf16[16,768]{1,0:T(8,128)(2,1)S(1)}, bf16[16,768]{1,0:T(8,128)(2,1)S(1)}, u32[]{:S(2)}, u32[]{:S(2)}) collective-permute-start(bf16[16,768]{1,0:T(8,128)(2,1)S(1)} %get-tuple-element.11), channel_id=1, source_target_pairs={{0,32},{32,0},{64,96},{96,64},{1,33},{33,1},{65,97},{97,65},{2,34}... | collective-permute-start | bytes 73736 | tf_op jit(solution)/shard_map/ppermute | solution.py:241
  43.0 0.8 norms.2.na
  43.8 0.8 norms.3.nb
  44.5 0.5 collective-permute-done.11.s2
  45.1 7.6 %partial_kernels.1 = f32[32,144,128]{2,1,0:T(8,128)S(1)} custom-call(bf16[12,64,512]{2,1,0:T(8,128)(2,1)S(1)} %get-tuple-element.7.refs_0_.e0, bf16[12,64,512]{2,1,0:T(8,128)(2,1)S(1)} %collective-permute-done.refs_1_.e1, bf16[12,64,512]{2,1,0:T(8,128)(2,1)S(1)} %collective-permute-done.1.refs_0_.e2, ...), custom_call_target="tpu_custom_call" | custom-call | tf_op jit(solution)/shard_map/partial_kernels/pallas_call | solution.py:185
  52.7 0.2 convert_element_type.6
  52.8 28.2 %all_to_all.5 = f16[32,144,128]{2,1,0:T(8,128)(2,1)S(1)} all-to-all(f16[32,144,128]{2,1,0:T(8,128)(2,1)S(1)} %convert_element_type.6), channel_id=1, replica_groups=mesh['subj'=4,'vox'=32] {'vox'}, dimensions={0} | all-to-all | bytes 2359296 | tf_op jit(solution)/shard_map/all_to_all | solution.py:263
  81.1 0.2 convert_reduce_fusion
  81.2 4.2 %collective-permute-start.13 = (f32[144,128]{1,0:T(8,128)S(1)}, f32[144,128]{1,0:T(8,128)S(1)}, u32[]{:S(2)}, u32[]{:S(2)}) collective-permute-start(f32[144,128]{1,0:T(8,128)S(1)} %convert_reduce_fusion), channel_id=1, source_target_pairs={{0,0},{1,1},{2,32},{3,33},{4,64},{5,65},{6,96},{7,97},{8,8},{9,9},... | collective-permute-start | bytes 221192 | tf_op jit(solution)/shard_map/ppermute | solution.py:272
  85.5 4.4 %collective-permute-done.13.y_ref = f32[144,128]{1,0:T(8,128)S(1)} collective-permute-done((f32[144,128]{1,0:T(8,128)S(1)}, f32[144,128]{1,0:T(8,128)S(1)}, u32[]{:S(2)}, u32[]{:S(2)}) %collective-permute-start.13) | collective-permute-done | bytes 73760 | tf_op jit(solution)/shard_map/ppermute | solution.py:272
  89.9 0.9 %in_order.1 = f32[2,48,192]{2,1,0:T(8,128)} custom-call(f32[144,128]{1,0:T(8,128)S(1)} %collective-permute-done.13.y_ref), custom_call_target="tpu_custom_call" | custom-call | tf_op jit(solution)/shard_map/in_order/pallas_call | solution.py:222
  (14 shorter events, 0.1 us)
Async XLA Ops:
  0.0 1.2 %copy-start = (bf16[4,256,512]{2,1,0:T(8,128)(2,1)S(1)}, bf16[4,256,512]{2,1,0:T(8,128)(2,1)}, u32[]{:S(2)}) copy-start(bf16[4,256,512]{2,1,0:T(8,128)(2,1)} %series_ref.1) | copy-start | bytes 3145732
  1.2 0.7 copy-start.1
  1.9 0.7 copy-start.2
  3.9 19.4 %collective-permute-start.1 = (bf16[12,64,512]{2,1,0:T(8,128)(2,1)S(1)}, bf16[12,64,512]{2,1,0:T(8,128)(2,1)S(1)}, u32[]{:S(2)}, u32[]{:S(2)}) collective-permute-start(bf16[12,64,512]{2,1,0:T(8,128)(2,1)S(1)} %get-tuple-element.7.refs_0_.e0), channel_id=1, source_target_pairs={{0,64},{32,96},{64,0},{96,32},{1,65},{33,97},{65,1},{97,33},{2,66}... | collective-permute-start | bytes 2359304 | tf_op jit(solution)/shard_map/ppermute | solution.py:241
  4.3 18.9 %collective-permute-start.5 = (bf16[64,768]{1,0:T(8,128)(2,1)S(1)}, bf16[64,768]{1,0:T(8,128)(2,1)S(1)}, u32[]{:S(2)}, u32[]{:S(2)}) collective-permute-start(bf16[64,768]{1,0:T(8,128)(2,1)S(1)} %get-tuple-element.8), channel_id=1, source_target_pairs={{0,24},{1,25},{2,26},{3,27},{4,28},{5,29},{6,30},{7,31},{8,0},{9,1... | collective-permute-start | bytes 294920 | tf_op jit(solution)/shard_map/ppermute | solution.py:245
  8.5 14.8 %collective-permute-start.4 = (bf16[64,768]{1,0:T(8,128)(2,1)S(1)}, bf16[64,768]{1,0:T(8,128)(2,1)S(1)}, u32[]{:S(2)}, u32[]{:S(2)}) collective-permute-start(bf16[64,768]{1,0:T(8,128)(2,1)S(1)} %get-tuple-element.8), channel_id=1, source_target_pairs={{0,16},{1,17},{2,18},{3,19},{4,20},{5,21},{6,22},{7,23},{8,24},{9,... | collective-permute-start | bytes 294920 | tf_op jit(solution)/shard_map/ppermute | solution.py:245
  8.5 14.8 %collective-permute-start.3 = (bf16[64,768]{1,0:T(8,128)(2,1)S(1)}, bf16[64,768]{1,0:T(8,128)(2,1)S(1)}, u32[]{:S(2)}, u32[]{:S(2)}) collective-permute-start(bf16[64,768]{1,0:T(8,128)(2,1)S(1)} %get-tuple-element.8), channel_id=1, source_target_pairs={{0,8},{1,9},{2,10},{3,11},{4,12},{5,13},{6,14},{7,15},{8,16},{9,17... | collective-permute-start | bytes 294920 | tf_op jit(solution)/shard_map/ppermute | solution.py:245
  9.8 33.3 %collective-permute-start = (bf16[12,64,512]{2,1,0:T(8,128)(2,1)S(1)}, bf16[12,64,512]{2,1,0:T(8,128)(2,1)S(1)}, u32[]{:S(2)}, u32[]{:S(2)}) collective-permute-start(bf16[12,64,512]{2,1,0:T(8,128)(2,1)S(1)} %get-tuple-element.7.refs_0_.e0), channel_id=1, source_target_pairs={{0,32},{32,0},{64,96},{96,64},{1,33},{33,1},{65,97},{97,65},{2,34}... | collective-permute-start | bytes 2359304 | tf_op jit(solution)/shard_map/ppermute | solution.py:241
  23.3 20.5 %collective-permute-start.2 = (bf16[12,64,512]{2,1,0:T(8,128)(2,1)S(1)}, bf16[12,64,512]{2,1,0:T(8,128)(2,1)S(1)}, u32[]{:S(2)}, u32[]{:S(2)}) collective-permute-start(bf16[12,64,512]{2,1,0:T(8,128)(2,1)S(1)} %collective-permute-done.1.refs_0_.e2), channel_id=1, source_target_pairs={{0,32},{32,0},{64,96},{96,64},{1,33},{33,1},{65,97},{97,65},{2,34}... | collective-permute-start | bytes 2359304 | tf_op jit(solution)/shard_map/ppermute | solution.py:241
  23.3 7.7 %collective-permute-start.8 = (bf16[64,768]{1,0:T(8,128)(2,1)S(1)}, bf16[64,768]{1,0:T(8,128)(2,1)S(1)}, u32[]{:S(2)}, u32[]{:S(2)}) collective-permute-start(bf16[64,768]{1,0:T(8,128)(2,1)S(1)} %add_add_fusion.1), channel_id=1, source_target_pairs={{0,6},{1,7},{2,0},{3,1},{4,2},{5,3},{6,4},{7,5},{8,14},{9,15},{10,... | collective-permute-start | bytes 294920 | tf_op jit(solution)/shard_map/ppermute | solution.py:245
  26.2 7.2 %collective-permute-start.7 = (bf16[64,768]{1,0:T(8,128)(2,1)S(1)}, bf16[64,768]{1,0:T(8,128)(2,1)S(1)}, u32[]{:S(2)}, u32[]{:S(2)}) collective-permute-start(bf16[64,768]{1,0:T(8,128)(2,1)S(1)} %add_add_fusion.1), channel_id=1, source_target_pairs={{0,4},{1,5},{2,6},{3,7},{4,0},{5,1},{6,2},{7,3},{8,12},{9,13},{10,... | collective-permute-start | bytes 294920 | tf_op jit(solution)/shard_map/ppermute | solution.py:245
  27.0 7.7 %collective-permute-start.6 = (bf16[64,768]{1,0:T(8,128)(2,1)S(1)}, bf16[64,768]{1,0:T(8,128)(2,1)S(1)}, u32[]{:S(2)}, u32[]{:S(2)}) collective-permute-start(bf16[64,768]{1,0:T(8,128)(2,1)S(1)} %add_add_fusion.1), channel_id=1, source_target_pairs={{0,2},{1,3},{2,4},{3,5},{4,6},{5,7},{6,0},{7,1},{8,10},{9,11},{10,... | collective-permute-start | bytes 294920 | tf_op jit(solution)/shard_map/ppermute | solution.py:245
  34.7 6.3 %collective-permute-start.9 = (bf16[64,768]{1,0:T(8,128)(2,1)S(1)}, bf16[64,768]{1,0:T(8,128)(2,1)S(1)}, u32[]{:S(2)}, u32[]{:S(2)}) collective-permute-start(bf16[64,768]{1,0:T(8,128)(2,1)S(1)} %add_add_fusion), channel_id=1, source_target_pairs={{0,1},{1,0},{2,3},{3,2},{4,5},{5,4},{6,7},{7,6},{8,9},{9,8},{10,11... | collective-permute-start | bytes 294920 | tf_op jit(solution)/shard_map/ppermute | solution.py:245
  41.1 3.5 %collective-permute-start.12 = (bf16[16,768]{1,0:T(8,128)(2,1)S(1)}, bf16[16,768]{1,0:T(8,128)(2,1)S(1)}, u32[]{:S(2)}, u32[]{:S(2)}) collective-permute-start(bf16[16,768]{1,0:T(8,128)(2,1)S(1)} %get-tuple-element.9), channel_id=1, source_target_pairs={{0,96},{32,64},{64,32},{96,0},{1,97},{33,65},{65,33},{97,1},{2,98}... | collective-permute-start | bytes 73736 | tf_op jit(solution)/shard_map/ppermute | solution.py:241
  41.2 3.9 %collective-permute-start.11 = (bf16[16,768]{1,0:T(8,128)(2,1)S(1)}, bf16[16,768]{1,0:T(8,128)(2,1)S(1)}, u32[]{:S(2)}, u32[]{:S(2)}) collective-permute-start(bf16[16,768]{1,0:T(8,128)(2,1)S(1)} %get-tuple-element.10), channel_id=1, source_target_pairs={{0,64},{32,96},{64,0},{96,32},{1,65},{33,97},{65,1},{97,33},{2,66}... | collective-permute-start | bytes 73736 | tf_op jit(solution)/shard_map/ppermute | solution.py:241
  42.0 3.1 %collective-permute-start.10 = (bf16[16,768]{1,0:T(8,128)(2,1)S(1)}, bf16[16,768]{1,0:T(8,128)(2,1)S(1)}, u32[]{:S(2)}, u32[]{:S(2)}) collective-permute-start(bf16[16,768]{1,0:T(8,128)(2,1)S(1)} %get-tuple-element.11), channel_id=1, source_target_pairs={{0,32},{32,0},{64,96},{96,64},{1,33},{33,1},{65,97},{97,65},{2,34}... | collective-permute-start | bytes 73736 | tf_op jit(solution)/shard_map/ppermute | solution.py:241
  81.2 8.6 %collective-permute-start.13 = (f32[144,128]{1,0:T(8,128)S(1)}, f32[144,128]{1,0:T(8,128)S(1)}, u32[]{:S(2)}, u32[]{:S(2)}) collective-permute-start(f32[144,128]{1,0:T(8,128)S(1)} %convert_reduce_fusion), channel_id=1, source_target_pairs={{0,0},{1,1},{2,32},{3,33},{4,64},{5,65},{6,96},{7,97},{8,8},{9,9},... | collective-permute-start | bytes 221192 | tf_op jit(solution)/shard_map/ppermute | solution.py:272

commit v3 on v2

--- a/solution.py
+++ b/solution.py
@@ -12,6 +12,9 @@
 SL = 4
 SB = GR * SL
 KL = 16
+HALF = EP * SB // 3
+BLOCKS = ((0, 0), (0, 1), (0, 2), (1, 1), (1, 2), (2, 2))
+QUARTER = len(BLOCKS) * HALF // GR
 VOX = 16384
 F32 = jnp.float32
 BF16 = jnp.bfloat16
@@ -84,7 +87,11 @@
         scratch_shapes=[pltpu.VMEM((EP * TR, series.shape[1]), BF16)],
         compiler_params=pltpu.CompilerParams(vmem_limit_bytes=8 << 20),
         name="windows",
-    )(offsets, selected, series)
+    )(
+        pltpu.with_memory_space_constraint(offsets, pltpu.HBM),
+        pltpu.with_memory_space_constraint(selected, pltpu.HBM),
+        pltpu.with_memory_space_constraint(series, pltpu.HBM),
+    )
 
 
 def meeting(j, first, count):
@@ -118,7 +125,7 @@
 
 
 def kernel_kernel(
-    e0, e1, e2, e3, s0, s1, s2, s3, na, nb, o_ref, lh_ref, ll_ref, c_ref, n_ref, z_ref, g_ref
+    e0, e1, e2, e3, s0, s1, s2, s3, na, nb, o_ref, lh_ref, ll_ref, c_ref, n_ref, z_ref
 ):
     j = lax.axis_index("subj")
     epochs = (e0, e1, e2, e3)
@@ -152,6 +159,7 @@
         c_ref[e] = dot(lh_ref[...], x) + dot(ll_ref[...], x)
 
     def pair(q, carry):
+        base = (q // 2) * 8 + q % 2
         for h in range(2):
             start = pl.multiple_of((q * 2 + h) * SB, SB)
             for c in range(0, width, 128):
@@ -167,14 +175,13 @@
                 scale = lax.rsqrt(spread * (1.0 / EP) + 4.0 * spread_floor)
                 for e in range(EP):
                     z_ref[h, e * SB : (e + 1) * SB, c : c + 128] = (fisher[e] * scale).astype(BF16)
-            product = dot_nt(z_ref[h], z_ref[h])
-            g_ref[h] = product[:, 0:128]
-            g_ref[2, :, h * 64 : (h + 1) * 64] = product[:, 128 : EP * SB]
-        base = (q // 2) * 8 + q % 2
-        for r in range(GR):
-            lines = pl.ds(r, EP * SL, stride=GR)
-            both = jnp.concatenate([g_ref[n, lines, :] for n in range(3)], axis=0)
-            o_ref[base + 2 * r] = both.astype(o_ref.dtype)
+            for n, (low, high) in enumerate(BLOCKS):
+                left = z_ref[h, low * HALF : (low + 1) * HALF, :]
+                tile = dot_nt(left, z_ref[h, high * HALF : (high + 1) * HALF, :])
+                for first in range(0, HALF, HALF // 2):
+                    at, line = divmod(n * HALF + first, QUARTER)
+                    part = tile[first : first + HALF // 2]
+                    o_ref[base + 2 * at, line : line + HALF // 2, h * HALF : (h + 1) * HALF] = part
         return carry
 
     lax.fori_loop(0, KL // 2, pair, 0)
@@ -184,7 +191,7 @@
     width = epochs[0].shape[2]
     return pl.pallas_call(
         kernel_kernel,
-        out_shape=pltpu.VMEM((devices, 3 * EP * SL, 128), dtype),
+        out_shape=pltpu.VMEM((devices, QUARTER, 2 * HALF), dtype),
         in_specs=[pl.BlockSpec(memory_space=pltpu.VMEM)] * (2 * GR + 2),
         out_specs=pl.BlockSpec(memory_space=pltpu.VMEM),
         scratch_shapes=[
@@ -193,40 +200,55 @@
             pltpu.VMEM((EP, KL * SB, width), F32),
             pltpu.VMEM((EP, SB, width), F32),
             pltpu.VMEM((2, EP * SB, width), BF16),
-            pltpu.VMEM((3, EP * SB, 128), F32),
         ],
         compiler_params=pltpu.CompilerParams(vmem_limit_bytes=20 << 20),
         name="partial_kernels",
     )(*map(near, (*epochs, *slabs, *powers)))
 
 
-def order_kernel(y_ref, o_ref):
-    rows = EP * SL
+def order_kernel(y0, y1, y2, y3, o_ref, b_ref, k_ref):
+    j = lax.axis_index("subj")
+    for r, y in enumerate((y0, y1, y2, y3)):
+        b_ref[pl.ds(pl.multiple_of((j ^ r) * QUARTER, QUARTER), QUARTER), :] = y[...]
+    for n, (low, high) in enumerate(BLOCKS):
+        tile = b_ref[n * HALF : (n + 1) * HALF, :]
+        mirrored = tile.T
+        for h in range(2):
+            block = tile[:, h * HALF : (h + 1) * HALF]
+            at = (high % 2) * HALF
+            k_ref[h, high // 2, low * HALF : (low + 1) * HALF, at : at + HALF] = block
+            if low != high:
+                block = mirrored[h * HALF : (h + 1) * HALF]
+                at = (low % 2) * HALF
+                k_ref[h, low // 2, high * HALF : (high + 1) * HALF, at : at + HALF] = block
     cols = EP * SB
     source = iota((cols, cols), 0)
-    target = (source % GR) * rows + ((source // GR) % SL) * EP + source // SB
+    target = (source % GR) * (EP * SL) + ((source // GR) % SL) * EP + source // SB
     column = jnp.where(iota((cols, cols), 1) == target, 1.0, 0.0).astype(BF16)
     for h in range(2):
         lines = []
         for s in range(SL):
-            left = y_ref[pl.ds(h * rows + s, EP, stride=SL), :]
-            right = y_ref[pl.ds(2 * rows + s, EP, stride=SL), :]
-            lines.append(jnp.concatenate([left, right[:, h * 64 : (h + 1) * 64]], axis=1))
+            own = pl.ds(s * GR + j, EP, stride=SB)
+            lines.append(jnp.concatenate([k_ref[h, 0, own, :], k_ref[h, 1, own, :][:, 0:HALF]], axis=1))
         whole = jnp.concatenate(lines, axis=0)
         high, _ = split(whole)
         middle, low = split(whole - high.astype(F32))
         o_ref[h] = (dot(high, column) + dot(middle, column) + dot(low, column)) * (1.0 / VOX)
 
 
-def in_order(tile):
+def in_order(tiles):
     return pl.pallas_call(
         order_kernel,
         out_shape=jax.ShapeDtypeStruct((2, EP * SL, EP * SB), F32),
-        in_specs=[pl.BlockSpec(memory_space=pltpu.VMEM)],
+        in_specs=[pl.BlockSpec(memory_space=pltpu.VMEM)] * GR,
         out_specs=pl.BlockSpec(memory_space=pltpu.VMEM),
+        scratch_shapes=[
+            pltpu.VMEM((len(BLOCKS) * HALF, 2 * HALF), F32),
+            pltpu.VMEM((2, 2, EP * SB, 2 * HALF), F32),
+        ],
         compiler_params=pltpu.CompilerParams(vmem_limit_bytes=4 << 20),
         name="in_order",
-    )(near(tile))
+    )(*map(near, tiles))
 
 
 def ring(step, size, stride, devices):
@@ -269,7 +291,8 @@
         for x in range(4)
         for y in range(2)
     ]
-    return in_order(lax.ppermute(tile, ("subj", "vox"), turn))
+    tile = lax.ppermute(tile, ("subj", "vox"), turn)
+    return in_order([tile] + [swapped(tile, r) for r in range(1, GR)])
 
 
 def solution(mesh):

time: 91 us -> 90.9 us (level); the launches traced: 90.8 us -> 89.7 us
  blocking collectives: 28.2 us -> 24 us
  waiting for transfers between devices: 29.3 us -> 31.9 us
  local copies, waits for them, and re-layouts: 2.58 us -> 0.01 us
  starting transfers between devices: 18.9 us -> 20.5 us
  Pallas kernels: 11.3 us -> 12.8 us
    all_to_all x1, blocking collectives: 28.2 us -> 24 us  [body(): lax.all_to_all(tiles.astype(LINK), 'vox', split_axis=0, concat_axis=0, ti...]
    ppermute x6 -> x9, waiting for transfers between devices: 14.1 us -> 16.8 us  [swapped(): return lax.ppermute(x, 'subj', [(n, n ^ r) for n in range(GR)])]
    unnamed x6 -> x0, local copies, waits for them, and re-layouts: 2.58 us -> none
    ppermute x6 -> x9, starting transfers between devices: 2.36 us -> 4.22 us  [swapped(): return lax.ppermute(x, 'subj', [(n, n ^ r) for n in range(GR)])]
  transfers between devices with their start and end apart: 14 -> 17, of which waited for: 7 -> 9; matrix products, arithmetic and copies ran while one was open for 0% -> 0% of each run, Pallas kernels for 2% -> 2%
where the time goes in v3:
time: 90.9 us; the launch traced here: 89.7 us
  waiting for transfers between devices  31.9 us (35%)
  blocking collectives  24 us (26%)
  starting transfers between devices  20.5 us (23%)
  Pallas kernels  12.8 us (14%)
    all_to_all x1, blocking collectives, body(): lax.all_to_all(tiles.astype(LINK), 'vox', split_axis=0, concat_axis=0, ti...  24 us
    ppermute x9, waiting for transfers between devices, swapped(): return lax.ppermute(x, 'subj', [(n, n ^ r) for n in range(GR)])  16.8 us
    ppermute x7, starting transfers between devices, summed(): lax.ppermute(x, 'vox', ring(n, size, stride, devices))  12.3 us
    ppermute x7, waiting for transfers between devices, summed(): lax.ppermute(x, 'vox', ring(n, size, stride, devices))  10.8 us
    pallas_call x1, Pallas kernels, partial_kernels(): pl.pallas_call(kernel_kernel, out_shape=pltpu.VMEM((devices, QUARTER, 2 *...  8.26 us
    ppermute x1, waiting for transfers between devices, body(): tile = lax.ppermute(tile, ('subj', 'vox'), turn)  4.33 us
    ppermute x9, starting transfers between devices, swapped(): return lax.ppermute(x, 'subj', [(n, n ^ r) for n in range(GR)])  4.22 us
    ppermute x1, starting transfers between devices, body(): tile = lax.ppermute(tile, ('subj', 'vox'), turn)  4.04 us
  transfers between devices with their start and end apart: 17, of which 9 were waited for; matrix products, arithmetic and copies ran while one was open for 0% of the time, Pallas kernels for 2%

profile of v3, /device:TPU:8, one launch (start us, length us, event | category | flops | bytes accessed | tf_op | source)
XLA Modules:
  0.0 89.7 jit_solution(8464930782455088512)
XLA Ops:
  0.0 1.9 %windows.1 = (bf16[12,64,512]{2,1,0:T(8,128)(2,1)S(1)}, bf16[64,768]{1,0:T(8,128)(2,1)S(1)}) custom-call(s32[16,12]{1,0:T(8,128)} %off_ref.1, s32[64]{0:T(128)} %sel_ref.1, bf16[4,256,512]{2,1,0:T(8,128)(2,1)} %series_ref.1), custom_call_target="tpu_custom_call" | custom-call | tf_op jit(solution)/shard_map/windows/pallas_call | solution.py:75
  1.9 0.4 collective-permute-start.1
  2.3 4.1 %collective-permute-start.5 = (bf16[64,768]{1,0:T(8,128)(2,1)S(1)}, bf16[64,768]{1,0:T(8,128)(2,1)S(1)}, u32[]{:S(2)}, u32[]{:S(2)}) collective-permute-start(bf16[64,768]{1,0:T(8,128)(2,1)S(1)} %get-tuple-element.8), channel_id=1, source_target_pairs={{0,24},{1,25},{2,26},{3,27},{4,28},{5,29},{6,30},{7,31},{8,0},{9,1... | collective-permute-start | bytes 294920 | tf_op jit(solution)/shard_map/ppermute | solution.py:267
  6.5 0.0 collective-permute-start.4
  6.5 1.3 %collective-permute-start.3 = (bf16[64,768]{1,0:T(8,128)(2,1)S(1)}, bf16[64,768]{1,0:T(8,128)(2,1)S(1)}, u32[]{:S(2)}, u32[]{:S(2)}) collective-permute-start(bf16[64,768]{1,0:T(8,128)(2,1)S(1)} %get-tuple-element.8), channel_id=1, source_target_pairs={{0,8},{1,9},{2,10},{3,11},{4,12},{5,13},{6,14},{7,15},{8,16},{9,17... | collective-permute-start | bytes 294920 | tf_op jit(solution)/shard_map/ppermute | solution.py:267
  7.7 13.5 %collective-permute-done.1.refs_0_.e2 = bf16[12,64,512]{2,1,0:T(8,128)(2,1)S(1)} collective-permute-done((bf16[12,64,512]{2,1,0:T(8,128)(2,1)S(1)}, bf16[12,64,512]{2,1,0:T(8,128)(2,1)S(1)}, u32[]{:S(2)}, u32[]{:S(2)}) %collective-permute-start.1) | collective-permute-done | bytes 786464 | tf_op jit(solution)/shard_map/ppermute | solution.py:263
  21.3 0.0 collective-permute-done.4
  21.3 0.0 collective-permute-done.3
  21.3 2.8 %collective-permute-start.8 = (bf16[64,768]{1,0:T(8,128)(2,1)S(1)}, bf16[64,768]{1,0:T(8,128)(2,1)S(1)}, u32[]{:S(2)}, u32[]{:S(2)}) collective-permute-start(bf16[64,768]{1,0:T(8,128)(2,1)S(1)} %add_add_fusion.1), channel_id=1, source_target_pairs={{0,6},{1,7},{2,0},{3,1},{4,2},{5,3},{6,4},{7,5},{8,14},{9,15},{10,... | collective-permute-start | bytes 294920 | tf_op jit(solution)/shard_map/ppermute | solution.py:267
  24.2 0.8 collective-permute-start.7
  25.0 0.9 collective-permute-start.6
  25.8 3.2 %collective-permute-done.8 = bf16[64,768]{1,0:T(8,128)(2,1)S(1)} collective-permute-done((bf16[64,768]{1,0:T(8,128)(2,1)S(1)}, bf16[64,768]{1,0:T(8,128)(2,1)S(1)}, u32[]{:S(2)}, u32[]{:S(2)}) %collective-permute-start.8) | collective-permute-done | bytes 98336 | tf_op jit(solution)/shard_map/ppermute | solution.py:267
  29.0 2.3 %collective-permute-done.7 = bf16[64,768]{1,0:T(8,128)(2,1)S(1)} collective-permute-done((bf16[64,768]{1,0:T(8,128)(2,1)S(1)}, bf16[64,768]{1,0:T(8,128)(2,1)S(1)}, u32[]{:S(2)}, u32[]{:S(2)}) %collective-permute-start.7) | collective-permute-done | bytes 98336 | tf_op jit(solution)/shard_map/ppermute | solution.py:267
  31.3 1.4 %collective-permute-done.6 = bf16[64,768]{1,0:T(8,128)(2,1)S(1)} collective-permute-done((bf16[64,768]{1,0:T(8,128)(2,1)S(1)}, bf16[64,768]{1,0:T(8,128)(2,1)S(1)}, u32[]{:S(2)}, u32[]{:S(2)}) %collective-permute-start.6) | collective-permute-done | bytes 98336 | tf_op jit(solution)/shard_map/ppermute | solution.py:267
  32.7 2.4 %collective-permute-start.9 = (bf16[64,768]{1,0:T(8,128)(2,1)S(1)}, bf16[64,768]{1,0:T(8,128)(2,1)S(1)}, u32[]{:S(2)}, u32[]{:S(2)}) collective-permute-start(bf16[64,768]{1,0:T(8,128)(2,1)S(1)} %add_add_fusion), channel_id=1, source_target_pairs={{0,1},{1,0},{2,3},{3,2},{4,5},{5,4},{6,7},{7,6},{8,9},{9,8},{10,11... | collective-permute-start | bytes 294920 | tf_op jit(solution)/shard_map/ppermute | solution.py:267
  35.1 3.9 %collective-permute-done.9 = bf16[64,768]{1,0:T(8,128)(2,1)S(1)} collective-permute-done((bf16[64,768]{1,0:T(8,128)(2,1)S(1)}, bf16[64,768]{1,0:T(8,128)(2,1)S(1)}, u32[]{:S(2)}, u32[]{:S(2)}) %collective-permute-start.9) | collective-permute-done | bytes 98336 | tf_op jit(solution)/shard_map/ppermute | solution.py:267
  39.1 0.1 collective-permute-start.12
  39.2 0.8 collective-permute-start.11
  39.9 1.1 %collective-permute-start.10 = (bf16[16,768]{1,0:T(8,128)(2,1)S(1)}, bf16[16,768]{1,0:T(8,128)(2,1)S(1)}, u32[]{:S(2)}, u32[]{:S(2)}) collective-permute-start(bf16[16,768]{1,0:T(8,128)(2,1)S(1)} %get-tuple-element.11), channel_id=1, source_target_pairs={{0,32},{32,0},{64,96},{96,64},{1,33},{33,1},{65,97},{97,65},{2,34}... | collective-permute-start | bytes 73736 | tf_op jit(solution)/shard_map/ppermute | solution.py:263
  41.0 0.8 norms.2.na
  41.8 0.8 norms.3.nb
  42.5 0.5 collective-permute-done.11.s2
  43.1 8.3 %partial_kernels.1 = f32[32,96,128]{2,1,0:T(8,128)S(1)} custom-call(bf16[12,64,512]{2,1,0:T(8,128)(2,1)S(1)} %get-tuple-element.7.refs_0_.e0, bf16[12,64,512]{2,1,0:T(8,128)(2,1)S(1)} %collective-permute-done.refs_1_.e1, bf16[12,64,512]{2,1,0:T(8,128)(2,1)S(1)} %collective-permute-done.1.refs_0_.e2, ...), custom_call_target="tpu_custom_call" | custom-call | tf_op jit(solution)/shard_map/partial_kernels/pallas_call | solution.py:192
  51.3 0.1 convert_element_type.6
  51.5 24.0 %all_to_all.5 = f16[32,96,128]{2,1,0:T(8,128)(2,1)S(1)} all-to-all(f16[32,96,128]{2,1,0:T(8,128)(2,1)S(1)} %convert_element_type.6), channel_id=1, replica_groups=mesh['subj'=4,'vox'=32] {'vox'}, dimensions={0} | all-to-all | bytes 1572864 | tf_op jit(solution)/shard_map/all_to_all | solution.py:285
  75.5 0.1 convert_reduce_fusion
  75.6 4.0 %collective-permute-start.13 = (f32[96,128]{1,0:T(8,128)S(1)}, f32[96,128]{1,0:T(8,128)S(1)}, u32[]{:S(2)}, u32[]{:S(2)}) collective-permute-start(f32[96,128]{1,0:T(8,128)S(1)} %convert_reduce_fusion), channel_id=1, source_target_pairs={{0,0},{1,1},{2,32},{3,33},{4,64},{5,65},{6,96},{7,97},{8,8},{9,9},... | collective-permute-start | bytes 147464 | tf_op jit(solution)/shard_map/ppermute | solution.py:294
  79.6 4.3 %collective-permute-done.13.y0 = f32[96,128]{1,0:T(8,128)S(1)} collective-permute-done((f32[96,128]{1,0:T(8,128)S(1)}, f32[96,128]{1,0:T(8,128)S(1)}, u32[]{:S(2)}, u32[]{:S(2)}) %collective-permute-start.13) | collective-permute-done | bytes 49184 | tf_op jit(solution)/shard_map/ppermute | solution.py:294
  84.0 1.9 %collective-permute-start.14 = (f32[96,128]{1,0:T(8,128)S(1)}, f32[96,128]{1,0:T(8,128)S(1)}, u32[]{:S(2)}, u32[]{:S(2)}) collective-permute-start(f32[96,128]{1,0:T(8,128)S(1)} %collective-permute-done.13.y0), channel_id=1, source_target_pairs={{0,32},{32,0},{64,96},{96,64},{1,33},{33,1},{65,97},{97,65},{2,34}... | collective-permute-start | bytes 147464 | tf_op jit(solution)/shard_map/ppermute | solution.py:263
  85.8 1.7 %collective-permute-done.16.y3 = f32[96,128]{1,0:T(8,128)S(1)} collective-permute-done((f32[96,128]{1,0:T(8,128)S(1)}, f32[96,128]{1,0:T(8,128)S(1)}, u32[]{:S(2)}, u32[]{:S(2)}) %collective-permute-start.16) | collective-permute-done | bytes 49184 | tf_op jit(solution)/shard_map/ppermute | solution.py:263
  87.5 1.1 %collective-permute-done.15.y2 = f32[96,128]{1,0:T(8,128)S(1)} collective-permute-done((f32[96,128]{1,0:T(8,128)S(1)}, f32[96,128]{1,0:T(8,128)S(1)}, u32[]{:S(2)}, u32[]{:S(2)}) %collective-permute-start.15) | collective-permute-done | bytes 49184 | tf_op jit(solution)/shard_map/ppermute | solution.py:263
  88.6 1.1 %in_order.1 = f32[2,48,192]{2,1,0:T(8,128)} custom-call(f32[96,128]{1,0:T(8,128)S(1)} %collective-permute-done.13.y0, f32[96,128]{1,0:T(8,128)S(1)} %collective-permute-done.14.y1, f32[96,128]{1,0:T(8,128)S(1)} %collective-permute-done.15.y2, f32[96,128]{1,0:T(8,128)S(1)} %collective-permute-done.16.y3), custom_call_target="tpu_custom_call" | custom-call | tf_op jit(solution)/shard_map/in_order/pallas_call | solution.py:240
  (14 shorter events, 0.1 us)
Async XLA Ops:
  1.9 19.4 %collective-permute-start.1 = (bf16[12,64,512]{2,1,0:T(8,128)(2,1)S(1)}, bf16[12,64,512]{2,1,0:T(8,128)(2,1)S(1)}, u32[]{:S(2)}, u32[]{:S(2)}) collective-permute-start(bf16[12,64,512]{2,1,0:T(8,128)(2,1)S(1)} %get-tuple-element.7.refs_0_.e0), channel_id=1, source_target_pairs={{0,64},{32,96},{64,0},{96,32},{1,65},{33,97},{65,1},{97,33},{2,66}... | collective-permute-start | bytes 2359304 | tf_op jit(solution)/shard_map/ppermute | solution.py:263
  2.3 19.0 %collective-permute-start.5 = (bf16[64,768]{1,0:T(8,128)(2,1)S(1)}, bf16[64,768]{1,0:T(8,128)(2,1)S(1)}, u32[]{:S(2)}, u32[]{:S(2)}) collective-permute-start(bf16[64,768]{1,0:T(8,128)(2,1)S(1)} %get-tuple-element.8), channel_id=1, source_target_pairs={{0,24},{1,25},{2,26},{3,27},{4,28},{5,29},{6,30},{7,31},{8,0},{9,1... | collective-permute-start | bytes 294920 | tf_op jit(solution)/shard_map/ppermute | solution.py:267
  6.5 14.8 %collective-permute-start.4 = (bf16[64,768]{1,0:T(8,128)(2,1)S(1)}, bf16[64,768]{1,0:T(8,128)(2,1)S(1)}, u32[]{:S(2)}, u32[]{:S(2)}) collective-permute-start(bf16[64,768]{1,0:T(8,128)(2,1)S(1)} %get-tuple-element.8), channel_id=1, source_target_pairs={{0,16},{1,17},{2,18},{3,19},{4,20},{5,21},{6,22},{7,23},{8,24},{9,... | collective-permute-start | bytes 294920 | tf_op jit(solution)/shard_map/ppermute | solution.py:267
  6.5 14.8 %collective-permute-start.3 = (bf16[64,768]{1,0:T(8,128)(2,1)S(1)}, bf16[64,768]{1,0:T(8,128)(2,1)S(1)}, u32[]{:S(2)}, u32[]{:S(2)}) collective-permute-start(bf16[64,768]{1,0:T(8,128)(2,1)S(1)} %get-tuple-element.8), channel_id=1, source_target_pairs={{0,8},{1,9},{2,10},{3,11},{4,12},{5,13},{6,14},{7,15},{8,16},{9,17... | collective-permute-start | bytes 294920 | tf_op jit(solution)/shard_map/ppermute | solution.py:267
  7.7 33.3 %collective-permute-start = (bf16[12,64,512]{2,1,0:T(8,128)(2,1)S(1)}, bf16[12,64,512]{2,1,0:T(8,128)(2,1)S(1)}, u32[]{:S(2)}, u32[]{:S(2)}) collective-permute-start(bf16[12,64,512]{2,1,0:T(8,128)(2,1)S(1)} %get-tuple-element.7.refs_0_.e0), channel_id=1, source_target_pairs={{0,32},{32,0},{64,96},{96,64},{1,33},{33,1},{65,97},{97,65},{2,34}... | collective-permute-start | bytes 2359304 | tf_op jit(solution)/shard_map/ppermute | solution.py:263
  21.3 20.5 %collective-permute-start.2 = (bf16[12,64,512]{2,1,0:T(8,128)(2,1)S(1)}, bf16[12,64,512]{2,1,0:T(8,128)(2,1)S(1)}, u32[]{:S(2)}, u32[]{:S(2)}) collective-permute-start(bf16[12,64,512]{2,1,0:T(8,128)(2,1)S(1)} %collective-permute-done.1.refs_0_.e2), channel_id=1, source_target_pairs={{0,32},{32,0},{64,96},{96,64},{1,33},{33,1},{65,97},{97,65},{2,34}... | collective-permute-start | bytes 2359304 | tf_op jit(solution)/shard_map/ppermute | solution.py:263
  21.3 7.7 %collective-permute-start.8 = (bf16[64,768]{1,0:T(8,128)(2,1)S(1)}, bf16[64,768]{1,0:T(8,128)(2,1)S(1)}, u32[]{:S(2)}, u32[]{:S(2)}) collective-permute-start(bf16[64,768]{1,0:T(8,128)(2,1)S(1)} %add_add_fusion.1), channel_id=1, source_target_pairs={{0,6},{1,7},{2,0},{3,1},{4,2},{5,3},{6,4},{7,5},{8,14},{9,15},{10,... | collective-permute-start | bytes 294920 | tf_op jit(solution)/shard_map/ppermute | solution.py:267
  24.2 7.2 %collective-permute-start.7 = (bf16[64,768]{1,0:T(8,128)(2,1)S(1)}, bf16[64,768]{1,0:T(8,128)(2,1)S(1)}, u32[]{:S(2)}, u32[]{:S(2)}) collective-permute-start(bf16[64,768]{1,0:T(8,128)(2,1)S(1)} %add_add_fusion.1), channel_id=1, source_target_pairs={{0,4},{1,5},{2,6},{3,7},{4,0},{5,1},{6,2},{7,3},{8,12},{9,13},{10,... | collective-permute-start | bytes 294920 | tf_op jit(solution)/shard_map/ppermute | solution.py:267
  25.0 7.7 %collective-permute-start.6 = (bf16[64,768]{1,0:T(8,128)(2,1)S(1)}, bf16[64,768]{1,0:T(8,128)(2,1)S(1)}, u32[]{:S(2)}, u32[]{:S(2)}) collective-permute-start(bf16[64,768]{1,0:T(8,128)(2,1)S(1)} %add_add_fusion.1), channel_id=1, source_target_pairs={{0,2},{1,3},{2,4},{3,5},{4,6},{5,7},{6,0},{7,1},{8,10},{9,11},{10,... | collective-permute-start | bytes 294920 | tf_op jit(solution)/shard_map/ppermute | solution.py:267
  32.7 6.3 %collective-permute-start.9 = (bf16[64,768]{1,0:T(8,128)(2,1)S(1)}, bf16[64,768]{1,0:T(8,128)(2,1)S(1)}, u32[]{:S(2)}, u32[]{:S(2)}) collective-permute-start(bf16[64,768]{1,0:T(8,128)(2,1)S(1)} %add_add_fusion), channel_id=1, source_target_pairs={{0,1},{1,0},{2,3},{3,2},{4,5},{5,4},{6,7},{7,6},{8,9},{9,8},{10,11... | collective-permute-start | bytes 294920 | tf_op jit(solution)/shard_map/ppermute | solution.py:267
  39.1 3.5 %collective-permute-start.12 = (bf16[16,768]{1,0:T(8,128)(2,1)S(1)}, bf16[16,768]{1,0:T(8,128)(2,1)S(1)}, u32[]{:S(2)}, u32[]{:S(2)}) collective-permute-start(bf16[16,768]{1,0:T(8,128)(2,1)S(1)} %get-tuple-element.9), channel_id=1, source_target_pairs={{0,96},{32,64},{64,32},{96,0},{1,97},{33,65},{65,33},{97,1},{2,98}... | collective-permute-start | bytes 73736 | tf_op jit(solution)/shard_map/ppermute | solution.py:263
  39.2 3.9 %collective-permute-start.11 = (bf16[16,768]{1,0:T(8,128)(2,1)S(1)}, bf16[16,768]{1,0:T(8,128)(2,1)S(1)}, u32[]{:S(2)}, u32[]{:S(2)}) collective-permute-start(bf16[16,768]{1,0:T(8,128)(2,1)S(1)} %get-tuple-element.10), channel_id=1, source_target_pairs={{0,64},{32,96},{64,0},{96,32},{1,65},{33,97},{65,1},{97,33},{2,66}... | collective-permute-start | bytes 73736 | tf_op jit(solution)/shard_map/ppermute | solution.py:263
  39.9 3.1 %collective-permute-start.10 = (bf16[16,768]{1,0:T(8,128)(2,1)S(1)}, bf16[16,768]{1,0:T(8,128)(2,1)S(1)}, u32[]{:S(2)}, u32[]{:S(2)}) collective-permute-start(bf16[16,768]{1,0:T(8,128)(2,1)S(1)} %get-tuple-element.11), channel_id=1, source_target_pairs={{0,32},{32,0},{64,96},{96,64},{1,33},{33,1},{65,97},{97,65},{2,34}... | collective-permute-start | bytes 73736 | tf_op jit(solution)/shard_map/ppermute | solution.py:263
  75.6 8.4 %collective-permute-start.13 = (f32[96,128]{1,0:T(8,128)S(1)}, f32[96,128]{1,0:T(8,128)S(1)}, u32[]{:S(2)}, u32[]{:S(2)}) collective-permute-start(f32[96,128]{1,0:T(8,128)S(1)} %convert_reduce_fusion), channel_id=1, source_target_pairs={{0,0},{1,1},{2,32},{3,33},{4,64},{5,65},{6,96},{7,97},{8,8},{9,9},... | collective-permute-start | bytes 147464 | tf_op jit(solution)/shard_map/ppermute | solution.py:294
  84.0 3.5 %collective-permute-start.16 = (f32[96,128]{1,0:T(8,128)S(1)}, f32[96,128]{1,0:T(8,128)S(1)}, u32[]{:S(2)}, u32[]{:S(2)}) collective-permute-start(f32[96,128]{1,0:T(8,128)S(1)} %collective-permute-done.13.y0), channel_id=1, source_target_pairs={{0,96},{32,64},{64,32},{96,0},{1,97},{33,65},{65,33},{97,1},{2,98}... | collective-permute-start | bytes 147464 | tf_op jit(solution)/shard_map/ppermute | solution.py:263
  84.0 4.6 %collective-permute-start.15 = (f32[96,128]{1,0:T(8,128)S(1)}, f32[96,128]{1,0:T(8,128)S(1)}, u32[]{:S(2)}, u32[]{:S(2)}) collective-permute-start(f32[96,128]{1,0:T(8,128)S(1)} %collective-permute-done.13.y0), channel_id=1, source_target_pairs={{0,64},{32,96},{64,0},{96,32},{1,65},{33,97},{65,1},{97,33},{2,66}... | collective-permute-start | bytes 147464 | tf_op jit(solution)/shard_map/ppermute | solution.py:263
  84.0 4.6 %collective-permute-start.14 = (f32[96,128]{1,0:T(8,128)S(1)}, f32[96,128]{1,0:T(8,128)S(1)}, u32[]{:S(2)}, u32[]{:S(2)}) collective-permute-start(f32[96,128]{1,0:T(8,128)S(1)} %collective-permute-done.13.y0), channel_id=1, source_target_pairs={{0,32},{32,0},{64,96},{96,64},{1,33},{33,1},{65,97},{97,65},{2,34}... | collective-permute-start | bytes 147464 | tf_op jit(solution)/shard_map/ppermute | solution.py:263

commit v4 on v2

--- a/solution.py
+++ b/solution.py
@@ -84,7 +84,11 @@
         scratch_shapes=[pltpu.VMEM((EP * TR, series.shape[1]), BF16)],
         compiler_params=pltpu.CompilerParams(vmem_limit_bytes=8 << 20),
         name="windows",
-    )(offsets, selected, series)
+    )(
+        pltpu.with_memory_space_constraint(offsets, pltpu.HBM),
+        pltpu.with_memory_space_constraint(selected, pltpu.HBM),
+        pltpu.with_memory_space_constraint(series, pltpu.HBM),
+    )
 
 
 def meeting(j, first, count):
@@ -118,7 +122,7 @@
 
 
 def kernel_kernel(
-    e0, e1, e2, e3, s0, s1, s2, s3, na, nb, o_ref, lh_ref, ll_ref, c_ref, n_ref, z_ref, g_ref
+    e0, e1, e2, e3, s0, s1, s2, s3, na, nb, o_ref, lh_ref, ll_ref, c_ref, z_ref, g_ref
 ):
     j = lax.axis_index("subj")
     epochs = (e0, e1, e2, e3)
@@ -141,24 +145,25 @@
     power = dot(high, same) + dot(low, same)
     slab_std = centred * (lax.rsqrt(power + series_floor) * shrink_factor)
 
+    high, low = (half.astype(F32) for half in split(slab_std))
+    mine = jnp.where(mine, 1.0, 0.0).astype(BF16)
     for e in range(EP):
         x = jnp.concatenate([p[e] for p in epochs], axis=0)
-        n_ref[e] = lax.rsqrt(na[e] + nb[e] + series_floor)
+        norm = jnp.sqrt(na[e] + nb[e] + series_floor)[None]
         for k in range(KL):
-            line = jnp.where(mine, slab_std[e * KL + k : e * KL + k + 1, :], 0.0)
-            lh, ll = split(line)
-            lh_ref[k * SB : (k + 1) * SB, :] = lh
-            ll_ref[k * SB : (k + 1) * SB, :] = ll
-        c_ref[e] = dot(lh_ref[...], x) + dot(ll_ref[...], x)
-
-    def pair(q, carry):
+            row = slice(e * KL + k, e * KL + k + 1)
+            for half, to in ((high, lh_ref), (low, ll_ref)):
+                line = jnp.broadcast_to(half[row], mine.shape).astype(BF16) * mine
+                to[e % 2, k * SB : (k + 1) * SB, :] = line
+        shrunk = dot(lh_ref[e % 2], x) + dot(ll_ref[e % 2], x)
+        shrunk = shrunk.reshape(KL, SB, width)
+        c_ref[e] = jnp.log((norm + shrunk) / (norm - shrunk)).reshape(KL * SB, width)
+
+    def scores(q, slot):
         for h in range(2):
-            start = pl.multiple_of((q * 2 + h) * SB, SB)
+            rows = pl.ds(pl.multiple_of((q * 2 + h) * SB, SB), SB)
             for c in range(0, width, 128):
-                fisher = []
-                for e in range(EP):
-                    shrunk = c_ref[e, pl.ds(start, SB), c : c + 128] * n_ref[e, :, c : c + 128]
-                    fisher.append(jnp.log((1.0 + shrunk) / (1.0 - shrunk)))
+                fisher = [c_ref[e, rows, c : c + 128] for e in range(EP)]
                 mean = sum(fisher[1:], fisher[0]) * (1.0 / EP)
                 fisher = [f - mean for f in fisher]
                 spread = fisher[0] * fisher[0]
@@ -166,18 +171,32 @@
                     spread = spread + f * f
                 scale = lax.rsqrt(spread * (1.0 / EP) + 4.0 * spread_floor)
                 for e in range(EP):
-                    z_ref[h, e * SB : (e + 1) * SB, c : c + 128] = (fisher[e] * scale).astype(BF16)
-            product = dot_nt(z_ref[h], z_ref[h])
-            g_ref[h] = product[:, 0:128]
-            g_ref[2, :, h * 64 : (h + 1) * 64] = product[:, 128 : EP * SB]
-        base = (q // 2) * 8 + q % 2
+                    at = slice(e * SB, (e + 1) * SB)
+                    z_ref[slot, h, at, c : c + 128] = (fisher[e] * scale).astype(BF16)
+
+    def products(q, slot):
+        for h in range(2):
+            product = dot_nt(z_ref[slot, h], z_ref[slot, h])
+            g_ref[slot, h] = product[:, 0:128]
+            g_ref[slot, 2, :, h * 64 : (h + 1) * 64] = product[:, 128 : EP * SB]
         for r in range(GR):
             lines = pl.ds(r, EP * SL, stride=GR)
-            both = jnp.concatenate([g_ref[n, lines, :] for n in range(3)], axis=0)
-            o_ref[base + 2 * r] = both.astype(o_ref.dtype)
+            both = jnp.concatenate([g_ref[slot, n, lines, :] for n in range(3)], axis=0)
+            o_ref[(q // 2) * 8 + 2 * r + slot] = both.astype(o_ref.dtype)
+
+    def step(t, carry):
+        scores(2 * t + 1, 1)
+        products(2 * t, 0)
+        scores(2 * t + 2, 0)
+        products(2 * t + 1, 1)
         return carry
 
-    lax.fori_loop(0, KL // 2, pair, 0)
+    last = KL // 2 - 1
+    scores(0, 0)
+    lax.fori_loop(0, last // 2, step, 0)
+    scores(last, 1)
+    products(last - 1, 0)
+    products(last, 1)
 
 
 def partial_kernels(epochs, slabs, powers, devices, dtype):
@@ -188,12 +207,11 @@
         in_specs=[pl.BlockSpec(memory_space=pltpu.VMEM)] * (2 * GR + 2),
         out_specs=pl.BlockSpec(memory_space=pltpu.VMEM),
         scratch_shapes=[
-            pltpu.VMEM((KL * SB, SB * TR), BF16),
-            pltpu.VMEM((KL * SB, SB * TR), BF16),
+            pltpu.VMEM((2, KL * SB, SB * TR), BF16),
+            pltpu.VMEM((2, KL * SB, SB * TR), BF16),
             pltpu.VMEM((EP, KL * SB, width), F32),
-            pltpu.VMEM((EP, SB, width), F32),
-            pltpu.VMEM((2, EP * SB, width), BF16),
-            pltpu.VMEM((3, EP * SB, 128), F32),
+            pltpu.VMEM((2, 2, EP * SB, width), BF16),
+            pltpu.VMEM((2, 3, EP * SB, 128), F32),
         ],
         compiler_params=pltpu.CompilerParams(vmem_limit_bytes=20 << 20),
         name="partial_kernels",

time: 91 us -> 86.6 us (0.952)
  local copies, waits for them, and re-layouts: 2.58 us -> 0.01 us
  Pallas kernels: 11.3 us -> 9.59 us
    unnamed x6 -> x0, local copies, waits for them, and re-layouts: 2.58 us -> none
    pallas_call x1, Pallas kernels: 7.58 us -> 5.26 us  [partial_kernels(): pl.pallas_call(kernel_kernel, out_shape=pltpu.VMEM((devices, 3 * EP * SL,...]
where the time goes in v4:
time: 86.6 us; the launch traced here: 86.5 us
  waiting for transfers between devices  29.3 us (34%)
  blocking collectives  28.2 us (33%)
  starting transfers between devices  18.9 us (22%)
  Pallas kernels  9.59 us (11%)
    all_to_all x1, blocking collectives, body(): lax.all_to_all(tiles.astype(LINK), 'vox', split_axis=0, concat_axis=0, ti...  28.2 us
    ppermute x6, waiting for transfers between devices, swapped(): return lax.ppermute(x, 'subj', [(n, n ^ r) for n in range(GR)])  14.1 us
    ppermute x7, starting transfers between devices, summed(): lax.ppermute(x, 'vox', ring(n, size, stride, devices))  12.3 us
    ppermute x7, waiting for transfers between devices, summed(): lax.ppermute(x, 'vox', ring(n, size, stride, devices))  10.8 us
    pallas_call x1, Pallas kernels, partial_kernels(): pl.pallas_call(kernel_kernel, out_shape=pltpu.VMEM((devices, 3 * EP * SL,...  5.26 us
    ppermute x1, waiting for transfers between devices, body(): return in_order(lax.ppermute(tile, ('subj', 'vox'), turn))  4.42 us
    ppermute x1, starting transfers between devices, body(): return in_order(lax.ppermute(tile, ('subj', 'vox'), turn))  4.23 us
    ppermute x6, starting transfers between devices, swapped(): return lax.ppermute(x, 'subj', [(n, n ^ r) for n in range(GR)])  2.35 us
  transfers between devices with their start and end apart: 14, of which 7 were waited for; matrix products, arithmetic and copies ran while one was open for 0% of the time, Pallas kernels for 2%

profile of v4, /device:TPU:8, one launch (start us, length us, event | category | flops | bytes accessed | tf_op | source)
XLA Modules:
  0.0 86.5 jit_solution(12520593947547827045)
XLA Ops:
  0.0 1.9 %windows.1 = (bf16[12,64,512]{2,1,0:T(8,128)(2,1)S(1)}, bf16[64,768]{1,0:T(8,128)(2,1)S(1)}) custom-call(s32[16,12]{1,0:T(8,128)} %off_ref.1, s32[64]{0:T(128)} %sel_ref.1, bf16[4,256,512]{2,1,0:T(8,128)(2,1)} %series_ref.1), custom_call_target="tpu_custom_call" | custom-call | tf_op jit(solution)/shard_map/windows/pallas_call | solution.py:72
  1.9 0.4 collective-permute-start.1
  2.3 4.1 %collective-permute-start.5 = (bf16[64,768]{1,0:T(8,128)(2,1)S(1)}, bf16[64,768]{1,0:T(8,128)(2,1)S(1)}, u32[]{:S(2)}, u32[]{:S(2)}) collective-permute-start(bf16[64,768]{1,0:T(8,128)(2,1)S(1)} %get-tuple-element.8), channel_id=1, source_target_pairs={{0,24},{1,25},{2,26},{3,27},{4,28},{5,29},{6,30},{7,31},{8,0},{9,1... | collective-permute-start | bytes 294920 | tf_op jit(solution)/shard_map/ppermute | solution.py:263
  6.5 0.0 collective-permute-start.4
  6.5 1.3 %collective-permute-start.3 = (bf16[64,768]{1,0:T(8,128)(2,1)S(1)}, bf16[64,768]{1,0:T(8,128)(2,1)S(1)}, u32[]{:S(2)}, u32[]{:S(2)}) collective-permute-start(bf16[64,768]{1,0:T(8,128)(2,1)S(1)} %get-tuple-element.8), channel_id=1, source_target_pairs={{0,8},{1,9},{2,10},{3,11},{4,12},{5,13},{6,14},{7,15},{8,16},{9,17... | collective-permute-start | bytes 294920 | tf_op jit(solution)/shard_map/ppermute | solution.py:263
  7.7 0.0 collective-permute-start
  7.7 13.5 %collective-permute-done.1.refs_0_.e2 = bf16[12,64,512]{2,1,0:T(8,128)(2,1)S(1)} collective-permute-done((bf16[12,64,512]{2,1,0:T(8,128)(2,1)S(1)}, bf16[12,64,512]{2,1,0:T(8,128)(2,1)S(1)}, u32[]{:S(2)}, u32[]{:S(2)}) %collective-permute-start.1) | collective-permute-done | bytes 786464 | tf_op jit(solution)/shard_map/ppermute | solution.py:259
  21.3 0.0 collective-permute-done.4
  21.3 0.0 collective-permute-done.3
  21.3 2.8 %collective-permute-start.8 = (bf16[64,768]{1,0:T(8,128)(2,1)S(1)}, bf16[64,768]{1,0:T(8,128)(2,1)S(1)}, u32[]{:S(2)}, u32[]{:S(2)}) collective-permute-start(bf16[64,768]{1,0:T(8,128)(2,1)S(1)} %add_add_fusion.1), channel_id=1, source_target_pairs={{0,6},{1,7},{2,0},{3,1},{4,2},{5,3},{6,4},{7,5},{8,14},{9,15},{10,... | collective-permute-start | bytes 294920 | tf_op jit(solution)/shard_map/ppermute | solution.py:263
  24.2 0.8 collective-permute-start.7
  25.0 0.9 %collective-permute-start.6 = (bf16[64,768]{1,0:T(8,128)(2,1)S(1)}, bf16[64,768]{1,0:T(8,128)(2,1)S(1)}, u32[]{:S(2)}, u32[]{:S(2)}) collective-permute-start(bf16[64,768]{1,0:T(8,128)(2,1)S(1)} %add_add_fusion.1), channel_id=1, source_target_pairs={{0,2},{1,3},{2,4},{3,5},{4,6},{5,7},{6,0},{7,1},{8,10},{9,11},{10,... | collective-permute-start | bytes 294920 | tf_op jit(solution)/shard_map/ppermute | solution.py:263
  25.8 3.2 %collective-permute-done.8 = bf16[64,768]{1,0:T(8,128)(2,1)S(1)} collective-permute-done((bf16[64,768]{1,0:T(8,128)(2,1)S(1)}, bf16[64,768]{1,0:T(8,128)(2,1)S(1)}, u32[]{:S(2)}, u32[]{:S(2)}) %collective-permute-start.8) | collective-permute-done | bytes 98336 | tf_op jit(solution)/shard_map/ppermute | solution.py:263
  29.0 2.3 %collective-permute-done.7 = bf16[64,768]{1,0:T(8,128)(2,1)S(1)} collective-permute-done((bf16[64,768]{1,0:T(8,128)(2,1)S(1)}, bf16[64,768]{1,0:T(8,128)(2,1)S(1)}, u32[]{:S(2)}, u32[]{:S(2)}) %collective-permute-start.7) | collective-permute-done | bytes 98336 | tf_op jit(solution)/shard_map/ppermute | solution.py:263
  31.3 1.4 %collective-permute-done.6 = bf16[64,768]{1,0:T(8,128)(2,1)S(1)} collective-permute-done((bf16[64,768]{1,0:T(8,128)(2,1)S(1)}, bf16[64,768]{1,0:T(8,128)(2,1)S(1)}, u32[]{:S(2)}, u32[]{:S(2)}) %collective-permute-start.6) | collective-permute-done | bytes 98336 | tf_op jit(solution)/shard_map/ppermute | solution.py:263
  32.7 2.4 %collective-permute-start.9 = (bf16[64,768]{1,0:T(8,128)(2,1)S(1)}, bf16[64,768]{1,0:T(8,128)(2,1)S(1)}, u32[]{:S(2)}, u32[]{:S(2)}) collective-permute-start(bf16[64,768]{1,0:T(8,128)(2,1)S(1)} %add_add_fusion), channel_id=1, source_target_pairs={{0,1},{1,0},{2,3},{3,2},{4,5},{5,4},{6,7},{7,6},{8,9},{9,8},{10,11... | collective-permute-start | bytes 294920 | tf_op jit(solution)/shard_map/ppermute | solution.py:263
  35.1 3.9 %collective-permute-done.9 = bf16[64,768]{1,0:T(8,128)(2,1)S(1)} collective-permute-done((bf16[64,768]{1,0:T(8,128)(2,1)S(1)}, bf16[64,768]{1,0:T(8,128)(2,1)S(1)}, u32[]{:S(2)}, u32[]{:S(2)}) %collective-permute-start.9) | collective-permute-done | bytes 98336 | tf_op jit(solution)/shard_map/ppermute | solution.py:263
  39.1 0.1 collective-permute-start.12
  39.2 0.8 collective-permute-start.11
  39.9 1.1 %collective-permute-start.10 = (bf16[16,768]{1,0:T(8,128)(2,1)S(1)}, bf16[16,768]{1,0:T(8,128)(2,1)S(1)}, u32[]{:S(2)}, u32[]{:S(2)}) collective-permute-start(bf16[16,768]{1,0:T(8,128)(2,1)S(1)} %get-tuple-element.11), channel_id=1, source_target_pairs={{0,32},{32,0},{64,96},{96,64},{1,33},{33,1},{65,97},{97,65},{2,34}... | collective-permute-start | bytes 73736 | tf_op jit(solution)/shard_map/ppermute | solution.py:259
  41.0 0.8 norms.2.na
  41.8 0.8 norms.3.nb
  42.5 0.0 collective-permute-done.12.s3
  42.5 0.5 collective-permute-done.11.s2
  43.1 0.0 collective-permute-done.10.s1
  43.1 5.3 %partial_kernels.1 = f32[32,144,128]{2,1,0:T(8,128)S(1)} custom-call(bf16[12,64,512]{2,1,0:T(8,128)(2,1)S(1)} %get-tuple-element.7.refs_0_.e0, bf16[12,64,512]{2,1,0:T(8,128)(2,1)S(1)} %collective-permute-done.refs_1_.e1, bf16[12,64,512]{2,1,0:T(8,128)(2,1)S(1)} %collective-permute-done.1.refs_0_.e2, ...), custom_call_target="tpu_custom_call" | custom-call | tf_op jit(solution)/shard_map/partial_kernels/pallas_call | solution.py:204
  48.3 0.2 convert_element_type.6
  48.5 28.2 %all_to_all.5 = f16[32,144,128]{2,1,0:T(8,128)(2,1)S(1)} all-to-all(f16[32,144,128]{2,1,0:T(8,128)(2,1)S(1)} %convert_element_type.6), channel_id=1, replica_groups=mesh['subj'=4,'vox'=32] {'vox'}, dimensions={0} | all-to-all | bytes 2359296 | tf_op jit(solution)/shard_map/all_to_all | solution.py:281
  76.7 0.2 convert_reduce_fusion
  76.9 4.2 %collective-permute-start.13 = (f32[144,128]{1,0:T(8,128)S(1)}, f32[144,128]{1,0:T(8,128)S(1)}, u32[]{:S(2)}, u32[]{:S(2)}) collective-permute-start(f32[144,128]{1,0:T(8,128)S(1)} %convert_reduce_fusion), channel_id=1, source_target_pairs={{0,0},{1,1},{2,32},{3,33},{4,64},{5,65},{6,96},{7,97},{8,8},{9,9},... | collective-permute-start | bytes 221192 | tf_op jit(solution)/shard_map/ppermute | solution.py:290
  81.1 4.4 %collective-permute-done.13.y_ref = f32[144,128]{1,0:T(8,128)S(1)} collective-permute-done((f32[144,128]{1,0:T(8,128)S(1)}, f32[144,128]{1,0:T(8,128)S(1)}, u32[]{:S(2)}, u32[]{:S(2)}) %collective-permute-start.13) | collective-permute-done | bytes 73760 | tf_op jit(solution)/shard_map/ppermute | solution.py:290
  85.5 0.9 %in_order.1 = f32[2,48,192]{2,1,0:T(8,128)} custom-call(f32[144,128]{1,0:T(8,128)S(1)} %collective-permute-done.13.y_ref), custom_call_target="tpu_custom_call" | custom-call | tf_op jit(solution)/shard_map/in_order/pallas_call | solution.py:240
  (8 shorter events, 0.1 us)
Async XLA Ops:
  1.9 19.4 %collective-permute-start.1 = (bf16[12,64,512]{2,1,0:T(8,128)(2,1)S(1)}, bf16[12,64,512]{2,1,0:T(8,128)(2,1)S(1)}, u32[]{:S(2)}, u32[]{:S(2)}) collective-permute-start(bf16[12,64,512]{2,1,0:T(8,128)(2,1)S(1)} %get-tuple-element.7.refs_0_.e0), channel_id=1, source_target_pairs={{0,64},{32,96},{64,0},{96,32},{1,65},{33,97},{65,1},{97,33},{2,66}... | collective-permute-start | bytes 2359304 | tf_op jit(solution)/shard_map/ppermute | solution.py:259
  2.3 19.0 %collective-permute-start.5 = (bf16[64,768]{1,0:T(8,128)(2,1)S(1)}, bf16[64,768]{1,0:T(8,128)(2,1)S(1)}, u32[]{:S(2)}, u32[]{:S(2)}) collective-permute-start(bf16[64,768]{1,0:T(8,128)(2,1)S(1)} %get-tuple-element.8), channel_id=1, source_target_pairs={{0,24},{1,25},{2,26},{3,27},{4,28},{5,29},{6,30},{7,31},{8,0},{9,1... | collective-permute-start | bytes 294920 | tf_op jit(solution)/shard_map/ppermute | solution.py:263
  6.5 14.8 %collective-permute-start.4 = (bf16[64,768]{1,0:T(8,128)(2,1)S(1)}, bf16[64,768]{1,0:T(8,128)(2,1)S(1)}, u32[]{:S(2)}, u32[]{:S(2)}) collective-permute-start(bf16[64,768]{1,0:T(8,128)(2,1)S(1)} %get-tuple-element.8), channel_id=1, source_target_pairs={{0,16},{1,17},{2,18},{3,19},{4,20},{5,21},{6,22},{7,23},{8,24},{9,... | collective-permute-start | bytes 294920 | tf_op jit(solution)/shard_map/ppermute | solution.py:263
  6.5 14.8 %collective-permute-start.3 = (bf16[64,768]{1,0:T(8,128)(2,1)S(1)}, bf16[64,768]{1,0:T(8,128)(2,1)S(1)}, u32[]{:S(2)}, u32[]{:S(2)}) collective-permute-start(bf16[64,768]{1,0:T(8,128)(2,1)S(1)} %get-tuple-element.8), channel_id=1, source_target_pairs={{0,8},{1,9},{2,10},{3,11},{4,12},{5,13},{6,14},{7,15},{8,16},{9,17... | collective-permute-start | bytes 294920 | tf_op jit(solution)/shard_map/ppermute | solution.py:263
  7.7 33.3 %collective-permute-start = (bf16[12,64,512]{2,1,0:T(8,128)(2,1)S(1)}, bf16[12,64,512]{2,1,0:T(8,128)(2,1)S(1)}, u32[]{:S(2)}, u32[]{:S(2)}) collective-permute-start(bf16[12,64,512]{2,1,0:T(8,128)(2,1)S(1)} %get-tuple-element.7.refs_0_.e0), channel_id=1, source_target_pairs={{0,32},{32,0},{64,96},{96,64},{1,33},{33,1},{65,97},{97,65},{2,34}... | collective-permute-start | bytes 2359304 | tf_op jit(solution)/shard_map/ppermute | solution.py:259
  21.3 20.5 %collective-permute-start.2 = (bf16[12,64,512]{2,1,0:T(8,128)(2,1)S(1)}, bf16[12,64,512]{2,1,0:T(8,128)(2,1)S(1)}, u32[]{:S(2)}, u32[]{:S(2)}) collective-permute-start(bf16[12,64,512]{2,1,0:T(8,128)(2,1)S(1)} %collective-permute-done.1.refs_0_.e2), channel_id=1, source_target_pairs={{0,32},{32,0},{64,96},{96,64},{1,33},{33,1},{65,97},{97,65},{2,34}... | collective-permute-start | bytes 2359304 | tf_op jit(solution)/shard_map/ppermute | solution.py:259
  21.3 7.7 %collective-permute-start.8 = (bf16[64,768]{1,0:T(8,128)(2,1)S(1)}, bf16[64,768]{1,0:T(8,128)(2,1)S(1)}, u32[]{:S(2)}, u32[]{:S(2)}) collective-permute-start(bf16[64,768]{1,0:T(8,128)(2,1)S(1)} %add_add_fusion.1), channel_id=1, source_target_pairs={{0,6},{1,7},{2,0},{3,1},{4,2},{5,3},{6,4},{7,5},{8,14},{9,15},{10,... | collective-permute-start | bytes 294920 | tf_op jit(solution)/shard_map/ppermute | solution.py:263
  24.2 7.2 %collective-permute-start.7 = (bf16[64,768]{1,0:T(8,128)(2,1)S(1)}, bf16[64,768]{1,0:T(8,128)(2,1)S(1)}, u32[]{:S(2)}, u32[]{:S(2)}) collective-permute-start(bf16[64,768]{1,0:T(8,128)(2,1)S(1)} %add_add_fusion.1), channel_id=1, source_target_pairs={{0,4},{1,5},{2,6},{3,7},{4,0},{5,1},{6,2},{7,3},{8,12},{9,13},{10,... | collective-permute-start | bytes 294920 | tf_op jit(solution)/shard_map/ppermute | solution.py:263
  25.0 7.7 %collective-permute-start.6 = (bf16[64,768]{1,0:T(8,128)(2,1)S(1)}, bf16[64,768]{1,0:T(8,128)(2,1)S(1)}, u32[]{:S(2)}, u32[]{:S(2)}) collective-permute-start(bf16[64,768]{1,0:T(8,128)(2,1)S(1)} %add_add_fusion.1), channel_id=1, source_target_pairs={{0,2},{1,3},{2,4},{3,5},{4,6},{5,7},{6,0},{7,1},{8,10},{9,11},{10,... | collective-permute-start | bytes 294920 | tf_op jit(solution)/shard_map/ppermute | solution.py:263
  32.7 6.3 %collective-permute-start.9 = (bf16[64,768]{1,0:T(8,128)(2,1)S(1)}, bf16[64,768]{1,0:T(8,128)(2,1)S(1)}, u32[]{:S(2)}, u32[]{:S(2)}) collective-permute-start(bf16[64,768]{1,0:T(8,128)(2,1)S(1)} %add_add_fusion), channel_id=1, source_target_pairs={{0,1},{1,0},{2,3},{3,2},{4,5},{5,4},{6,7},{7,6},{8,9},{9,8},{10,11... | collective-permute-start | bytes 294920 | tf_op jit(solution)/shard_map/ppermute | solution.py:263
  39.1 3.5 %collective-permute-start.12 = (bf16[16,768]{1,0:T(8,128)(2,1)S(1)}, bf16[16,768]{1,0:T(8,128)(2,1)S(1)}, u32[]{:S(2)}, u32[]{:S(2)}) collective-permute-start(bf16[16,768]{1,0:T(8,128)(2,1)S(1)} %get-tuple-element.9), channel_id=1, source_target_pairs={{0,96},{32,64},{64,32},{96,0},{1,97},{33,65},{65,33},{97,1},{2,98}... | collective-permute-start | bytes 73736 | tf_op jit(solution)/shard_map/ppermute | solution.py:259
  39.2 3.9 %collective-permute-start.11 = (bf16[16,768]{1,0:T(8,128)(2,1)S(1)}, bf16[16,768]{1,0:T(8,128)(2,1)S(1)}, u32[]{:S(2)}, u32[]{:S(2)}) collective-permute-start(bf16[16,768]{1,0:T(8,128)(2,1)S(1)} %get-tuple-element.10), channel_id=1, source_target_pairs={{0,64},{32,96},{64,0},{96,32},{1,65},{33,97},{65,1},{97,33},{2,66}... | collective-permute-start | bytes 73736 | tf_op jit(solution)/shard_map/ppermute | solution.py:259
  39.9 3.1 %collective-permute-start.10 = (bf16[16,768]{1,0:T(8,128)(2,1)S(1)}, bf16[16,768]{1,0:T(8,128)(2,1)S(1)}, u32[]{:S(2)}, u32[]{:S(2)}) collective-permute-start(bf16[16,768]{1,0:T(8,128)(2,1)S(1)} %get-tuple-element.11), channel_id=1, source_target_pairs={{0,32},{32,0},{64,96},{96,64},{1,33},{33,1},{65,97},{97,65},{2,34}... | collective-permute-start | bytes 73736 | tf_op jit(solution)/shard_map/ppermute | solution.py:259
  76.9 8.6 %collective-permute-start.13 = (f32[144,128]{1,0:T(8,128)S(1)}, f32[144,128]{1,0:T(8,128)S(1)}, u32[]{:S(2)}, u32[]{:S(2)}) collective-permute-start(f32[144,128]{1,0:T(8,128)S(1)} %convert_reduce_fusion), channel_id=1, source_target_pairs={{0,0},{1,1},{2,32},{3,33},{4,64},{5,65},{6,96},{7,97},{8,8},{9,9},... | collective-permute-start | bytes 221192 | tf_op jit(solution)/shard_map/ppermute | solution.py:290

commit v5 on v4

--- a/solution.py
+++ b/solution.py
@@ -12,6 +12,8 @@
 SL = 4
 SB = GR * SL
 KL = 16
+ROWS = GR * KL
+SLOTS = 8
 VOX = 16384
 F32 = jnp.float32
 BF16 = jnp.bfloat16
@@ -25,6 +27,10 @@
     return pltpu.with_memory_space_constraint(x, pltpu.VMEM)
 
 
+def far(x):
+    return pltpu.with_memory_space_constraint(x, pltpu.HBM)
+
+
 def iota(shape, dim):
     return lax.broadcasted_iota(jnp.int32, shape, dim)
 
@@ -42,7 +48,42 @@
     return hi, (x - hi.astype(F32)).astype(BF16)
 
 
-def window_kernel(off_ref, sel_ref, series_ref, e_ref, t_ref, w_ref):
+def selected_ids(sel_ref, j):
+    row = iota((ROWS, 128), 0)
+    lane = iota((8, 128), 1)
+    down = jnp.zeros((ROWS, 128), jnp.int32)
+    along = jnp.full((8, 128), -VOX, jnp.int32)
+    for r in range(GR):
+        for k in range(KL):
+            voxel = sel_ref[2 * ((k // 4) * 8 + (j ^ r) * 2 + (k // 2) % 2) + k % 2]
+            down = jnp.where(row == r * KL + k, voxel, down)
+            along = jnp.where(lane == r * KL + k, voxel, along)
+    return down, along
+
+
+def places(down, along, width):
+    shift = width.bit_length() - 1
+    shard_down = down >> shift
+    shard_along = along >> shift
+    same = shard_down == jnp.broadcast_to(shard_along[0:1], (ROWS, 128))
+    row = iota((ROWS, 128), 0)
+    lane = iota((ROWS, 128), 1)
+    rank_down = jnp.sum(jnp.where(same & (lane < row), 1.0, 0.0), axis=1, keepdims=True)
+    rank_along = jnp.sum(jnp.where(same & (row < lane), 1.0, 0.0), axis=0, keepdims=True)
+    return shard_down, rank_down.astype(jnp.int32), shard_along, rank_along.astype(jnp.int32)
+
+
+def pack_slots(send_ref, picked, shard_along, rank_along, i, turn):
+    slot = iota((SLOTS, 128), 0) + turn * SLOTS
+    rank = jnp.broadcast_to(rank_along, (SLOTS, 128))
+    chosen = (rank == slot) & (shard_along[0:SLOTS] == i)
+    chosen = jnp.where(chosen, 1.0, 0.0).astype(BF16)
+    slots = dot(chosen[:, 0:ROWS], picked).astype(BF16)
+    for n in range(send_ref.shape[0]):
+        send_ref[n] = slots
+
+
+def window_kernel(off_ref, sel_ref, series_ref, e_ref, t_ref, send_ref, turns_ref, w_ref):
     j = lax.axis_index("subj")
     i = lax.axis_index("vox")
     width = series_ref.shape[2]
@@ -54,41 +95,91 @@
         rows = dot(w_ref[...], series_ref[s]).astype(BF16)
         for e in range(EP):
             e_ref[e, s * TR : (s + 1) * TR, :] = rows[e * TR : (e + 1) * TR]
-    row = iota((GR * KL, 128), 0)
-    column = jnp.zeros((GR * KL, 128), jnp.int32)
-    for r in range(GR):
-        for k in range(KL):
-            owner = (k // 4) * 8 + (j ^ r) * 2 + (k // 2) % 2
-            column = jnp.where(row == r * KL + k, sel_ref[2 * owner + k % 2] - i * width, column)
-    lane = iota((GR * KL, 128), 1)
+    down, along = selected_ids(sel_ref, j)
+    lane = iota((ROWS, 128), 1)
     picker = jnp.concatenate(
-        [jnp.where(column == lane + c, 1.0, 0.0).astype(BF16) for c in range(0, width, 128)], axis=1
-    )
-    t_ref[...] = dot_nt(picker, e_ref[...].reshape(EP * SL * TR, width)).astype(BF16)
-
-
-def take_windows(series, offsets, selected):
+        [
+            jnp.where(down - i * width == lane + c, 1.0, 0.0).astype(BF16)
+            for c in range(0, width, 128)
+        ],
+        axis=1,
+    )
+    picked = dot_nt(picker, e_ref[...].reshape(EP * SL * TR, width)).astype(BF16)
+    t_ref[...] = picked
+    _, rank_down, shard_along, rank_along = places(down, along, width)
+    pack_slots(send_ref, picked, shard_along, rank_along, i, 0)
+    turns_ref[0] = jnp.max(rank_down) // SLOTS + 1
+
+
+SMEM = pl.BlockSpec(memory_space=pltpu.SMEM)
+VMEM = pl.BlockSpec(memory_space=pltpu.VMEM)
+
+
+def small(mib):
+    return pltpu.CompilerParams(vmem_limit_bytes=mib << 20)
+
+
+def take_windows(series, offsets, selected, devices):
     width = series.shape[2]
     return pl.pallas_call(
         window_kernel,
         out_shape=(
             pltpu.VMEM((EP, SL * TR, width), BF16),
-            pltpu.VMEM((GR * KL, EP * SL * TR), BF16),
+            pltpu.VMEM((ROWS, EP * SL * TR), BF16),
+            pltpu.VMEM((devices, SLOTS, EP * SL * TR), BF16),
+            jax.ShapeDtypeStruct((1,), jnp.int32),
         ),
-        in_specs=[
-            pl.BlockSpec(memory_space=pltpu.SMEM),
-            pl.BlockSpec(memory_space=pltpu.SMEM),
-            pl.BlockSpec(memory_space=pltpu.VMEM),
+        in_specs=[SMEM, SMEM, VMEM],
+        out_specs=(VMEM, VMEM, VMEM, SMEM),
+        scratch_shapes=[pltpu.VMEM((EP * TR, series.shape[1]), BF16)],
+        compiler_params=small(8),
+        name="windows",
+    )(far(offsets), far(selected), far(series))
+
+
+def pack_kernel(width, sel_ref, turn_ref, t_ref, send_ref):
+    down, along = selected_ids(sel_ref, lax.axis_index("subj"))
+    _, _, shard_along, rank_along = places(down, along, width)
+    pack_slots(send_ref, t_ref[...], shard_along, rank_along, lax.axis_index("vox"), turn_ref[0])
+
+
+def pack(selected, turn, picked, devices, width):
+    return pl.pallas_call(
+        lambda *refs: pack_kernel(width, *refs),
+        out_shape=jax.ShapeDtypeStruct((devices, SLOTS, picked.shape[1]), BF16),
+        in_specs=[SMEM, SMEM, VMEM],
+        out_specs=VMEM,
+        compiler_params=small(4),
+        name="pack",
+    )(selected, turn, picked)
+
+
+def unpack_kernel(width, sel_ref, turn_ref, r_ref, base_ref, s_ref):
+    down, along = selected_ids(sel_ref, lax.axis_index("subj"))
+    shard, rank, _, _ = places(down, along, width)
+    held = r_ref.shape[0] * SLOTS
+    rank = jnp.broadcast_to(rank, (ROWS, 128)) - turn_ref[0] * SLOTS
+    source = jnp.where((rank >= 0) & (rank < SLOTS), shard * SLOTS + rank, -1)
+    chosen = jnp.concatenate(
+        [
+            jnp.where(source == iota((ROWS, 128), 1) + c, 1.0, 0.0).astype(BF16)
+            for c in range(0, held, 128)
         ],
-        out_specs=(pl.BlockSpec(memory_space=pltpu.VMEM), pl.BlockSpec(memory_space=pltpu.VMEM)),
-        scratch_shapes=[pltpu.VMEM((EP * TR, series.shape[1]), BF16)],
-        compiler_params=pltpu.CompilerParams(vmem_limit_bytes=8 << 20),
-        name="windows",
-    )(
-        pltpu.with_memory_space_constraint(offsets, pltpu.HBM),
-        pltpu.with_memory_space_constraint(selected, pltpu.HBM),
-        pltpu.with_memory_space_constraint(series, pltpu.HBM),
-    )
+        axis=1,
+    )
+    found = dot(chosen, r_ref[...].reshape(held, r_ref.shape[2]))
+    s_ref[...] = (base_ref[...].astype(F32) + found).astype(BF16)
+
+
+def unpack(selected, turn, arrived, base, width):
+    return pl.pallas_call(
+        lambda *refs: unpack_kernel(width, *refs),
+        out_shape=jax.ShapeDtypeStruct(base.shape, BF16),
+        in_specs=[SMEM, SMEM, VMEM, VMEM],
+        out_specs=VMEM,
+        compiler_params=small(4),
+        name="unpack",
+    )(selected, turn, arrived, base)
 
 
 def meeting(j, first, count):
@@ -247,37 +338,39 @@
     )(near(tile))
 
 
-def ring(step, size, stride, devices):
-    def moved(n):
-        place = (n // stride) % size
-        return n + ((place + step) % size - place) * stride
-
-    return [(n, moved(n)) for n in range(devices)]
-
-
 def swapped(x, r):
     return lax.ppermute(x, "subj", [(n, n ^ r) for n in range(GR)])
 
 
-def summed(x, size, stride, devices):
-    parts = [lax.ppermute(x, "vox", ring(n, size, stride, devices)) for n in range(1, size)]
-    return sum(parts, x)
+def whole_slab(selected, picked, send, turns, devices, width):
+    def exchanged(send, turn, base):
+        arrived = lax.all_to_all(send, "vox", split_axis=0, concat_axis=0, tiled=True)
+        return unpack(selected, turn, arrived, base, width)
+
+    def again(state):
+        turn, slab = state
+        send = pack(selected, turn, picked, devices, width)
+        return turn + 1, exchanged(send, turn, slab)
+
+    slab = exchanged(send, jnp.zeros((1,), jnp.int32), jnp.zeros_like(picked))
+    first = jnp.ones((1,), jnp.int32)
+    return lax.while_loop(lambda state: state[0][0] < turns[0], again, (first, slab))[1]
 
 
 def body(series, offsets, selected):
     devices = lax.axis_size("vox")
-    own, picked = take_windows(series, offsets, selected)
+    own, picked, send, turns = take_windows(series, offsets, selected, devices)
     across = swapped(own, 2)
     beside = swapped(own, 1)
     first = norms(own, beside, 0)
-    slab = summed(picked, 4, 8, devices)
-    slab = summed(slab, 4, 2, devices)
-    slab = summed(slab, 2, 1, devices)
+    slab = whole_slab(selected, picked, send, turns, devices, series.shape[2])
     beyond = swapped(across, 1)
     second = norms(across, beyond, 2)
     parts = [slab[r * KL : (r + 1) * KL] for r in range(GR)]
     parts = [parts[0]] + [swapped(parts[r], r) for r in range(1, GR)]
-    tiles = partial_kernels((own, beside, across, beyond), parts, (first, second), devices, F32)
+    tiles = partial_kernels(
+        (own, beside, across, beyond), parts, (first, second), devices, F32
+    )
     tiles = lax.all_to_all(tiles.astype(LINK), "vox", split_axis=0, concat_axis=0, tiled=True)
     tile = jnp.sum(tiles.astype(F32), axis=0)
     turn = [

time: 86.6 us -> 92.3 us (1.066)
  waiting for transfers between devices: 29.3 us -> 36.6 us
  Pallas kernels: 9.59 us -> 13.6 us
  blocking collectives: 28.2 us -> 24.4 us
  starting transfers between devices: 18.9 us -> 16.2 us
    all_to_all x0 -> x1, waiting for transfers between devices: none -> 13 us  [exchanged(): lax.all_to_all(send, 'vox', split_axis=0, concat_axis=0, tiled=True)]
    ppermute x7 -> x0, starting transfers between devices: 12.3 us -> none  [summed(): lax.ppermute(x, 'vox', ring(n, size, stride, devices))]
    ppermute x7 -> x0, waiting for transfers between devices: 10.8 us -> none  [summed(): lax.ppermute(x, 'vox', ring(n, size, stride, devices))]
    all_to_all x0 -> x1, starting transfers between devices: none -> 9.89 us  [exchanged(): lax.all_to_all(send, 'vox', split_axis=0, concat_axis=0, tiled=True)]
    ppermute x6, waiting for transfers between devices: 14.1 us -> 19 us  [swapped(): return lax.ppermute(x, 'subj', [(n, n ^ r) for n in range(GR)])]
    all_to_all x1, blocking collectives: 28.2 us -> 24.4 us  [body(): lax.all_to_all(tiles.astype(LINK), 'vox', split_axis=0, concat_axis=0, ti...]
    pallas_call x1, Pallas kernels: 5.26 us -> 6.4 us  [partial_kernels(): pl.pallas_call(kernel_kernel, out_shape=pltpu.VMEM((devices, 3 * EP * SL,...]
    pallas_call x2, Pallas kernels: 1.51 us -> 2.64 us  [norms(): pl.pallas_call(lambda *refs: norm_kernel(first, *refs), out_shape=pltpu.V...]
  transfers between devices with their start and end apart: 14 -> 8, of which waited for: 7 -> 3; matrix products, arithmetic and copies ran while one was open for 0% -> 0% of each run, Pallas kernels for 2% -> 4%
where the time goes in v5:
time: 92.3 us; the launch traced here: 92 us
  waiting for transfers between devices  36.6 us (40%)
  blocking collectives  24.4 us (26%)
  starting transfers between devices  16.2 us (18%)
  Pallas kernels  13.6 us (15%)
    all_to_all x1, blocking collectives, body(): lax.all_to_all(tiles.astype(LINK), 'vox', split_axis=0, concat_axis=0, ti...  24.4 us
    ppermute x6, waiting for transfers between devices, swapped(): return lax.ppermute(x, 'subj', [(n, n ^ r) for n in range(GR)])  19 us
    all_to_all x1, waiting for transfers between devices, exchanged(): lax.all_to_all(send, 'vox', split_axis=0, concat_axis=0, tiled=True)  13 us
    all_to_all x1, starting transfers between devices, exchanged(): lax.all_to_all(send, 'vox', split_axis=0, concat_axis=0, tiled=True)  9.89 us
    pallas_call x1, Pallas kernels, partial_kernels(): pl.pallas_call(kernel_kernel, out_shape=pltpu.VMEM((devices, 3 * EP * SL,...  6.4 us
    ppermute x1, waiting for transfers between devices, body(): return in_order(lax.ppermute(tile, ('subj', 'vox'), turn))  4.65 us
    ppermute x1, starting transfers between devices, body(): return in_order(lax.ppermute(tile, ('subj', 'vox'), turn))  3.99 us
    pallas_call x1, Pallas kernels, take_windows(): pl.pallas_call(window_kernel, out_shape=(pltpu.VMEM((EP, SL * TR, width),...  2.84 us
  transfers between devices with their start and end apart: 8, of which 3 were waited for; matrix products, arithmetic and copies ran while one was open for 0% of the time, Pallas kernels for 4%

profile of v5, /device:TPU:8, one launch (start us, length us, event | category | flops | bytes accessed | tf_op | source)
XLA Modules:
  0.0 92.0 jit_solution(17567838998872123725)
XLA Ops:
  0.0 0.0 copy-start
  0.0 2.8 %windows.1 = (bf16[12,64,512]{2,1,0:T(8,128)(2,1)S(1)}, bf16[64,768]{1,0:T(8,128)(2,1)S(1)}, bf16[32,8,768]{2,1,0:T(8,128)(2,1)}, s32[1]{0:T(128)}) custom-call(s32[16,12]{1,0:T(8,128)} %off_ref.1, s32[64]{0:T(128)} %refs_0_.1, bf16[4,256,512]{2,1,0:T(8,128)(2,1)} %series_ref.1), custom_call_target="tpu_custom_call" | custom-call | tf_op jit(solution)/shard_map/windows/pallas_call | solution.py:124
  2.8 0.4 collective-permute-start.1
  3.3 0.0 collective-permute-start
  3.3 18.9 %collective-permute-done.1.refs_0_.e2 = bf16[12,64,512]{2,1,0:T(8,128)(2,1)S(1)} collective-permute-done((bf16[12,64,512]{2,1,0:T(8,128)(2,1)S(1)}, bf16[12,64,512]{2,1,0:T(8,128)(2,1)S(1)}, u32[]{:S(2)}, u32[]{:S(2)}) %collective-permute-start.1) | collective-permute-done | bytes 786464 | tf_op jit(solution)/shard_map/ppermute | solution.py:342
  22.2 0.0 collective-permute-start.2
  22.2 9.9 %all-to-all-start.1 = ((bf16[32,8,768]{2,1,0:T(8,128)(2,1)}), bf16[32,8,768]{2,1,0:T(8,128)(2,1)S(1)}, u32[]{:S(2)}, u32[]{:S(2)}) async-start(bf16[32,8,768]{2,1,0:T(8,128)(2,1)} %get-tuple-element.38), calls=%async_computation.1 | async-start | bytes 786432 | tf_op jit(solution)/shard_map/all_to_all | solution.py:347
  32.1 13.0 %all-to-all-done.1.refs_2_ = bf16[32,8,768]{2,1,0:T(8,128)(2,1)S(1)} async-done(((bf16[32,8,768]{2,1,0:T(8,128)(2,1)}), bf16[32,8,768]{2,1,0:T(8,128)(2,1)S(1)}, u32[]{:S(2)}, u32[]{:S(2)}) %all-to-all-start.1) | async-done | bytes 393248 | tf_op jit(solution)/shard_map/all_to_all | solution.py:347
  45.1 0.0 copy-done
  45.1 0.8 unpack.2
  46.0 0.7 while.10
  46.7 0.1 collective-permute-start.5
  46.8 1.4 %collective-permute-start.4 = (bf16[16,768]{1,0:T(8,128)(2,1)S(1)}, bf16[16,768]{1,0:T(8,128)(2,1)S(1)}, u32[]{:S(2)}, u32[]{:S(2)}) collective-permute-start(bf16[16,768]{1,0:T(8,128)(2,1)S(1)} %get-tuple-element.53), channel_id=1, source_target_pairs={{0,64},{32,96},{64,0},{96,32},{1,65},{33,97},{65,1},{97,33},{2,66}... | collective-permute-start | bytes 73736 | tf_op jit(solution)/shard_map/ppermute | solution.py:342
  48.2 0.4 collective-permute-start.3
  48.6 0.0 collective-permute-done.refs_1_.e1
  48.6 0.8 norms.2.na
  49.4 0.0 collective-permute-done.2.refs_1_.e3
  49.4 1.9 %norms.3.nb = f32[12,16,512]{2,1,0:T(8,128)S(1)} custom-call(bf16[12,64,512]{2,1,0:T(8,128)(2,1)S(1)} %collective-permute-done.1.refs_0_.e2, bf16[12,64,512]{2,1,0:T(8,128)(2,1)} %collective-permute-done.2.refs_1_.e3), custom_call_target="tpu_custom_call" | custom-call | tf_op jit(solution)/shard_map/norms/pallas_call | solution.py:205
  51.2 0.0 collective-permute-done.5.s3
  51.2 0.0 collective-permute-done.4.s2
  51.3 0.0 collective-permute-done.3.s1
  51.3 6.4 %partial_kernels.1 = f32[32,144,128]{2,1,0:T(8,128)S(1)} custom-call(bf16[12,64,512]{2,1,0:T(8,128)(2,1)S(1)} %get-tuple-element.37.refs_0_.e0, bf16[12,64,512]{2,1,0:T(8,128)(2,1)S(1)} %collective-permute-done.refs_1_.e1, bf16[12,64,512]{2,1,0:T(8,128)(2,1)S(1)} %collective-permute-done.1.refs_0_.e2, ...), custom_call_target="tpu_custom_call" | custom-call | tf_op jit(solution)/shard_map/partial_kernels/pallas_call | solution.py:295
  57.7 0.2 convert_element_type.6
  57.8 24.4 %all_to_all.15 = f16[32,144,128]{2,1,0:T(8,128)(2,1)S(1)} all-to-all(f16[32,144,128]{2,1,0:T(8,128)(2,1)S(1)} %convert_element_type.6), channel_id=1, replica_groups=mesh['subj'=4,'vox'=32] {'vox'}, dimensions={0} | all-to-all | bytes 2359296 | tf_op jit(solution)/shard_map/all_to_all | solution.py:374
  82.3 0.2 convert_reduce_fusion
  82.4 4.0 %collective-permute-start.6 = (f32[144,128]{1,0:T(8,128)S(1)}, f32[144,128]{1,0:T(8,128)S(1)}, u32[]{:S(2)}, u32[]{:S(2)}) collective-permute-start(f32[144,128]{1,0:T(8,128)S(1)} %convert_reduce_fusion), channel_id=1, source_target_pairs={{0,0},{1,1},{2,32},{3,33},{4,64},{5,65},{6,96},{7,97},{8,8},{9,9},... | collective-permute-start | bytes 221192 | tf_op jit(solution)/shard_map/ppermute | solution.py:383
  86.4 4.6 %collective-permute-done.6.y_ref = f32[144,128]{1,0:T(8,128)S(1)} collective-permute-done((f32[144,128]{1,0:T(8,128)S(1)}, f32[144,128]{1,0:T(8,128)S(1)}, u32[]{:S(2)}, u32[]{:S(2)}) %collective-permute-start.6) | collective-permute-done | bytes 73760 | tf_op jit(solution)/shard_map/ppermute | solution.py:383
  91.1 0.9 in_order.1
  (2 shorter events, 0.0 us)
Async XLA Ops:
  0.0 45.1 %copy-start = (s32[64]{0:T(128)S(1)}, s32[64]{0:T(128)}, u32[]{:S(2)}) copy-start(s32[64]{0:T(128)} %refs_0_.1) | copy-start | bytes 772
  2.8 19.4 %collective-permute-start.1 = (bf16[12,64,512]{2,1,0:T(8,128)(2,1)S(1)}, bf16[12,64,512]{2,1,0:T(8,128)(2,1)S(1)}, u32[]{:S(2)}, u32[]{:S(2)}) collective-permute-start(bf16[12,64,512]{2,1,0:T(8,128)(2,1)S(1)} %get-tuple-element.37.refs_0_.e0), channel_id=1, source_target_pairs={{0,64},{32,96},{64,0},{96,32},{1,65},{33,97},{65,1},{97,33},{2,66}... | collective-permute-start | bytes 2359304 | tf_op jit(solution)/shard_map/ppermute | solution.py:342
  3.3 45.3 %collective-permute-start = (bf16[12,64,512]{2,1,0:T(8,128)(2,1)S(1)}, bf16[12,64,512]{2,1,0:T(8,128)(2,1)S(1)}, u32[]{:S(2)}, u32[]{:S(2)}) collective-permute-start(bf16[12,64,512]{2,1,0:T(8,128)(2,1)S(1)} %get-tuple-element.37.refs_0_.e0), channel_id=1, source_target_pairs={{0,32},{32,0},{64,96},{96,64},{1,33},{33,1},{65,97},{97,65},{2,34}... | collective-permute-start | bytes 2359304 | tf_op jit(solution)/shard_map/ppermute | solution.py:342
  22.2 27.1 %collective-permute-start.2 = (bf16[12,64,512]{2,1,0:T(8,128)(2,1)S(1)}, bf16[12,64,512]{2,1,0:T(8,128)(2,1)}, u32[]{:S(2)}, u32[]{:S(2)}) collective-permute-start(bf16[12,64,512]{2,1,0:T(8,128)(2,1)S(1)} %collective-permute-done.1.refs_0_.e2), channel_id=1, source_target_pairs={{0,32},{32,0},{64,96},{96,64},{1,33},{33,1},{65,97},{97,65},{2,34}... | collective-permute-start | bytes 2359304 | tf_op jit(solution)/shard_map/ppermute | solution.py:342
  22.2 22.9 %all-to-all-start.1 = ((bf16[32,8,768]{2,1,0:T(8,128)(2,1)}), bf16[32,8,768]{2,1,0:T(8,128)(2,1)S(1)}, u32[]{:S(2)}, u32[]{:S(2)}) async-start(bf16[32,8,768]{2,1,0:T(8,128)(2,1)} %get-tuple-element.38), calls=%async_computation.1 | async-start | bytes 786432 | tf_op jit(solution)/shard_map/all_to_all | solution.py:347
  46.7 4.6 %collective-permute-start.5 = (bf16[16,768]{1,0:T(8,128)(2,1)S(1)}, bf16[16,768]{1,0:T(8,128)(2,1)S(1)}, u32[]{:S(2)}, u32[]{:S(2)}) collective-permute-start(bf16[16,768]{1,0:T(8,128)(2,1)S(1)} %get-tuple-element.52), channel_id=1, source_target_pairs={{0,96},{32,64},{64,32},{96,0},{1,97},{33,65},{65,33},{97,1},{2,98}... | collective-permute-start | bytes 73736 | tf_op jit(solution)/shard_map/ppermute | solution.py:342
  46.8 4.5 %collective-permute-start.4 = (bf16[16,768]{1,0:T(8,128)(2,1)S(1)}, bf16[16,768]{1,0:T(8,128)(2,1)S(1)}, u32[]{:S(2)}, u32[]{:S(2)}) collective-permute-start(bf16[16,768]{1,0:T(8,128)(2,1)S(1)} %get-tuple-element.53), channel_id=1, source_target_pairs={{0,64},{32,96},{64,0},{96,32},{1,65},{33,97},{65,1},{97,33},{2,66}... | collective-permute-start | bytes 73736 | tf_op jit(solution)/shard_map/ppermute | solution.py:342
  48.2 3.1 %collective-permute-start.3 = (bf16[16,768]{1,0:T(8,128)(2,1)S(1)}, bf16[16,768]{1,0:T(8,128)(2,1)S(1)}, u32[]{:S(2)}, u32[]{:S(2)}) collective-permute-start(bf16[16,768]{1,0:T(8,128)(2,1)S(1)} %get-tuple-element.54), channel_id=1, source_target_pairs={{0,32},{32,0},{64,96},{96,64},{1,33},{33,1},{65,97},{97,65},{2,34}... | collective-permute-start | bytes 73736 | tf_op jit(solution)/shard_map/ppermute | solution.py:342
  82.4 8.6 %collective-permute-start.6 = (f32[144,128]{1,0:T(8,128)S(1)}, f32[144,128]{1,0:T(8,128)S(1)}, u32[]{:S(2)}, u32[]{:S(2)}) collective-permute-start(f32[144,128]{1,0:T(8,128)S(1)} %convert_reduce_fusion), channel_id=1, source_target_pairs={{0,0},{1,1},{2,32},{3,33},{4,64},{5,65},{6,96},{7,97},{8,8},{9,9},... | collective-permute-start | bytes 221192 | tf_op jit(solution)/shard_map/ppermute | solution.py:383

commit v6 on v4

--- a/solution.py
+++ b/solution.py
@@ -42,7 +42,11 @@
     return hi, (x - hi.astype(F32)).astype(BF16)
 
 
-def window_kernel(off_ref, sel_ref, series_ref, e_ref, t_ref, w_ref):
+def owner(g, p):
+    return (p // 2) * 8 + ((p % 2) * 2 + g % 2) * 2 + g // 2
+
+
+def window_kernel(off_ref, sel_ref, series_ref, e_ref, keep_ref, give_ref, w_ref):
     j = lax.axis_index("subj")
     i = lax.axis_index("vox")
     width = series_ref.shape[2]
@@ -56,15 +60,17 @@
             e_ref[e, s * TR : (s + 1) * TR, :] = rows[e * TR : (e + 1) * TR]
     row = iota((GR * KL, 128), 0)
     column = jnp.zeros((GR * KL, 128), jnp.int32)
-    for r in range(GR):
+    for b, r in enumerate((0, 2, 1, 3)):
         for k in range(KL):
-            owner = (k // 4) * 8 + (j ^ r) * 2 + (k // 2) % 2
-            column = jnp.where(row == r * KL + k, sel_ref[2 * owner + k % 2] - i * width, column)
+            voxel = sel_ref[2 * owner(j ^ r, k // 2) + k % 2]
+            column = jnp.where(row == b * KL + k, voxel - i * width, column)
     lane = iota((GR * KL, 128), 1)
     picker = jnp.concatenate(
         [jnp.where(column == lane + c, 1.0, 0.0).astype(BF16) for c in range(0, width, 128)], axis=1
     )
-    t_ref[...] = dot_nt(picker, e_ref[...].reshape(EP * SL * TR, width)).astype(BF16)
+    picked = dot_nt(picker, e_ref[...].reshape(EP * SL * TR, width)).astype(BF16)
+    keep_ref[...] = picked[0 : 2 * KL]
+    give_ref[...] = picked[2 * KL :]
 
 
 def take_windows(series, offsets, selected):
@@ -73,14 +79,15 @@
         window_kernel,
         out_shape=(
             pltpu.VMEM((EP, SL * TR, width), BF16),
-            pltpu.VMEM((GR * KL, EP * SL * TR), BF16),
+            pltpu.VMEM((2 * KL, EP * SL * TR), BF16),
+            pltpu.VMEM((2 * KL, EP * SL * TR), BF16),
         ),
         in_specs=[
             pl.BlockSpec(memory_space=pltpu.SMEM),
             pl.BlockSpec(memory_space=pltpu.SMEM),
             pl.BlockSpec(memory_space=pltpu.VMEM),
         ],
-        out_specs=(pl.BlockSpec(memory_space=pltpu.VMEM), pl.BlockSpec(memory_space=pltpu.VMEM)),
+        out_specs=(pl.BlockSpec(memory_space=pltpu.VMEM),) * 3,
         scratch_shapes=[pltpu.VMEM((EP * TR, series.shape[1]), BF16)],
         compiler_params=pltpu.CompilerParams(vmem_limit_bytes=8 << 20),
         name="windows",
@@ -126,7 +133,10 @@
 ):
     j = lax.axis_index("subj")
     epochs = (e0, e1, e2, e3)
-    slabs = (s0, s1, s2, s3)
+    slabs = []
+    for one, other in ((s0, s1), (s2, s3)):
+        both = (one[...].astype(F32) + other[...].astype(F32)).astype(BF16)
+        slabs += [both[0:KL], both[KL : 2 * KL]]
     width = e0.shape[2]
     deep = SB * TR
     chunk = SL * TR
@@ -182,7 +192,7 @@
         for r in range(GR):
             lines = pl.ds(r, EP * SL, stride=GR)
             both = jnp.concatenate([g_ref[slot, n, lines, :] for n in range(3)], axis=0)
-            o_ref[(q // 2) * 8 + 2 * r + slot] = both.astype(o_ref.dtype)
+            o_ref[(q // 2) * 8 + slot * 4 + (r % 2) * 2 + r // 2] = both.astype(o_ref.dtype)
 
     def step(t, carry):
         scores(2 * t + 1, 1)
@@ -264,24 +274,44 @@
     return sum(parts, x)
 
 
+def along_y(x, chips, halves, devices):
+    moves = [
+        (j * devices + i, (j ^ (2 * chips)) * devices + (i ^ halves))
+        for j in range(GR)
+        for i in range(devices)
+    ]
+    return lax.ppermute(x, ("subj", "vox"), moves)
+
+
 def body(series, offsets, selected):
     devices = lax.axis_size("vox")
-    own, picked = take_windows(series, offsets, selected)
+    own, keep, give = take_windows(series, offsets, selected)
+    taken = swapped(give, 1)
     across = swapped(own, 2)
     beside = swapped(own, 1)
     first = norms(own, beside, 0)
-    slab = summed(picked, 4, 8, devices)
+    slab = jnp.concatenate([keep[:KL], taken[:KL], keep[KL:], taken[KL:]], axis=0)
+    slab = summed(slab, 4, 8, devices)
     slab = summed(slab, 4, 2, devices)
-    slab = summed(slab, 2, 1, devices)
     beyond = swapped(across, 1)
+    mine, theirs = slab[: 2 * KL], slab[2 * KL :]
+    parts = [
+        mine,
+        along_y(mine, 0, 1, devices),
+        along_y(theirs, 1, 0, devices),
+        along_y(theirs, 1, 1, devices),
+    ]
     second = norms(across, beyond, 2)
-    parts = [slab[r * KL : (r + 1) * KL] for r in range(GR)]
-    parts = [parts[0]] + [swapped(parts[r], r) for r in range(1, GR)]
-    tiles = partial_kernels((own, beside, across, beyond), parts, (first, second), devices, F32)
+    tiles = partial_kernels(
+        (own, beside, across, beyond), parts, (first, second), devices, F32
+    )
     tiles = lax.all_to_all(tiles.astype(LINK), "vox", split_axis=0, concat_axis=0, tiled=True)
     tile = jnp.sum(tiles.astype(F32), axis=0)
     turn = [
-        (j * devices + z * 8 + x * 2 + y, x * devices + z * 8 + j * 2 + y)
+        (
+            j * devices + z * 8 + x * 2 + y,
+            (2 * y + x % 2) * devices + z * 8 + (x // 2 * 2 + j % 2) * 2 + j // 2,
+        )
         for j in range(GR)
         for z in range(4)
         for x in range(4)

time: 86.6 us -> 80.2 us (0.926)
  blocking collectives: 28.2 us -> 25 us
  starting transfers between devices: 18.9 us -> 16.7 us
  waiting for transfers between devices: 29.3 us -> 27.9 us
    ppermute x0 -> x3, waiting for transfers between devices: none -> 4.04 us  [along_y(): return lax.ppermute(x, ('subj', 'vox'), moves)]
    ppermute x7 -> x6, waiting for transfers between devices: 10.8 us -> 6.86 us  [summed(): lax.ppermute(x, 'vox', ring(n, size, stride, devices))]
    ppermute x0 -> x3, starting transfers between devices: none -> 3.57 us  [along_y(): return lax.ppermute(x, ('subj', 'vox'), moves)]
    all_to_all x1, blocking collectives: 28.2 us -> 25 us  [body(): lax.all_to_all(tiles.astype(LINK), 'vox', split_axis=0, concat_axis=0, ti...]
    ppermute x1, starting transfers between devices: 4.23 us -> 2.07 us  [body(): return in_order(lax.ppermute(tile, ('subj', 'vox'), turn))]
    ppermute x6 -> x4, starting transfers between devices: 2.35 us -> 0.43 us  [swapped(): return lax.ppermute(x, 'subj', [(n, n ^ r) for n in range(GR)])]
    ppermute x7 -> x6, starting transfers between devices: 12.3 us -> 10.6 us  [summed(): lax.ppermute(x, 'vox', ring(n, size, stride, devices))]
    ppermute x6 -> x4, waiting for transfers between devices: 14.1 us -> 12.8 us  [swapped(): return lax.ppermute(x, 'subj', [(n, n ^ r) for n in range(GR)])]
  transfers between devices with their start and end apart: 14 -> 14, of which waited for: 7 -> 8; matrix products, arithmetic and copies ran while one was open for 0% -> 0% of each run, Pallas kernels for 2% -> 2%
where the time goes in v6:
time: 80.2 us; the launch traced here: 79.6 us
  waiting for transfers between devices  27.9 us (35%)
  blocking collectives  25 us (31%)
  starting transfers between devices  16.7 us (21%)
  Pallas kernels  9.57 us (12%)
    all_to_all x1, blocking collectives, body(): lax.all_to_all(tiles.astype(LINK), 'vox', split_axis=0, concat_axis=0, ti...  25 us
    ppermute x4, waiting for transfers between devices, swapped(): return lax.ppermute(x, 'subj', [(n, n ^ r) for n in range(GR)])  12.8 us
    ppermute x6, starting transfers between devices, summed(): lax.ppermute(x, 'vox', ring(n, size, stride, devices))  10.6 us
    ppermute x6, waiting for transfers between devices, summed(): lax.ppermute(x, 'vox', ring(n, size, stride, devices))  6.86 us
    pallas_call x1, Pallas kernels, partial_kernels(): pl.pallas_call(kernel_kernel, out_shape=pltpu.VMEM((devices, 3 * EP * SL,...  5.25 us
    ppermute x1, waiting for transfers between devices, body(): return in_order(lax.ppermute(tile, ('subj', 'vox'), turn))  4.17 us
    ppermute x3, waiting for transfers between devices, along_y(): return lax.ppermute(x, ('subj', 'vox'), moves)  4.04 us
    ppermute x3, starting transfers between devices, along_y(): return lax.ppermute(x, ('subj', 'vox'), moves)  3.57 us
  transfers between devices with their start and end apart: 14, of which 8 were waited for; matrix products, arithmetic and copies ran while one was open for 0% of the time, Pallas kernels for 2%

profile of v6, /device:TPU:8, one launch (start us, length us, event | category | flops | bytes accessed | tf_op | source)
XLA Modules:
  0.0 79.6 jit_solution(17521817643160797880)
XLA Ops:
  0.0 1.9 %windows.1 = (bf16[12,64,512]{2,1,0:T(8,128)(2,1)S(1)}, bf16[32,768]{1,0:T(8,128)(2,1)S(1)}, bf16[32,768]{1,0:T(8,128)(2,1)S(1)}) custom-call(s32[16,12]{1,0:T(8,128)} %off_ref.1, s32[64]{0:T(128)} %sel_ref.1, bf16[4,256,512]{2,1,0:T(8,128)(2,1)} %series_ref.1), custom_call_target="tpu_custom_call" | custom-call | tf_op jit(solution)/shard_map/windows/pallas_call | solution.py:78
  1.9 0.4 collective-permute-start.1
  2.3 1.2 %collective-permute-done.3 = bf16[32,768]{1,0:T(8,128)(2,1)S(1)} collective-permute-done((bf16[32,768]{1,0:T(8,128)(2,1)S(1)}, bf16[32,768]{1,0:T(8,128)(2,1)S(1)}, u32[]{:S(2)}, u32[]{:S(2)}) %collective-permute-start.3) | collective-permute-done | bytes 49184 | tf_op jit(solution)/shard_map/ppermute | solution.py:269
  3.6 4.1 %collective-permute-start.5 = (bf16[64,768]{1,0:T(8,128)(2,1)S(1)}, bf16[64,768]{1,0:T(8,128)(2,1)S(1)}, u32[]{:S(2)}, u32[]{:S(2)}) collective-permute-start(bf16[64,768]{1,0:T(8,128)(2,1)S(1)} %pad_maximum_fusion), channel_id=1, source_target_pairs={{0,16},{1,17},{2,18},{3,19},{4,20},{5,21},{6,22},{7,23},{8,24},{9,... | collective-permute-start | bytes 294920 | tf_op jit(solution)/shard_map/ppermute | solution.py:273
  7.6 0.7 collective-permute-start.6
  8.4 1.3 %collective-permute-start.4 = (bf16[64,768]{1,0:T(8,128)(2,1)S(1)}, bf16[64,768]{1,0:T(8,128)(2,1)S(1)}, u32[]{:S(2)}, u32[]{:S(2)}) collective-permute-start(bf16[64,768]{1,0:T(8,128)(2,1)S(1)} %pad_maximum_fusion), channel_id=1, source_target_pairs={{0,8},{1,9},{2,10},{3,11},{4,12},{5,13},{6,14},{7,15},{8,16},{9,17... | collective-permute-start | bytes 294920 | tf_op jit(solution)/shard_map/ppermute | solution.py:273
  9.7 0.0 collective-permute-start
  9.7 11.6 %collective-permute-done.1.refs_0_.e2 = bf16[12,64,512]{2,1,0:T(8,128)(2,1)S(1)} collective-permute-done((bf16[12,64,512]{2,1,0:T(8,128)(2,1)S(1)}, bf16[12,64,512]{2,1,0:T(8,128)(2,1)S(1)}, u32[]{:S(2)}, u32[]{:S(2)}) %collective-permute-start.1) | collective-permute-done | bytes 786464 | tf_op jit(solution)/shard_map/ppermute | solution.py:269
  21.3 0.0 collective-permute-start.2
  21.3 0.0 collective-permute-done.5
  21.3 0.0 collective-permute-done.6
  21.3 0.1 add_add_fusion.1
  21.4 2.8 %collective-permute-start.9 = (bf16[64,768]{1,0:T(8,128)(2,1)S(1)}, bf16[64,768]{1,0:T(8,128)(2,1)S(1)}, u32[]{:S(2)}, u32[]{:S(2)}) collective-permute-start(bf16[64,768]{1,0:T(8,128)(2,1)S(1)} %add_add_fusion.1), channel_id=1, source_target_pairs={{0,6},{1,7},{2,0},{3,1},{4,2},{5,3},{6,4},{7,5},{8,14},{9,15},{10,... | collective-permute-start | bytes 294920 | tf_op jit(solution)/shard_map/ppermute | solution.py:273
  24.2 0.8 collective-permute-start.8
  25.0 0.9 %collective-permute-start.7 = (bf16[64,768]{1,0:T(8,128)(2,1)S(1)}, bf16[64,768]{1,0:T(8,128)(2,1)S(1)}, u32[]{:S(2)}, u32[]{:S(2)}) collective-permute-start(bf16[64,768]{1,0:T(8,128)(2,1)S(1)} %add_add_fusion.1), channel_id=1, source_target_pairs={{0,2},{1,3},{2,4},{3,5},{4,6},{5,7},{6,0},{7,1},{8,10},{9,11},{10,... | collective-permute-start | bytes 294920 | tf_op jit(solution)/shard_map/ppermute | solution.py:273
  25.9 3.2 %collective-permute-done.9 = bf16[64,768]{1,0:T(8,128)(2,1)S(1)} collective-permute-done((bf16[64,768]{1,0:T(8,128)(2,1)S(1)}, bf16[64,768]{1,0:T(8,128)(2,1)S(1)}, u32[]{:S(2)}, u32[]{:S(2)}) %collective-permute-start.9) | collective-permute-done | bytes 98336 | tf_op jit(solution)/shard_map/ppermute | solution.py:273
  29.0 2.3 %collective-permute-done.8 = bf16[64,768]{1,0:T(8,128)(2,1)S(1)} collective-permute-done((bf16[64,768]{1,0:T(8,128)(2,1)S(1)}, bf16[64,768]{1,0:T(8,128)(2,1)S(1)}, u32[]{:S(2)}, u32[]{:S(2)}) %collective-permute-start.8) | collective-permute-done | bytes 98336 | tf_op jit(solution)/shard_map/ppermute | solution.py:273
  31.4 1.4 %collective-permute-done.7 = bf16[64,768]{1,0:T(8,128)(2,1)S(1)} collective-permute-done((bf16[64,768]{1,0:T(8,128)(2,1)S(1)}, bf16[64,768]{1,0:T(8,128)(2,1)S(1)}, u32[]{:S(2)}, u32[]{:S(2)}) %collective-permute-start.7) | collective-permute-done | bytes 98336 | tf_op jit(solution)/shard_map/ppermute | solution.py:273
  32.8 1.6 %collective-permute-start.12 = (bf16[32,768]{1,0:T(8,128)(2,1)S(1)}, bf16[32,768]{1,0:T(8,128)(2,1)S(1)}, u32[]{:S(2)}, u32[]{:S(2)}) collective-permute-start(bf16[32,768]{1,0:T(8,128)(2,1)S(1)} %get-tuple-element.11), channel_id=1, source_target_pairs={{0,65},{1,64},{2,67},{3,66},{4,69},{5,68},{6,71},{7,70},{8,73},{9,... | collective-permute-start | bytes 147464 | tf_op jit(solution)/shard_map/ppermute | solution.py:283
  34.4 1.9 %collective-permute-start.11 = (bf16[32,768]{1,0:T(8,128)(2,1)S(1)}, bf16[32,768]{1,0:T(8,128)(2,1)S(1)}, u32[]{:S(2)}, u32[]{:S(2)}) collective-permute-start(bf16[32,768]{1,0:T(8,128)(2,1)S(1)} %get-tuple-element.11), channel_id=1, source_target_pairs={{0,64},{1,65},{2,66},{3,67},{4,68},{5,69},{6,70},{7,71},{8,72},{9,... | collective-permute-start | bytes 147464 | tf_op jit(solution)/shard_map/ppermute | solution.py:283
  36.3 0.0 collective-permute-start.10
  36.3 0.8 norms.2.na
  37.1 0.8 norms.3.nb
  37.9 1.0 %collective-permute-done.11.s2 = bf16[32,768]{1,0:T(8,128)(2,1)S(1)} collective-permute-done((bf16[32,768]{1,0:T(8,128)(2,1)S(1)}, bf16[32,768]{1,0:T(8,128)(2,1)S(1)}, u32[]{:S(2)}, u32[]{:S(2)}) %collective-permute-start.11) | collective-permute-done | bytes 49184 | tf_op jit(solution)/shard_map/ppermute | solution.py:283
  38.8 3.1 %collective-permute-done.10.s1 = bf16[32,768]{1,0:T(8,128)(2,1)S(1)} collective-permute-done((bf16[32,768]{1,0:T(8,128)(2,1)S(1)}, bf16[32,768]{1,0:T(8,128)(2,1)S(1)}, u32[]{:S(2)}, u32[]{:S(2)}) %collective-permute-start.10) | collective-permute-done | bytes 49184 | tf_op jit(solution)/shard_map/ppermute | solution.py:283
  41.9 5.2 %partial_kernels.1 = f32[32,144,128]{2,1,0:T(8,128)S(1)} custom-call(bf16[12,64,512]{2,1,0:T(8,128)(2,1)S(1)} %get-tuple-element.8.refs_0_.e0, bf16[12,64,512]{2,1,0:T(8,128)(2,1)S(1)} %collective-permute-done.refs_1_.e1, bf16[12,64,512]{2,1,0:T(8,128)(2,1)S(1)} %collective-permute-done.1.refs_0_.e2, ...), custom_call_target="tpu_custom_call" | custom-call | tf_op jit(solution)/shard_map/partial_kernels/pallas_call | solution.py:214
  47.1 0.2 convert_element_type.6
  47.3 25.0 %all_to_all.5 = f16[32,144,128]{2,1,0:T(8,128)(2,1)S(1)} all-to-all(f16[32,144,128]{2,1,0:T(8,128)(2,1)S(1)} %convert_element_type.6), channel_id=1, replica_groups=mesh['subj'=4,'vox'=32] {'vox'}, dimensions={0} | all-to-all | bytes 2359296 | tf_op jit(solution)/shard_map/all_to_all | solution.py:308
  72.3 0.2 convert_reduce_fusion
  72.5 2.1 %collective-permute-start.13 = (f32[144,128]{1,0:T(8,128)S(1)}, f32[144,128]{1,0:T(8,128)S(1)}, u32[]{:S(2)}, u32[]{:S(2)}) collective-permute-start(f32[144,128]{1,0:T(8,128)S(1)} %convert_reduce_fusion), channel_id=1, source_target_pairs={{0,0},{1,64},{2,32},{3,96},{4,4},{5,68},{6,36},{7,100},{8,8},{9,72... | collective-permute-start | bytes 221192 | tf_op jit(solution)/shard_map/ppermute | solution.py:320
  74.5 4.2 %collective-permute-done.13.y_ref = f32[144,128]{1,0:T(8,128)S(1)} collective-permute-done((f32[144,128]{1,0:T(8,128)S(1)}, f32[144,128]{1,0:T(8,128)S(1)}, u32[]{:S(2)}, u32[]{:S(2)}) %collective-permute-start.13) | collective-permute-done | bytes 73760 | tf_op jit(solution)/shard_map/ppermute | solution.py:320
  78.7 0.9 %in_order.1 = f32[2,48,192]{2,1,0:T(8,128)} custom-call(f32[144,128]{1,0:T(8,128)S(1)} %collective-permute-done.13.y_ref), custom_call_target="tpu_custom_call" | custom-call | tf_op jit(solution)/shard_map/in_order/pallas_call | solution.py:250
  (10 shorter events, 0.1 us)
Async XLA Ops:
  1.9 19.4 %collective-permute-start.1 = (bf16[12,64,512]{2,1,0:T(8,128)(2,1)S(1)}, bf16[12,64,512]{2,1,0:T(8,128)(2,1)S(1)}, u32[]{:S(2)}, u32[]{:S(2)}) collective-permute-start(bf16[12,64,512]{2,1,0:T(8,128)(2,1)S(1)} %get-tuple-element.8.refs_0_.e0), channel_id=1, source_target_pairs={{0,64},{32,96},{64,0},{96,32},{1,65},{33,97},{65,1},{97,33},{2,66}... | collective-permute-start | bytes 2359304 | tf_op jit(solution)/shard_map/ppermute | solution.py:269
  2.3 1.2 %collective-permute-start.3 = (bf16[32,768]{1,0:T(8,128)(2,1)S(1)}, bf16[32,768]{1,0:T(8,128)(2,1)S(1)}, u32[]{:S(2)}, u32[]{:S(2)}) collective-permute-start(bf16[32,768]{1,0:T(8,128)(2,1)S(1)} %get-tuple-element.10), channel_id=1, source_target_pairs={{0,32},{32,0},{64,96},{96,64},{1,33},{33,1},{65,97},{97,65},{2,34}... | collective-permute-start | bytes 147464 | tf_op jit(solution)/shard_map/ppermute | solution.py:269
  3.6 17.7 %collective-permute-start.5 = (bf16[64,768]{1,0:T(8,128)(2,1)S(1)}, bf16[64,768]{1,0:T(8,128)(2,1)S(1)}, u32[]{:S(2)}, u32[]{:S(2)}) collective-permute-start(bf16[64,768]{1,0:T(8,128)(2,1)S(1)} %pad_maximum_fusion), channel_id=1, source_target_pairs={{0,16},{1,17},{2,18},{3,19},{4,20},{5,21},{6,22},{7,23},{8,24},{9,... | collective-permute-start | bytes 294920 | tf_op jit(solution)/shard_map/ppermute | solution.py:273
  7.6 13.6 %collective-permute-start.6 = (bf16[64,768]{1,0:T(8,128)(2,1)S(1)}, bf16[64,768]{1,0:T(8,128)(2,1)S(1)}, u32[]{:S(2)}, u32[]{:S(2)}) collective-permute-start(bf16[64,768]{1,0:T(8,128)(2,1)S(1)} %pad_maximum_fusion), channel_id=1, source_target_pairs={{0,24},{1,25},{2,26},{3,27},{4,28},{5,29},{6,30},{7,31},{8,0},{9,1... | collective-permute-start | bytes 294920 | tf_op jit(solution)/shard_map/ppermute | solution.py:273
  8.4 12.9 %collective-permute-start.4 = (bf16[64,768]{1,0:T(8,128)(2,1)S(1)}, bf16[64,768]{1,0:T(8,128)(2,1)S(1)}, u32[]{:S(2)}, u32[]{:S(2)}) collective-permute-start(bf16[64,768]{1,0:T(8,128)(2,1)S(1)} %pad_maximum_fusion), channel_id=1, source_target_pairs={{0,8},{1,9},{2,10},{3,11},{4,12},{5,13},{6,14},{7,15},{8,16},{9,17... | collective-permute-start | bytes 294920 | tf_op jit(solution)/shard_map/ppermute | solution.py:273
  9.7 26.7 %collective-permute-start = (bf16[12,64,512]{2,1,0:T(8,128)(2,1)S(1)}, bf16[12,64,512]{2,1,0:T(8,128)(2,1)S(1)}, u32[]{:S(2)}, u32[]{:S(2)}) collective-permute-start(bf16[12,64,512]{2,1,0:T(8,128)(2,1)S(1)} %get-tuple-element.8.refs_0_.e0), channel_id=1, source_target_pairs={{0,32},{32,0},{64,96},{96,64},{1,33},{33,1},{65,97},{97,65},{2,34}... | collective-permute-start | bytes 2359304 | tf_op jit(solution)/shard_map/ppermute | solution.py:269
  21.3 15.8 %collective-permute-start.2 = (bf16[12,64,512]{2,1,0:T(8,128)(2,1)S(1)}, bf16[12,64,512]{2,1,0:T(8,128)(2,1)S(1)}, u32[]{:S(2)}, u32[]{:S(2)}) collective-permute-start(bf16[12,64,512]{2,1,0:T(8,128)(2,1)S(1)} %collective-permute-done.1.refs_0_.e2), channel_id=1, source_target_pairs={{0,32},{32,0},{64,96},{96,64},{1,33},{33,1},{65,97},{97,65},{2,34}... | collective-permute-start | bytes 2359304 | tf_op jit(solution)/shard_map/ppermute | solution.py:269
  21.4 7.7 %collective-permute-start.9 = (bf16[64,768]{1,0:T(8,128)(2,1)S(1)}, bf16[64,768]{1,0:T(8,128)(2,1)S(1)}, u32[]{:S(2)}, u32[]{:S(2)}) collective-permute-start(bf16[64,768]{1,0:T(8,128)(2,1)S(1)} %add_add_fusion.1), channel_id=1, source_target_pairs={{0,6},{1,7},{2,0},{3,1},{4,2},{5,3},{6,4},{7,5},{8,14},{9,15},{10,... | collective-permute-start | bytes 294920 | tf_op jit(solution)/shard_map/ppermute | solution.py:273
  24.2 7.2 %collective-permute-start.8 = (bf16[64,768]{1,0:T(8,128)(2,1)S(1)}, bf16[64,768]{1,0:T(8,128)(2,1)S(1)}, u32[]{:S(2)}, u32[]{:S(2)}) collective-permute-start(bf16[64,768]{1,0:T(8,128)(2,1)S(1)} %add_add_fusion.1), channel_id=1, source_target_pairs={{0,4},{1,5},{2,6},{3,7},{4,0},{5,1},{6,2},{7,3},{8,12},{9,13},{10,... | collective-permute-start | bytes 294920 | tf_op jit(solution)/shard_map/ppermute | solution.py:273
  25.0 7.7 %collective-permute-start.7 = (bf16[64,768]{1,0:T(8,128)(2,1)S(1)}, bf16[64,768]{1,0:T(8,128)(2,1)S(1)}, u32[]{:S(2)}, u32[]{:S(2)}) collective-permute-start(bf16[64,768]{1,0:T(8,128)(2,1)S(1)} %add_add_fusion.1), channel_id=1, source_target_pairs={{0,2},{1,3},{2,4},{3,5},{4,6},{5,7},{6,0},{7,1},{8,10},{9,11},{10,... | collective-permute-start | bytes 294920 | tf_op jit(solution)/shard_map/ppermute | solution.py:273
  32.8 5.1 %collective-permute-start.12 = (bf16[32,768]{1,0:T(8,128)(2,1)S(1)}, bf16[32,768]{1,0:T(8,128)(2,1)S(1)}, u32[]{:S(2)}, u32[]{:S(2)}) collective-permute-start(bf16[32,768]{1,0:T(8,128)(2,1)S(1)} %get-tuple-element.11), channel_id=1, source_target_pairs={{0,65},{1,64},{2,67},{3,66},{4,69},{5,68},{6,71},{7,70},{8,73},{9,... | collective-permute-start | bytes 147464 | tf_op jit(solution)/shard_map/ppermute | solution.py:283
  34.4 4.4 %collective-permute-start.11 = (bf16[32,768]{1,0:T(8,128)(2,1)S(1)}, bf16[32,768]{1,0:T(8,128)(2,1)S(1)}, u32[]{:S(2)}, u32[]{:S(2)}) collective-permute-start(bf16[32,768]{1,0:T(8,128)(2,1)S(1)} %get-tuple-element.11), channel_id=1, source_target_pairs={{0,64},{1,65},{2,66},{3,67},{4,68},{5,69},{6,70},{7,71},{8,72},{9,... | collective-permute-start | bytes 147464 | tf_op jit(solution)/shard_map/ppermute | solution.py:283
  36.3 5.6 %collective-permute-start.10 = (bf16[32,768]{1,0:T(8,128)(2,1)S(1)}, bf16[32,768]{1,0:T(8,128)(2,1)S(1)}, u32[]{:S(2)}, u32[]{:S(2)}) collective-permute-start(bf16[32,768]{1,0:T(8,128)(2,1)S(1)} %get-tuple-element.12.s0), channel_id=1, source_target_pairs={{0,1},{1,0},{2,3},{3,2},{4,5},{5,4},{6,7},{7,6},{8,9},{9,8},{10,11... | collective-permute-start | bytes 147464 | tf_op jit(solution)/shard_map/ppermute | solution.py:283
  72.5 6.2 %collective-permute-start.13 = (f32[144,128]{1,0:T(8,128)S(1)}, f32[144,128]{1,0:T(8,128)S(1)}, u32[]{:S(2)}, u32[]{:S(2)}) collective-permute-start(f32[144,128]{1,0:T(8,128)S(1)} %convert_reduce_fusion), channel_id=1, source_target_pairs={{0,0},{1,64},{2,32},{3,96},{4,4},{5,68},{6,36},{7,100},{8,8},{9,72... | collective-permute-start | bytes 221192 | tf_op jit(solution)/shard_map/ppermute | solution.py:320

commit v7 on v3

v7 whole, which is shorter than its diff:
```python
import jax
import jax.numpy as jnp
from jax import lax
from jax.experimental import pallas as pl
from jax.experimental.pallas import tpu as pltpu
from jax.sharding import PartitionSpec as P


TR = 16
EP = 12
GR = 4
SL = 4
SB = GR * SL
KL = 16
PART = 2 * SL
HALF = EP * SB // 3
BLOCKS = ((0, 0), (0, 1), (0, 2), (1, 1), (1, 2), (2, 2))
QUARTER = len(BLOCKS) * HALF // GR
VOX = 16384
F32 = jnp.float32
BF16 = jnp.bfloat16
LINK = jnp.float16
series_floor = 1.0
spread_floor = 0.05
shrink_factor = 0.9


def near(x):
    return pltpu.with_memory_space_constraint(x, pltpu.VMEM)


SMEM = pl.BlockSpec(memory_space=pltpu.SMEM)
VMEM = pl.BlockSpec(memory_space=pltpu.VMEM)


def small(mib):
    return pltpu.CompilerParams(vmem_limit_bytes=mib << 20)


def iota(shape, dim):
    return lax.broadcasted_iota(jnp.int32, shape, dim)


def dot(a, b):
    return jnp.dot(a, b, preferred_element_type=F32)


def dot_nt(a, b):
    return lax.dot_general(a, b, (((1,), (1,)), ((), ())), preferred_element_type=F32)


def split(x):
    hi = x.astype(BF16)
    return hi, (x - hi.astype(F32)).astype(BF16)


def owner(g, p):
    return (p // 2) * 8 + ((p % 2) * 2 + g % 2) * 2 + g // 2


def window_kernel(off_ref, sel_ref, series_ref, e_ref, keep_ref, give_ref, w_ref):
    j = lax.axis_index("subj")
    i = lax.axis_index("vox")
    width = series_ref.shape[2]
    lead = iota((TR, series_ref.shape[1]), 1) - iota((TR, series_ref.shape[1]), 0)
    for s in range(SL):
        for e in range(EP):
            chosen = lead == off_ref[j * SL + s, e]
            w_ref[e * TR : (e + 1) * TR, :] = jnp.where(chosen, 1.0, 0.0).astype(BF16)
        rows = dot(w_ref[...], series_ref[s]).astype(BF16)
        for e in range(EP):
            e_ref[e, s * TR : (s + 1) * TR, :] = rows[e * TR : (e + 1) * TR]
    row = iota((GR * KL, 128), 0)
    column = jnp.zeros((GR * KL, 128), jnp.int32)
    for b, r in enumerate((0, 2, 1, 3)):
        for k in range(KL):
            voxel = sel_ref[2 * owner(j ^ r, k // 2) + k % 2]
            column = jnp.where(row == b * KL + k, voxel - i * width, column)
    lane = iota((GR * KL, 128), 1)
    picker = jnp.concatenate(
        [jnp.where(column == lane + c, 1.0, 0.0).astype(BF16) for c in range(0, width, 128)], axis=1
    )
    picked = dot_nt(picker, e_ref[...].reshape(EP * SL * TR, width)).astype(BF16)
    keep_ref[...] = picked[0 : 2 * KL]
    give_ref[...] = picked[2 * KL :]


def take_windows(series, offsets, selected):
    width = series.shape[2]
    return pl.pallas_call(
        window_kernel,
        out_shape=(
            pltpu.VMEM((EP, SL * TR, width), BF16),
            pltpu.VMEM((2 * KL, EP * SL * TR), BF16),
            pltpu.VMEM((2 * KL, EP * SL * TR), BF16),
        ),
        in_specs=[
            pl.BlockSpec(memory_space=pltpu.SMEM),
            pl.BlockSpec(memory_space=pltpu.SMEM),
            pl.BlockSpec(memory_space=pltpu.VMEM),
        ],
        out_specs=(pl.BlockSpec(memory_space=pltpu.VMEM),) * 3,
        scratch_shapes=[pltpu.VMEM((EP * TR, series.shape[1]), BF16)],
        compiler_params=pltpu.CompilerParams(vmem_limit_bytes=8 << 20),
        name="windows",
    )(
        pltpu.with_memory_space_constraint(offsets, pltpu.HBM),
        pltpu.with_memory_space_constraint(selected, pltpu.HBM),
        pltpu.with_memory_space_constraint(series, pltpu.HBM),
    )


def meeting(j):
    place = iota((PART, 2 * SL * TR), 1)
    home = ((place // TR) % SL) * 2 + ((place // (SL * TR)) ^ j) % 2
    return iota((PART, 2 * SL * TR), 0) == home


def norm_kernel(e0, e1, n_ref):
    gather = jnp.where(meeting(lax.axis_index("subj")), 1.0, 0.0).astype(BF16)
    for e in range(EP):
        x = jnp.concatenate([e0[e], e1[e]], axis=0)
        xf = x.astype(F32)
        high, low = split(xf * xf)
        total = dot(gather, x)
        square = dot(gather, high) + dot(gather, low)
        n_ref[e] = square - total * total * (1.0 / TR)


def norms(e0, e1):
    return pl.pallas_call(
        norm_kernel,
        out_shape=pltpu.VMEM((EP, PART, e0.shape[2]), F32),
        in_specs=[VMEM] * 2,
        out_specs=VMEM,
        compiler_params=small(4),
        name="norms",
    )(near(e0), near(e1))


def fisher_kernel(e0, e1, s0, s1, n_ref, f_ref, l_ref):
    width = e0.shape[2]
    deep = 2 * SL * TR
    chunk = SL * TR
    mine = jnp.where(meeting(lax.axis_index("subj")), 1.0, 0.0)
    mine = jnp.concatenate([mine, mine], axis=0).astype(BF16)
    same = (iota((deep, deep), 0) // TR == iota((deep, deep), 1) // TR).astype(F32).astype(BF16)
    both = (s0[...].astype(F32) + s1[...].astype(F32)).astype(BF16)
    slab = jnp.concatenate(
        [
            jnp.concatenate([both[r : r + KL, e * chunk : (e + 1) * chunk] for r in (0, KL)], axis=1)
            for e in range(EP)
        ],
        axis=0,
    )
    centred = slab.astype(F32) - dot(slab, same) * (1.0 / TR)
    high, low = split(centred * centred)
    power = dot(high, same) + dot(low, same)
    slab_std = centred * (lax.rsqrt(power + series_floor) * shrink_factor)
    halves = [half.astype(F32) for half in split(slab_std)]
    for e in range(EP):
        x = jnp.concatenate([e0[e], e1[e]] * 2, axis=0)
        norm = jnp.sqrt(n_ref[e] + series_floor)[None]
        for k in range(0, KL, 2):
            for n, half in enumerate(halves):
                row = e * KL + k
                line = [jnp.broadcast_to(half[r : r + 1], (PART, deep)) for r in (row, row + 1)]
                line = jnp.concatenate(line, axis=0).astype(BF16) * mine
                l_ref[e % 2, k * PART : (k + 2) * PART, n * deep : (n + 1) * deep] = line
        shrunk = dot(l_ref[e % 2], x).reshape(KL, PART, width)
        f_ref[e] = jnp.log((norm + shrunk) / (norm - shrunk)).reshape(KL * PART, width)


def fishers(e0, e1, s0, s1, power):
    width = e0.shape[2]
    return pl.pallas_call(
        fisher_kernel,
        out_shape=pltpu.VMEM((EP, KL * PART, width), F32),
        in_specs=[VMEM] * 5,
        out_specs=VMEM,
        scratch_shapes=[pltpu.VMEM((2, KL * PART, 4 * SL * TR), BF16)],
        compiler_params=small(8),
        name="fishers",
    )(*map(near, (e0, e1, s0, s1, power)))


def kernel_kernel(fa, fb, o_ref, z_ref):
    width = fa.shape[2]

    def scores(q, slot):
        for h in range(2):
            rows = pl.ds(pl.multiple_of((q * 2 + h) * PART, PART), PART)
            for c in range(0, width, 128):
                tiles = []
                for f_ref in (fa, fb):
                    fisher = [f_ref[e, rows, c : c + 128] for e in range(EP)]
                    mean = sum(fisher[1:], fisher[0]) * (1.0 / EP)
                    fisher = [f - mean for f in fisher]
                    spread = fisher[0] * fisher[0]
                    for f in fisher[1:]:
                        spread = spread + f * f
                    scale = lax.rsqrt(spread * (1.0 / EP) + 4.0 * spread_floor)
                    tiles.append([f * scale for f in fisher])
                for e in range(EP):
                    tile = jnp.concatenate([tiles[0][e], tiles[1][e]], axis=0).astype(BF16)
                    z_ref[slot, h, e * SB : (e + 1) * SB, c : c + 128] = tile

    def products(q, slot):
        for h in range(2):
            product = dot_nt(z_ref[slot, h], z_ref[slot, h])
            for n, (low, high) in enumerate(BLOCKS):
                tile = product[low * HALF : (low + 1) * HALF, high * HALF : (high + 1) * HALF]
                for first in range(0, HALF, HALF // 2):
                    r, line = divmod(n * HALF + first, QUARTER)
                    to = (q // 2) * 8 + (slot * 2 + r % 2) * 2 + r // 2
                    part = tile[first : first + HALF // 2]
                    o_ref[to, line : line + HALF // 2, h * HALF : (h + 1) * HALF] = part

    def step(t, carry):
        scores(2 * t + 1, 1)
        products(2 * t, 0)
        scores(2 * t + 2, 0)
        products(2 * t + 1, 1)
        return carry

    last = KL // 2 - 1
    scores(0, 0)
    lax.fori_loop(0, last // 2, step, 0)
    scores(last, 1)
    products(last - 1, 0)
    products(last, 1)


def partial_kernels(fa, fb, devices):
    width = fa.shape[2]
    return pl.pallas_call(
        kernel_kernel,
        out_shape=pltpu.VMEM((devices, QUARTER, 2 * HALF), F32),
        in_specs=[VMEM] * 2,
        out_specs=VMEM,
        scratch_shapes=[pltpu.VMEM((2, 2, EP * SB, width), BF16)],
        compiler_params=small(8),
        name="partial_kernels",
    )(near(fa), near(fb))


def order_kernel(y0, y1, y2, y3, o_ref, b_ref, k_ref):
    j = lax.axis_index("subj")
    for r, y in enumerate((y0, y1, y2, y3)):
        b_ref[pl.ds(pl.multiple_of((j ^ r) * QUARTER, QUARTER), QUARTER), :] = y[...]
    for n, (low, high) in enumerate(BLOCKS):
        tile = b_ref[n * HALF : (n + 1) * HALF, :]
        mirrored = tile.T
        for h in range(2):
            block = tile[:, h * HALF : (h + 1) * HALF]
            at = (high % 2) * HALF
            k_ref[h, high // 2, low * HALF : (low + 1) * HALF, at : at + HALF] = block
            if low != high:
                block = mirrored[h * HALF : (h + 1) * HALF]
                at = (low % 2) * HALF
                k_ref[h, low // 2, high * HALF : (high + 1) * HALF, at : at + HALF] = block
    cols = EP * SB
    turn = lax.axis_index("vox") % 2
    source = iota((cols, cols), 0)
    group = (((source // PART) % 2) ^ turn) * 2 + source % 2
    target = group * (EP * SL) + ((source // 2) % SL) * EP + source // SB
    column = jnp.where(iota((cols, cols), 1) == target, 1.0, 0.0).astype(BF16)
    for h in range(2):
        lines = []
        for s in range(SL):
            own = pl.ds((j // 2 ^ turn) * PART + s * 2 + j % 2, EP, stride=SB)
            lines.append(jnp.concatenate([k_ref[h, 0, own, :], k_ref[h, 1, own, :][:, 0:HALF]], axis=1))
        whole = jnp.concatenate(lines, axis=0)
        high, _ = split(whole)
        middle, low = split(whole - high.astype(F32))
        o_ref[h] = (dot(high, column) + dot(middle, column) + dot(low, column)) * (1.0 / VOX)


def in_order(tiles):
    return pl.pallas_call(
        order_kernel,
        out_shape=jax.ShapeDtypeStruct((2, EP * SL, EP * SB), F32),
        in_specs=[pl.BlockSpec(memory_space=pltpu.VMEM)] * GR,
        out_specs=pl.BlockSpec(memory_space=pltpu.VMEM),
        scratch_shapes=[
            pltpu.VMEM((len(BLOCKS) * HALF, 2 * HALF), F32),
            pltpu.VMEM((2, 2, EP * SB, 2 * HALF), F32),
        ],
        compiler_params=pltpu.CompilerParams(vmem_limit_bytes=4 << 20),
        name="in_order",
    )(*map(near, tiles))


def swapped(x, r):
    return lax.ppermute(x, "subj", [(n, n ^ r) for n in range(GR)])


def summed(x, stride, devices):
    parts = [
        lax.ppermute(x, "vox", [(n, n ^ (step * stride)) for n in range(devices)])
        for step in (1, 3, 2)
    ]
    return sum(parts, x)


def along_y(x, chips, halves, devices):
    moves = [
        (j * devices + i, (j ^ (2 * chips)) * devices + (i ^ halves))
        for j in range(GR)
        for i in range(devices)
    ]
    return lax.ppermute(x, ("subj", "vox"), moves)


def body(series, offsets, selected):
    devices = lax.axis_size("vox")
    own, keep, give = take_windows(series, offsets, selected)
    taken = swapped(give, 1)
    across = swapped(own, 2)
    beside = swapped(own, 1)
    first = norms(own, beside)
    slab = jnp.concatenate([keep[:KL], taken[:KL], keep[KL:], taken[KL:]], axis=0)
    slab = summed(slab, 8, devices)
    slab = summed(slab, 2, devices)
    beyond = swapped(across, 1)
    mine, theirs = slab[: 2 * KL], slab[2 * KL :]
    ours = along_y(mine, 0, 1, devices)
    left = along_y(theirs, 1, 0, devices)
    right = along_y(theirs, 1, 1, devices)
    second = norms(across, beyond)
    fa = fishers(own, beside, mine, ours, first)
    fb = fishers(across, beyond, left, right, second)
    tiles = partial_kernels(fa, fb, devices)
    tiles = lax.all_to_all(tiles.astype(LINK), "vox", split_axis=0, concat_axis=0, tiled=True)
    tile = jnp.sum(tiles.astype(F32), axis=0)

    def turned(chips):
        moves = [
            (
                j * devices + z * 8 + x * 2 + y,
                ((2 * y + x % 2) ^ (2 * chips)) * devices + z * 8 + (x // 2 * 2 + j % 2) * 2 + j // 2,
            )
            for j in range(GR)
            for z in range(4)
            for x in range(4)
            for y in range(2)
        ]
        return lax.ppermute(tile, ("subj", "vox"), moves)

    here, there = turned(0), turned(1)
    return in_order((here, swapped(here, 1), there, swapped(there, 1)))


def solution(mesh):
    placed = (P("subj", None, "vox"), P(), P())
    return jax.shard_map(
        body, mesh=mesh, in_specs=placed, out_specs=P("vox", "subj", None), check_vma=False
    )
```

time: 90.9 us -> 79.1 us (0.87)
  waiting for transfers between devices: 31.9 us -> 22.8 us
  Pallas kernels: 12.8 us -> 10.8 us
    ppermute x8 -> x11, waiting for transfers between devices: 15.1 us -> 7.84 us  [the longest x6 5 us: summed(): lax.ppermute(x, 'vox', [(n, n ^ step * stride) for n in range(devices)])]
    pallas_call x1, Pallas kernels: 8.26 us -> 2.99 us  [partial_kernels(): pl.pallas_call(kernel_kernel, out_shape=pltpu.VMEM((devices, QUARTER, 2 *...]
    ppermute x9 -> x6, starting transfers between devices: 4.22 us -> 0.51 us  [swapped(): return lax.ppermute(x, 'subj', [(n, n ^ r) for n in range(GR)])]
    pallas_call x2 -> x4, Pallas kernels: 1.51 us -> 4.83 us  [the longest x2 3.32 us: fishers(): pl.pallas_call(fisher_kernel, out_shape=pltpu.VMEM((EP, KL * PART, width)...]
    ppermute x8 -> x11, starting transfers between devices: 16.3 us -> 19.2 us  [the longest x6 9.41 us: summed(): lax.ppermute(x, 'vox', [(n, n ^ step * stride) for n in range(devices)])]
    ppermute x9 -> x6, waiting for transfers between devices: 16.8 us -> 15 us  [swapped(): return lax.ppermute(x, 'subj', [(n, n ^ r) for n in range(GR)])]
  transfers between devices with their start and end apart: 17 -> 17, of which waited for: 9 -> 7; matrix products, arithmetic and copies ran while one was open for 0% -> 0% of each run, Pallas kernels for 2% -> 4%
where the time goes in v7:
time: 79.1 us; the launch traced here: 78.2 us
  blocking collectives  24.5 us (31%)
  waiting for transfers between devices  22.8 us (29%)
  starting transfers between devices  19.7 us (25%)
  Pallas kernels  10.8 us (14%)
    all_to_all x1, blocking collectives, body(): lax.all_to_all(tiles.astype(LINK), 'vox', split_axis=0, concat_axis=0, ti...  24.5 us
    ppermute x6, waiting for transfers between devices, swapped(): return lax.ppermute(x, 'subj', [(n, n ^ r) for n in range(GR)])  15 us
    ppermute x6, starting transfers between devices, summed(): lax.ppermute(x, 'vox', [(n, n ^ step * stride) for n in range(devices)])  9.41 us
    ppermute x6, waiting for transfers between devices, summed(): lax.ppermute(x, 'vox', [(n, n ^ step * stride) for n in range(devices)])  5 us
    ppermute x2, starting transfers between devices, turned(): return lax.ppermute(tile, ('subj', 'vox'), moves)  4.97 us
    ppermute x3, starting transfers between devices, along_y(): return lax.ppermute(x, ('subj', 'vox'), moves)  4.78 us
    pallas_call x2, Pallas kernels, fishers(): pl.pallas_call(fisher_kernel, out_shape=pltpu.VMEM((EP, KL * PART, width)...  3.32 us
    pallas_call x1, Pallas kernels, partial_kernels(): pl.pallas_call(kernel_kernel, out_shape=pltpu.VMEM((devices, QUARTER, 2 *...  2.99 us
  transfers between devices with their start and end apart: 17, of which 7 were waited for; matrix products, arithmetic and copies ran while one was open for 0% of the time, Pallas kernels for 4%

profile of v7, /device:TPU:8, one launch (start us, length us, event | category | flops | bytes accessed | tf_op | source)
XLA Modules:
  0.0 78.2 jit_solution(12626082365997525862)
XLA Ops:
  0.0 1.9 %windows.1 = (bf16[12,64,512]{2,1,0:T(8,128)(2,1)S(1)}, bf16[32,768]{1,0:T(8,128)(2,1)S(1)}, bf16[32,768]{1,0:T(8,128)(2,1)S(1)}) custom-call(s32[16,12]{1,0:T(8,128)} %off_ref.1, s32[64]{0:T(128)} %sel_ref.1, bf16[4,256,512]{2,1,0:T(8,128)(2,1)} %series_ref.1), custom_call_target="tpu_custom_call" | custom-call | tf_op jit(solution)/shard_map/windows/pallas_call | solution.py:90
  1.9 0.4 collective-permute-start.9
  2.3 1.2 %collective-permute-done.1 = bf16[32,768]{1,0:T(8,128)(2,1)S(1)} collective-permute-done((bf16[32,768]{1,0:T(8,128)(2,1)S(1)}, bf16[32,768]{1,0:T(8,128)(2,1)S(1)}, u32[]{:S(2)}, u32[]{:S(2)}) %collective-permute-start.1) | collective-permute-done | bytes 49184 | tf_op jit(solution)/shard_map/ppermute | solution.py:295
  3.6 4.2 %collective-permute-start.3 = (bf16[64,768]{1,0:T(8,128)(2,1)S(1)}, bf16[64,768]{1,0:T(8,128)(2,1)S(1)}, u32[]{:S(2)}, u32[]{:S(2)}) collective-permute-start(bf16[64,768]{1,0:T(8,128)(2,1)S(1)} %pad_maximum_fusion), channel_id=1, source_target_pairs={{0,24},{1,25},{2,26},{3,27},{4,28},{5,29},{6,30},{7,31},{8,16},{9,... | collective-permute-start | bytes 294920 | tf_op jit(solution)/shard_map/ppermute | solution.py:300
  7.8 0.9 %collective-permute-start.2 = (bf16[64,768]{1,0:T(8,128)(2,1)S(1)}, bf16[64,768]{1,0:T(8,128)(2,1)S(1)}, u32[]{:S(2)}, u32[]{:S(2)}) collective-permute-start(bf16[64,768]{1,0:T(8,128)(2,1)S(1)} %pad_maximum_fusion), channel_id=1, source_target_pairs={{0,8},{1,9},{2,10},{3,11},{4,12},{5,13},{6,14},{7,15},{8,0},{9,1},... | collective-permute-start | bytes 294920 | tf_op jit(solution)/shard_map/ppermute | solution.py:300
  8.8 0.0 collective-permute-start
  8.8 12.5 %collective-permute-done.9.e0 = bf16[12,64,512]{2,1,0:T(8,128)(2,1)S(1)} collective-permute-done((bf16[12,64,512]{2,1,0:T(8,128)(2,1)S(1)}, bf16[12,64,512]{2,1,0:T(8,128)(2,1)S(1)}, u32[]{:S(2)}, u32[]{:S(2)}) %collective-permute-start.9) | collective-permute-done | bytes 786464 | tf_op jit(solution)/shard_map/ppermute | solution.py:295
  21.3 0.0 collective-permute-start.10
  21.3 0.0 collective-permute-done.3
  21.3 0.1 add_add_fusion.1
  21.4 3.1 %collective-permute-start.7 = (bf16[64,768]{1,0:T(8,128)(2,1)S(1)}, bf16[64,768]{1,0:T(8,128)(2,1)S(1)}, u32[]{:S(2)}, u32[]{:S(2)}) collective-permute-start(bf16[64,768]{1,0:T(8,128)(2,1)S(1)} %add_add_fusion.1), channel_id=1, source_target_pairs={{0,4},{1,5},{2,6},{3,7},{4,0},{5,1},{6,2},{7,3},{8,12},{9,13},{10,... | collective-permute-start | bytes 294920 | tf_op jit(solution)/shard_map/ppermute | solution.py:300
  24.5 1.1 %collective-permute-start.6 = (bf16[64,768]{1,0:T(8,128)(2,1)S(1)}, bf16[64,768]{1,0:T(8,128)(2,1)S(1)}, u32[]{:S(2)}, u32[]{:S(2)}) collective-permute-start(bf16[64,768]{1,0:T(8,128)(2,1)S(1)} %add_add_fusion.1), channel_id=1, source_target_pairs={{0,6},{1,7},{2,4},{3,5},{4,2},{5,3},{6,0},{7,1},{8,14},{9,15},{10,... | collective-permute-start | bytes 294920 | tf_op jit(solution)/shard_map/ppermute | solution.py:300
  25.6 2.5 %collective-permute-done.7 = bf16[64,768]{1,0:T(8,128)(2,1)S(1)} collective-permute-done((bf16[64,768]{1,0:T(8,128)(2,1)S(1)}, bf16[64,768]{1,0:T(8,128)(2,1)S(1)}, u32[]{:S(2)}, u32[]{:S(2)}) %collective-permute-start.7) | collective-permute-done | bytes 98336 | tf_op jit(solution)/shard_map/ppermute | solution.py:300
  28.1 2.4 %collective-permute-done.6 = bf16[64,768]{1,0:T(8,128)(2,1)S(1)} collective-permute-done((bf16[64,768]{1,0:T(8,128)(2,1)S(1)}, bf16[64,768]{1,0:T(8,128)(2,1)S(1)}, u32[]{:S(2)}, u32[]{:S(2)}) %collective-permute-start.6) | collective-permute-done | bytes 98336 | tf_op jit(solution)/shard_map/ppermute | solution.py:300
  30.6 2.4 %collective-permute-start.8 = (bf16[32,768]{1,0:T(8,128)(2,1)S(1)}, bf16[32,768]{1,0:T(8,128)(2,1)S(1)}, u32[]{:S(2)}, u32[]{:S(2)}) collective-permute-start(bf16[32,768]{1,0:T(8,128)(2,1)S(1)} %get-tuple-element.12.s0), channel_id=1, source_target_pairs={{0,1},{1,0},{2,3},{3,2},{4,5},{5,4},{6,7},{7,6},{8,9},{9,8},{10,11... | collective-permute-start | bytes 147464 | tf_op jit(solution)/shard_map/ppermute | solution.py:312
  33.0 2.4 %collective-permute-start.11 = (bf16[32,768]{1,0:T(8,128)(2,1)S(1)}, bf16[32,768]{1,0:T(8,128)(2,1)S(1)}, u32[]{:S(2)}, u32[]{:S(2)}) collective-permute-start(bf16[32,768]{1,0:T(8,128)(2,1)S(1)} %get-tuple-element.11), channel_id=1, source_target_pairs={{0,64},{1,65},{2,66},{3,67},{4,68},{5,69},{6,70},{7,71},{8,72},{9,... | collective-permute-start | bytes 147464 | tf_op jit(solution)/shard_map/ppermute | solution.py:312
  35.4 0.8 norms.2.n_ref
  36.2 0.4 collective-permute-done.8.s1
  36.5 1.7 %fishers.2.fa = f32[12,128,512]{2,1,0:T(8,128)S(1)} custom-call(bf16[12,64,512]{2,1,0:T(8,128)(2,1)S(1)} %get-tuple-element.8.e0, bf16[12,64,512]{2,1,0:T(8,128)(2,1)S(1)} %collective-permute-done.e1, bf16[32,768]{1,0:T(8,128)(2,1)S(1)} %get-tuple-element.12.s0, bf16[32,768]{1,0:T(8,128)(2,1)S(1)} %collective-permute-done.8.s1, f32[12,8,512]{2,1,0:T(8,128)S(1)} %norms.2.n_ref), custom_call_target="tpu_custom_call" | custom-call | tf_op jit(solution)/shard_map/fishers/pallas_call | solution.py:176
  38.2 0.7 norms.3.n_ref
  39.0 0.0 collective-permute-done.11.s0
  39.0 1.7 %fishers.3.fb = f32[12,128,512]{2,1,0:T(8,128)S(1)} custom-call(bf16[12,64,512]{2,1,0:T(8,128)(2,1)S(1)} %collective-permute-done.9.e0, bf16[12,64,512]{2,1,0:T(8,128)(2,1)S(1)} %collective-permute-done.10.e1, bf16[32,768]{1,0:T(8,128)(2,1)S(1)} %collective-permute-done.11.s0, bf16[32,768]{1,0:T(8,128)(2,1)S(1)} %collective-permute-done.12.s1, ...), custom_call_target="tpu_custom_call" | custom-call | tf_op jit(solution)/shard_map/fishers/pallas_call | solution.py:176
  40.6 3.0 %partial_kernels.1 = f32[32,96,128]{2,1,0:T(8,128)S(1)} custom-call(f32[12,128,512]{2,1,0:T(8,128)S(1)} %fishers.2.fa, f32[12,128,512]{2,1,0:T(8,128)S(1)} %fishers.3.fb), custom_call_target="tpu_custom_call" | custom-call | tf_op jit(solution)/shard_map/partial_kernels/pallas_call | solution.py:236
  43.6 0.1 convert_element_type.6
  43.8 24.5 %all_to_all.5 = f16[32,96,128]{2,1,0:T(8,128)(2,1)S(1)} all-to-all(f16[32,96,128]{2,1,0:T(8,128)(2,1)S(1)} %convert_element_type.6), channel_id=1, replica_groups=mesh['subj'=4,'vox'=32] {'vox'}, dimensions={0} | all-to-all | bytes 1572864 | tf_op jit(solution)/shard_map/all_to_all | solution.py:334
  68.2 0.1 convert_reduce_fusion
  68.3 0.3 collective-permute-start.15
  68.7 4.6 %collective-permute-start.13 = (f32[96,128]{1,0:T(8,128)S(1)}, f32[96,128]{1,0:T(8,128)S(1)}, u32[]{:S(2)}, u32[]{:S(2)}) collective-permute-start(f32[96,128]{1,0:T(8,128)S(1)} %convert_reduce_fusion), channel_id=1, source_target_pairs={{0,0},{1,64},{2,32},{3,96},{4,4},{5,68},{6,36},{7,100},{8,8},{9,72... | collective-permute-start | bytes 147464 | tf_op jit(solution)/shard_map/ppermute | solution.py:348
  73.3 0.1 collective-permute-start.16
  73.4 2.5 %collective-permute-done.13.y0 = f32[96,128]{1,0:T(8,128)S(1)} collective-permute-done((f32[96,128]{1,0:T(8,128)S(1)}, f32[96,128]{1,0:T(8,128)S(1)}, u32[]{:S(2)}, u32[]{:S(2)}) %collective-permute-start.13) | collective-permute-done | bytes 49184 | tf_op jit(solution)/shard_map/ppermute | solution.py:348
  75.9 1.2 %collective-permute-done.14.y1 = f32[96,128]{1,0:T(8,128)S(1)} collective-permute-done((f32[96,128]{1,0:T(8,128)S(1)}, f32[96,128]{1,0:T(8,128)S(1)}, u32[]{:S(2)}, u32[]{:S(2)}) %collective-permute-start.14) | collective-permute-done | bytes 49184 | tf_op jit(solution)/shard_map/ppermute | solution.py:295
  77.1 1.1 %in_order.1 = f32[2,48,192]{2,1,0:T(8,128)} custom-call(f32[96,128]{1,0:T(8,128)S(1)} %collective-permute-done.13.y0, f32[96,128]{1,0:T(8,128)S(1)} %collective-permute-done.14.y1, f32[96,128]{1,0:T(8,128)S(1)} %collective-permute-done.15.y2, f32[96,128]{1,0:T(8,128)S(1)} %collective-permute-done.16.y3), custom_call_target="tpu_custom_call" | custom-call | tf_op jit(solution)/shard_map/in_order/pallas_call | solution.py:280
  (18 shorter events, 0.1 us)
Async XLA Ops:
  1.9 19.4 %collective-permute-start.9 = (bf16[12,64,512]{2,1,0:T(8,128)(2,1)S(1)}, bf16[12,64,512]{2,1,0:T(8,128)(2,1)S(1)}, u32[]{:S(2)}, u32[]{:S(2)}) collective-permute-start(bf16[12,64,512]{2,1,0:T(8,128)(2,1)S(1)} %get-tuple-element.8.e0), channel_id=1, source_target_pairs={{0,64},{32,96},{64,0},{96,32},{1,65},{33,97},{65,1},{97,33},{2,66}... | collective-permute-start | bytes 2359304 | tf_op jit(solution)/shard_map/ppermute | solution.py:295
  2.3 1.2 %collective-permute-start.1 = (bf16[32,768]{1,0:T(8,128)(2,1)S(1)}, bf16[32,768]{1,0:T(8,128)(2,1)S(1)}, u32[]{:S(2)}, u32[]{:S(2)}) collective-permute-start(bf16[32,768]{1,0:T(8,128)(2,1)S(1)} %get-tuple-element.10), channel_id=1, source_target_pairs={{0,32},{32,0},{64,96},{96,64},{1,33},{33,1},{65,97},{97,65},{2,34}... | collective-permute-start | bytes 147464 | tf_op jit(solution)/shard_map/ppermute | solution.py:295
  3.6 17.7 %collective-permute-start.3 = (bf16[64,768]{1,0:T(8,128)(2,1)S(1)}, bf16[64,768]{1,0:T(8,128)(2,1)S(1)}, u32[]{:S(2)}, u32[]{:S(2)}) collective-permute-start(bf16[64,768]{1,0:T(8,128)(2,1)S(1)} %pad_maximum_fusion), channel_id=1, source_target_pairs={{0,24},{1,25},{2,26},{3,27},{4,28},{5,29},{6,30},{7,31},{8,16},{9,... | collective-permute-start | bytes 294920 | tf_op jit(solution)/shard_map/ppermute | solution.py:300
  7.8 13.5 %collective-permute-start.4 = (bf16[64,768]{1,0:T(8,128)(2,1)S(1)}, bf16[64,768]{1,0:T(8,128)(2,1)S(1)}, u32[]{:S(2)}, u32[]{:S(2)}) collective-permute-start(bf16[64,768]{1,0:T(8,128)(2,1)S(1)} %pad_maximum_fusion), channel_id=1, source_target_pairs={{0,16},{1,17},{2,18},{3,19},{4,20},{5,21},{6,22},{7,23},{8,24},{9,... | collective-permute-start | bytes 294920 | tf_op jit(solution)/shard_map/ppermute | solution.py:300
  7.8 13.5 %collective-permute-start.2 = (bf16[64,768]{1,0:T(8,128)(2,1)S(1)}, bf16[64,768]{1,0:T(8,128)(2,1)S(1)}, u32[]{:S(2)}, u32[]{:S(2)}) collective-permute-start(bf16[64,768]{1,0:T(8,128)(2,1)S(1)} %pad_maximum_fusion), channel_id=1, source_target_pairs={{0,8},{1,9},{2,10},{3,11},{4,12},{5,13},{6,14},{7,15},{8,0},{9,1},... | collective-permute-start | bytes 294920 | tf_op jit(solution)/shard_map/ppermute | solution.py:300
  8.8 26.7 %collective-permute-start = (bf16[12,64,512]{2,1,0:T(8,128)(2,1)S(1)}, bf16[12,64,512]{2,1,0:T(8,128)(2,1)S(1)}, u32[]{:S(2)}, u32[]{:S(2)}) collective-permute-start(bf16[12,64,512]{2,1,0:T(8,128)(2,1)S(1)} %get-tuple-element.8.e0), channel_id=1, source_target_pairs={{0,32},{32,0},{64,96},{96,64},{1,33},{33,1},{65,97},{97,65},{2,34}... | collective-permute-start | bytes 2359304 | tf_op jit(solution)/shard_map/ppermute | solution.py:295
  21.3 16.9 %collective-permute-start.10 = (bf16[12,64,512]{2,1,0:T(8,128)(2,1)S(1)}, bf16[12,64,512]{2,1,0:T(8,128)(2,1)S(1)}, u32[]{:S(2)}, u32[]{:S(2)}) collective-permute-start(bf16[12,64,512]{2,1,0:T(8,128)(2,1)S(1)} %collective-permute-done.9.e0), channel_id=1, source_target_pairs={{0,32},{32,0},{64,96},{96,64},{1,33},{33,1},{65,97},{97,65},{2,34}... | collective-permute-start | bytes 2359304 | tf_op jit(solution)/shard_map/ppermute | solution.py:295
  21.4 6.8 %collective-permute-start.7 = (bf16[64,768]{1,0:T(8,128)(2,1)S(1)}, bf16[64,768]{1,0:T(8,128)(2,1)S(1)}, u32[]{:S(2)}, u32[]{:S(2)}) collective-permute-start(bf16[64,768]{1,0:T(8,128)(2,1)S(1)} %add_add_fusion.1), channel_id=1, source_target_pairs={{0,4},{1,5},{2,6},{3,7},{4,0},{5,1},{6,2},{7,3},{8,12},{9,13},{10,... | collective-permute-start | bytes 294920 | tf_op jit(solution)/shard_map/ppermute | solution.py:300
  24.5 6.1 %collective-permute-start.6 = (bf16[64,768]{1,0:T(8,128)(2,1)S(1)}, bf16[64,768]{1,0:T(8,128)(2,1)S(1)}, u32[]{:S(2)}, u32[]{:S(2)}) collective-permute-start(bf16[64,768]{1,0:T(8,128)(2,1)S(1)} %add_add_fusion.1), channel_id=1, source_target_pairs={{0,6},{1,7},{2,4},{3,5},{4,2},{5,3},{6,0},{7,1},{8,14},{9,15},{10,... | collective-permute-start | bytes 294920 | tf_op jit(solution)/shard_map/ppermute | solution.py:300
  25.6 5.0 %collective-permute-start.5 = (bf16[64,768]{1,0:T(8,128)(2,1)S(1)}, bf16[64,768]{1,0:T(8,128)(2,1)S(1)}, u32[]{:S(2)}, u32[]{:S(2)}) collective-permute-start(bf16[64,768]{1,0:T(8,128)(2,1)S(1)} %add_add_fusion.1), channel_id=1, source_target_pairs={{0,2},{1,3},{2,0},{3,1},{4,6},{5,7},{6,4},{7,5},{8,10},{9,11},{10,... | collective-permute-start | bytes 294920 | tf_op jit(solution)/shard_map/ppermute | solution.py:300
  30.6 5.9 %collective-permute-start.8 = (bf16[32,768]{1,0:T(8,128)(2,1)S(1)}, bf16[32,768]{1,0:T(8,128)(2,1)S(1)}, u32[]{:S(2)}, u32[]{:S(2)}) collective-permute-start(bf16[32,768]{1,0:T(8,128)(2,1)S(1)} %get-tuple-element.12.s0), channel_id=1, source_target_pairs={{0,1},{1,0},{2,3},{3,2},{4,5},{5,4},{6,7},{7,6},{8,9},{9,8},{10,11... | collective-permute-start | bytes 147464 | tf_op jit(solution)/shard_map/ppermute | solution.py:312
  33.0 6.0 %collective-permute-start.12 = (bf16[32,768]{1,0:T(8,128)(2,1)S(1)}, bf16[32,768]{1,0:T(8,128)(2,1)S(1)}, u32[]{:S(2)}, u32[]{:S(2)}) collective-permute-start(bf16[32,768]{1,0:T(8,128)(2,1)S(1)} %get-tuple-element.11), channel_id=1, source_target_pairs={{0,65},{1,64},{2,67},{3,66},{4,69},{5,68},{6,71},{7,70},{8,73},{9,... | collective-permute-start | bytes 147464 | tf_op jit(solution)/shard_map/ppermute | solution.py:312
  33.0 6.0 %collective-permute-start.11 = (bf16[32,768]{1,0:T(8,128)(2,1)S(1)}, bf16[32,768]{1,0:T(8,128)(2,1)S(1)}, u32[]{:S(2)}, u32[]{:S(2)}) collective-permute-start(bf16[32,768]{1,0:T(8,128)(2,1)S(1)} %get-tuple-element.11), channel_id=1, source_target_pairs={{0,64},{1,65},{2,66},{3,67},{4,68},{5,69},{6,70},{7,71},{8,72},{9,... | collective-permute-start | bytes 147464 | tf_op jit(solution)/shard_map/ppermute | solution.py:312
  68.3 5.0 %collective-permute-start.15 = (f32[96,128]{1,0:T(8,128)S(1)}, f32[96,128]{1,0:T(8,128)S(1)}, u32[]{:S(2)}, u32[]{:S(2)}) collective-permute-start(f32[96,128]{1,0:T(8,128)S(1)} %convert_reduce_fusion), channel_id=1, source_target_pairs={{0,64},{1,0},{2,96},{3,32},{4,68},{5,4},{6,100},{7,36},{8,72},{9,8... | collective-permute-start | bytes 147464 | tf_op jit(solution)/shard_map/ppermute | solution.py:348
  68.7 7.2 %collective-permute-start.13 = (f32[96,128]{1,0:T(8,128)S(1)}, f32[96,128]{1,0:T(8,128)S(1)}, u32[]{:S(2)}, u32[]{:S(2)}) collective-permute-start(f32[96,128]{1,0:T(8,128)S(1)} %convert_reduce_fusion), channel_id=1, source_target_pairs={{0,0},{1,64},{2,32},{3,96},{4,4},{5,68},{6,36},{7,100},{8,8},{9,72... | collective-permute-start | bytes 147464 | tf_op jit(solution)/shard_map/ppermute | solution.py:348
  73.3 2.6 %collective-permute-start.16 = (f32[96,128]{1,0:T(8,128)S(1)}, f32[96,128]{1,0:T(8,128)S(1)}, u32[]{:S(2)}, u32[]{:S(2)}) collective-permute-start(f32[96,128]{1,0:T(8,128)S(1)} %collective-permute-done.15.y2), channel_id=1, source_target_pairs={{0,32},{32,0},{64,96},{96,64},{1,33},{33,1},{65,97},{97,65},{2,34}... | collective-permute-start | bytes 147464 | tf_op jit(solution)/shard_map/ppermute | solution.py:295
  75.9 1.2 %collective-permute-start.14 = (f32[96,128]{1,0:T(8,128)S(1)}, f32[96,128]{1,0:T(8,128)S(1)}, u32[]{:S(2)}, u32[]{:S(2)}) collective-permute-start(f32[96,128]{1,0:T(8,128)S(1)} %collective-permute-done.13.y0), channel_id=1, source_target_pairs={{0,32},{32,0},{64,96},{96,64},{1,33},{33,1},{65,97},{97,65},{2,34}... | collective-permute-start | bytes 147464 | tf_op jit(solution)/shard_map/ppermute | solution.py:295

commit v8 on v7

--- a/solution.py
+++ b/solution.py
@@ -35,6 +35,10 @@
 
 def small(mib):
     return pltpu.CompilerParams(vmem_limit_bytes=mib << 20)
+
+
+def side(h, high):
+    return (h + high) % 2
 
 
 def iota(shape, dim):
@@ -153,18 +157,21 @@
         ],
         axis=0,
     )
-    centred = slab.astype(F32) - dot(slab, same) * (1.0 / TR)
-    high, low = split(centred * centred)
-    power = dot(high, same) + dot(low, same)
-    slab_std = centred * (lax.rsqrt(power + series_floor) * shrink_factor)
-    halves = [half.astype(F32) for half in split(slab_std)]
+    raw = slab.astype(F32)
+    high, low = split(raw * raw)
+    total = dot(slab, same)
+    power = dot(high, same) + dot(low, same) - total * total * (1.0 / TR)
+    slab_std = (raw - total * (1.0 / TR)) * (lax.rsqrt(power + series_floor) * shrink_factor)
+    high = slab_std.astype(BF16).astype(F32)
+    middle = (slab_std - high).astype(BF16).astype(F32)
+    thirds = (high, middle, slab_std - high - middle)
     for e in range(EP):
-        x = jnp.concatenate([e0[e], e1[e]] * 2, axis=0)
+        x = jnp.concatenate([e0[e], e1[e]] * 3, axis=0)
         norm = jnp.sqrt(n_ref[e] + series_floor)[None]
         for k in range(0, KL, 2):
-            for n, half in enumerate(halves):
+            for n, third in enumerate(thirds):
                 row = e * KL + k
-                line = [jnp.broadcast_to(half[r : r + 1], (PART, deep)) for r in (row, row + 1)]
+                line = [jnp.broadcast_to(third[r : r + 1], (PART, deep)) for r in (row, row + 1)]
                 line = jnp.concatenate(line, axis=0).astype(BF16) * mine
                 l_ref[e % 2, k * PART : (k + 2) * PART, n * deep : (n + 1) * deep] = line
         shrunk = dot(l_ref[e % 2], x).reshape(KL, PART, width)
@@ -178,7 +185,7 @@
         out_shape=pltpu.VMEM((EP, KL * PART, width), F32),
         in_specs=[VMEM] * 5,
         out_specs=VMEM,
-        scratch_shapes=[pltpu.VMEM((2, KL * PART, 4 * SL * TR), BF16)],
+        scratch_shapes=[pltpu.VMEM((2, KL * PART, 6 * SL * TR), BF16)],
         compiler_params=small(8),
         name="fishers",
     )(*map(near, (e0, e1, s0, s1, power)))
@@ -202,32 +209,35 @@
                     scale = lax.rsqrt(spread * (1.0 / EP) + 4.0 * spread_floor)
                     tiles.append([f * scale for f in fisher])
                 for e in range(EP):
+                    at = (e - h * EP // 3) % EP * SB
                     tile = jnp.concatenate([tiles[0][e], tiles[1][e]], axis=0).astype(BF16)
-                    z_ref[slot, h, e * SB : (e + 1) * SB, c : c + 128] = tile
+                    z_ref[slot, h, at : at + SB, c : c + 128] = tile
 
     def products(q, slot):
         for h in range(2):
             product = dot_nt(z_ref[slot, h], z_ref[slot, h])
             for n, (low, high) in enumerate(BLOCKS):
-                tile = product[low * HALF : (low + 1) * HALF, high * HALF : (high + 1) * HALF]
+                line, column = ((m - h) % 3 * HALF for m in (low, high))
+                tile = product[line : line + HALF, column : column + HALF]
+                column = side(h, high) * HALF
                 for first in range(0, HALF, HALF // 2):
                     r, line = divmod(n * HALF + first, QUARTER)
                     to = (q // 2) * 8 + (slot * 2 + r % 2) * 2 + r // 2
                     part = tile[first : first + HALF // 2]
-                    o_ref[to, line : line + HALF // 2, h * HALF : (h + 1) * HALF] = part
+                    o_ref[to, line : line + HALF // 2, column : column + HALF] = part
 
     def step(t, carry):
+        products(2 * t, 0)
         scores(2 * t + 1, 1)
-        products(2 * t, 0)
+        products(2 * t + 1, 1)
         scores(2 * t + 2, 0)
-        products(2 * t + 1, 1)
         return carry
 
     last = KL // 2 - 1
     scores(0, 0)
     lax.fori_loop(0, last // 2, step, 0)
+    products(last - 1, 0)
     scores(last, 1)
-    products(last - 1, 0)
     products(last, 1)
 
 
@@ -252,11 +262,12 @@
         tile = b_ref[n * HALF : (n + 1) * HALF, :]
         mirrored = tile.T
         for h in range(2):
-            block = tile[:, h * HALF : (h + 1) * HALF]
+            place = side(h, high) * HALF
+            block = tile[:, place : place + HALF]
             at = (high % 2) * HALF
             k_ref[h, high // 2, low * HALF : (low + 1) * HALF, at : at + HALF] = block
             if low != high:
-                block = mirrored[h * HALF : (h + 1) * HALF]
+                block = mirrored[place : place + HALF]
                 at = (low % 2) * HALF
                 k_ref[h, low // 2, high * HALF : (high + 1) * HALF, at : at + HALF] = block
     cols = EP * SB

time: 79.1 us -> 79 us (level)
  no operation moved by 1% of the time
where the time goes in v8:
time: 79 us; the launch traced here: 78.2 us
  blocking collectives  24.5 us (31%)
  waiting for transfers between devices  22.8 us (29%)
  starting transfers between devices  19.7 us (25%)
  Pallas kernels  10.7 us (14%)
    all_to_all x1, blocking collectives, body(): lax.all_to_all(tiles.astype(LINK), 'vox', split_axis=0, concat_axis=0, ti...  24.5 us
    ppermute x6, waiting for transfers between devices, swapped(): return lax.ppermute(x, 'subj', [(n, n ^ r) for n in range(GR)])  15 us
    ppermute x6, starting transfers between devices, summed(): lax.ppermute(x, 'vox', [(n, n ^ step * stride) for n in range(devices)])  9.41 us
    ppermute x6, waiting for transfers between devices, summed(): lax.ppermute(x, 'vox', [(n, n ^ step * stride) for n in range(devices)])  5 us
    ppermute x2, starting transfers between devices, turned(): return lax.ppermute(tile, ('subj', 'vox'), moves)  4.97 us
    ppermute x3, starting transfers between devices, along_y(): return lax.ppermute(x, ('subj', 'vox'), moves)  4.78 us
    pallas_call x2, Pallas kernels, fishers(): pl.pallas_call(fisher_kernel, out_shape=pltpu.VMEM((EP, KL * PART, width)...  3.25 us
    pallas_call x1, Pallas kernels, partial_kernels(): pl.pallas_call(kernel_kernel, out_shape=pltpu.VMEM((devices, QUARTER, 2 *...  2.99 us
  transfers between devices with their start and end apart: 17, of which 7 were waited for; matrix products, arithmetic and copies ran while one was open for 0% of the time, Pallas kernels for 4%

profile of v8, /device:TPU:8, one launch (start us, length us, event | category | flops | bytes accessed | tf_op | source)
XLA Modules:
  0.0 78.2 jit_solution(14685734396987996740)
XLA Ops:
  0.0 1.9 %windows.1 = (bf16[12,64,512]{2,1,0:T(8,128)(2,1)S(1)}, bf16[32,768]{1,0:T(8,128)(2,1)S(1)}, bf16[32,768]{1,0:T(8,128)(2,1)S(1)}) custom-call(s32[16,12]{1,0:T(8,128)} %off_ref.1, s32[64]{0:T(128)} %sel_ref.1, bf16[4,256,512]{2,1,0:T(8,128)(2,1)} %series_ref.1), custom_call_target="tpu_custom_call" | custom-call | tf_op jit(solution)/shard_map/windows/pallas_call | solution.py:94
  1.9 0.4 collective-permute-start.9
  2.3 1.2 %collective-permute-done.1 = bf16[32,768]{1,0:T(8,128)(2,1)S(1)} collective-permute-done((bf16[32,768]{1,0:T(8,128)(2,1)S(1)}, bf16[32,768]{1,0:T(8,128)(2,1)S(1)}, u32[]{:S(2)}, u32[]{:S(2)}) %collective-permute-start.1) | collective-permute-done | bytes 49184 | tf_op jit(solution)/shard_map/ppermute | solution.py:306
  3.6 4.2 %collective-permute-start.3 = (bf16[64,768]{1,0:T(8,128)(2,1)S(1)}, bf16[64,768]{1,0:T(8,128)(2,1)S(1)}, u32[]{:S(2)}, u32[]{:S(2)}) collective-permute-start(bf16[64,768]{1,0:T(8,128)(2,1)S(1)} %pad_maximum_fusion), channel_id=1, source_target_pairs={{0,24},{1,25},{2,26},{3,27},{4,28},{5,29},{6,30},{7,31},{8,16},{9,... | collective-permute-start | bytes 294920 | tf_op jit(solution)/shard_map/ppermute | solution.py:311
  7.8 0.9 %collective-permute-start.2 = (bf16[64,768]{1,0:T(8,128)(2,1)S(1)}, bf16[64,768]{1,0:T(8,128)(2,1)S(1)}, u32[]{:S(2)}, u32[]{:S(2)}) collective-permute-start(bf16[64,768]{1,0:T(8,128)(2,1)S(1)} %pad_maximum_fusion), channel_id=1, source_target_pairs={{0,8},{1,9},{2,10},{3,11},{4,12},{5,13},{6,14},{7,15},{8,0},{9,1},... | collective-permute-start | bytes 294920 | tf_op jit(solution)/shard_map/ppermute | solution.py:311
  8.8 0.0 collective-permute-start
  8.8 12.5 %collective-permute-done.9.e0 = bf16[12,64,512]{2,1,0:T(8,128)(2,1)S(1)} collective-permute-done((bf16[12,64,512]{2,1,0:T(8,128)(2,1)S(1)}, bf16[12,64,512]{2,1,0:T(8,128)(2,1)S(1)}, u32[]{:S(2)}, u32[]{:S(2)}) %collective-permute-start.9) | collective-permute-done | bytes 786464 | tf_op jit(solution)/shard_map/ppermute | solution.py:306
  21.3 0.0 collective-permute-start.10
  21.3 0.0 collective-permute-done.3
  21.3 0.1 add_add_fusion.1
  21.4 3.1 %collective-permute-start.7 = (bf16[64,768]{1,0:T(8,128)(2,1)S(1)}, bf16[64,768]{1,0:T(8,128)(2,1)S(1)}, u32[]{:S(2)}, u32[]{:S(2)}) collective-permute-start(bf16[64,768]{1,0:T(8,128)(2,1)S(1)} %add_add_fusion.1), channel_id=1, source_target_pairs={{0,4},{1,5},{2,6},{3,7},{4,0},{5,1},{6,2},{7,3},{8,12},{9,13},{10,... | collective-permute-start | bytes 294920 | tf_op jit(solution)/shard_map/ppermute | solution.py:311
  24.5 1.1 %collective-permute-start.6 = (bf16[64,768]{1,0:T(8,128)(2,1)S(1)}, bf16[64,768]{1,0:T(8,128)(2,1)S(1)}, u32[]{:S(2)}, u32[]{:S(2)}) collective-permute-start(bf16[64,768]{1,0:T(8,128)(2,1)S(1)} %add_add_fusion.1), channel_id=1, source_target_pairs={{0,6},{1,7},{2,4},{3,5},{4,2},{5,3},{6,0},{7,1},{8,14},{9,15},{10,... | collective-permute-start | bytes 294920 | tf_op jit(solution)/shard_map/ppermute | solution.py:311
  25.6 2.5 %collective-permute-done.7 = bf16[64,768]{1,0:T(8,128)(2,1)S(1)} collective-permute-done((bf16[64,768]{1,0:T(8,128)(2,1)S(1)}, bf16[64,768]{1,0:T(8,128)(2,1)S(1)}, u32[]{:S(2)}, u32[]{:S(2)}) %collective-permute-start.7) | collective-permute-done | bytes 98336 | tf_op jit(solution)/shard_map/ppermute | solution.py:311
  28.1 2.4 %collective-permute-done.6 = bf16[64,768]{1,0:T(8,128)(2,1)S(1)} collective-permute-done((bf16[64,768]{1,0:T(8,128)(2,1)S(1)}, bf16[64,768]{1,0:T(8,128)(2,1)S(1)}, u32[]{:S(2)}, u32[]{:S(2)}) %collective-permute-start.6) | collective-permute-done | bytes 98336 | tf_op jit(solution)/shard_map/ppermute | solution.py:311
  30.6 2.4 %collective-permute-start.8 = (bf16[32,768]{1,0:T(8,128)(2,1)S(1)}, bf16[32,768]{1,0:T(8,128)(2,1)S(1)}, u32[]{:S(2)}, u32[]{:S(2)}) collective-permute-start(bf16[32,768]{1,0:T(8,128)(2,1)S(1)} %get-tuple-element.12.s0), channel_id=1, source_target_pairs={{0,1},{1,0},{2,3},{3,2},{4,5},{5,4},{6,7},{7,6},{8,9},{9,8},{10,11... | collective-permute-start | bytes 147464 | tf_op jit(solution)/shard_map/ppermute | solution.py:323
  33.0 2.4 %collective-permute-start.11 = (bf16[32,768]{1,0:T(8,128)(2,1)S(1)}, bf16[32,768]{1,0:T(8,128)(2,1)S(1)}, u32[]{:S(2)}, u32[]{:S(2)}) collective-permute-start(bf16[32,768]{1,0:T(8,128)(2,1)S(1)} %get-tuple-element.11), channel_id=1, source_target_pairs={{0,64},{1,65},{2,66},{3,67},{4,68},{5,69},{6,70},{7,71},{8,72},{9,... | collective-permute-start | bytes 147464 | tf_op jit(solution)/shard_map/ppermute | solution.py:323
  35.4 0.8 norms.2.n_ref
  36.2 0.4 collective-permute-done.8.s1
  36.5 1.6 %fishers.2.fa = f32[12,128,512]{2,1,0:T(8,128)S(1)} custom-call(bf16[12,64,512]{2,1,0:T(8,128)(2,1)S(1)} %get-tuple-element.8.e0, bf16[12,64,512]{2,1,0:T(8,128)(2,1)S(1)} %collective-permute-done.e1, bf16[32,768]{1,0:T(8,128)(2,1)S(1)} %get-tuple-element.12.s0, bf16[32,768]{1,0:T(8,128)(2,1)S(1)} %collective-permute-done.8.s1, f32[12,8,512]{2,1,0:T(8,128)S(1)} %norms.2.n_ref), custom_call_target="tpu_custom_call" | custom-call | tf_op jit(solution)/shard_map/fishers/pallas_call | solution.py:183
  38.2 0.7 norms.3.n_ref
  38.9 0.0 collective-permute-done.11.s0
  39.0 1.6 %fishers.3.fb = f32[12,128,512]{2,1,0:T(8,128)S(1)} custom-call(bf16[12,64,512]{2,1,0:T(8,128)(2,1)S(1)} %collective-permute-done.9.e0, bf16[12,64,512]{2,1,0:T(8,128)(2,1)S(1)} %collective-permute-done.10.e1, bf16[32,768]{1,0:T(8,128)(2,1)S(1)} %collective-permute-done.11.s0, bf16[32,768]{1,0:T(8,128)(2,1)S(1)} %collective-permute-done.12.s1, ...), custom_call_target="tpu_custom_call" | custom-call | tf_op jit(solution)/shard_map/fishers/pallas_call | solution.py:183
  40.6 3.0 %partial_kernels.1 = f32[32,96,128]{2,1,0:T(8,128)S(1)} custom-call(f32[12,128,512]{2,1,0:T(8,128)S(1)} %fishers.2.fa, f32[12,128,512]{2,1,0:T(8,128)S(1)} %fishers.3.fb), custom_call_target="tpu_custom_call" | custom-call | tf_op jit(solution)/shard_map/partial_kernels/pallas_call | solution.py:246
  43.6 0.1 convert_element_type.6
  43.7 24.5 %all_to_all.5 = f16[32,96,128]{2,1,0:T(8,128)(2,1)S(1)} all-to-all(f16[32,96,128]{2,1,0:T(8,128)(2,1)S(1)} %convert_element_type.6), channel_id=1, replica_groups=mesh['subj'=4,'vox'=32] {'vox'}, dimensions={0} | all-to-all | bytes 1572864 | tf_op jit(solution)/shard_map/all_to_all | solution.py:345
  68.2 0.1 convert_reduce_fusion
  68.3 0.3 collective-permute-start.15
  68.6 4.6 %collective-permute-start.13 = (f32[96,128]{1,0:T(8,128)S(1)}, f32[96,128]{1,0:T(8,128)S(1)}, u32[]{:S(2)}, u32[]{:S(2)}) collective-permute-start(f32[96,128]{1,0:T(8,128)S(1)} %convert_reduce_fusion), channel_id=1, source_target_pairs={{0,0},{1,64},{2,32},{3,96},{4,4},{5,68},{6,36},{7,100},{8,8},{9,72... | collective-permute-start | bytes 147464 | tf_op jit(solution)/shard_map/ppermute | solution.py:359
  73.3 0.1 collective-permute-start.16
  73.4 2.5 %collective-permute-done.13.y0 = f32[96,128]{1,0:T(8,128)S(1)} collective-permute-done((f32[96,128]{1,0:T(8,128)S(1)}, f32[96,128]{1,0:T(8,128)S(1)}, u32[]{:S(2)}, u32[]{:S(2)}) %collective-permute-start.13) | collective-permute-done | bytes 49184 | tf_op jit(solution)/shard_map/ppermute | solution.py:359
  75.8 1.2 %collective-permute-done.14.y1 = f32[96,128]{1,0:T(8,128)S(1)} collective-permute-done((f32[96,128]{1,0:T(8,128)S(1)}, f32[96,128]{1,0:T(8,128)S(1)}, u32[]{:S(2)}, u32[]{:S(2)}) %collective-permute-start.14) | collective-permute-done | bytes 49184 | tf_op jit(solution)/shard_map/ppermute | solution.py:306
  77.1 1.1 %in_order.1 = f32[2,48,192]{2,1,0:T(8,128)} custom-call(f32[96,128]{1,0:T(8,128)S(1)} %collective-permute-done.13.y0, f32[96,128]{1,0:T(8,128)S(1)} %collective-permute-done.14.y1, f32[96,128]{1,0:T(8,128)S(1)} %collective-permute-done.15.y2, f32[96,128]{1,0:T(8,128)S(1)} %collective-permute-done.16.y3), custom_call_target="tpu_custom_call" | custom-call | tf_op jit(solution)/shard_map/in_order/pallas_call | solution.py:291
  (18 shorter events, 0.1 us)
Async XLA Ops:
  1.9 19.4 %collective-permute-start.9 = (bf16[12,64,512]{2,1,0:T(8,128)(2,1)S(1)}, bf16[12,64,512]{2,1,0:T(8,128)(2,1)S(1)}, u32[]{:S(2)}, u32[]{:S(2)}) collective-permute-start(bf16[12,64,512]{2,1,0:T(8,128)(2,1)S(1)} %get-tuple-element.8.e0), channel_id=1, source_target_pairs={{0,64},{32,96},{64,0},{96,32},{1,65},{33,97},{65,1},{97,33},{2,66}... | collective-permute-start | bytes 2359304 | tf_op jit(solution)/shard_map/ppermute | solution.py:306
  2.3 1.2 %collective-permute-start.1 = (bf16[32,768]{1,0:T(8,128)(2,1)S(1)}, bf16[32,768]{1,0:T(8,128)(2,1)S(1)}, u32[]{:S(2)}, u32[]{:S(2)}) collective-permute-start(bf16[32,768]{1,0:T(8,128)(2,1)S(1)} %get-tuple-element.10), channel_id=1, source_target_pairs={{0,32},{32,0},{64,96},{96,64},{1,33},{33,1},{65,97},{97,65},{2,34}... | collective-permute-start | bytes 147464 | tf_op jit(solution)/shard_map/ppermute | solution.py:306
  3.6 17.7 %collective-permute-start.3 = (bf16[64,768]{1,0:T(8,128)(2,1)S(1)}, bf16[64,768]{1,0:T(8,128)(2,1)S(1)}, u32[]{:S(2)}, u32[]{:S(2)}) collective-permute-start(bf16[64,768]{1,0:T(8,128)(2,1)S(1)} %pad_maximum_fusion), channel_id=1, source_target_pairs={{0,24},{1,25},{2,26},{3,27},{4,28},{5,29},{6,30},{7,31},{8,16},{9,... | collective-permute-start | bytes 294920 | tf_op jit(solution)/shard_map/ppermute | solution.py:311
  7.8 13.5 %collective-permute-start.4 = (bf16[64,768]{1,0:T(8,128)(2,1)S(1)}, bf16[64,768]{1,0:T(8,128)(2,1)S(1)}, u32[]{:S(2)}, u32[]{:S(2)}) collective-permute-start(bf16[64,768]{1,0:T(8,128)(2,1)S(1)} %pad_maximum_fusion), channel_id=1, source_target_pairs={{0,16},{1,17},{2,18},{3,19},{4,20},{5,21},{6,22},{7,23},{8,24},{9,... | collective-permute-start | bytes 294920 | tf_op jit(solution)/shard_map/ppermute | solution.py:311
  7.8 13.5 %collective-permute-start.2 = (bf16[64,768]{1,0:T(8,128)(2,1)S(1)}, bf16[64,768]{1,0:T(8,128)(2,1)S(1)}, u32[]{:S(2)}, u32[]{:S(2)}) collective-permute-start(bf16[64,768]{1,0:T(8,128)(2,1)S(1)} %pad_maximum_fusion), channel_id=1, source_target_pairs={{0,8},{1,9},{2,10},{3,11},{4,12},{5,13},{6,14},{7,15},{8,0},{9,1},... | collective-permute-start | bytes 294920 | tf_op jit(solution)/shard_map/ppermute | solution.py:311
  8.8 26.7 %collective-permute-start = (bf16[12,64,512]{2,1,0:T(8,128)(2,1)S(1)}, bf16[12,64,512]{2,1,0:T(8,128)(2,1)S(1)}, u32[]{:S(2)}, u32[]{:S(2)}) collective-permute-start(bf16[12,64,512]{2,1,0:T(8,128)(2,1)S(1)} %get-tuple-element.8.e0), channel_id=1, source_target_pairs={{0,32},{32,0},{64,96},{96,64},{1,33},{33,1},{65,97},{97,65},{2,34}... | collective-permute-start | bytes 2359304 | tf_op jit(solution)/shard_map/ppermute | solution.py:306
  21.3 16.9 %collective-permute-start.10 = (bf16[12,64,512]{2,1,0:T(8,128)(2,1)S(1)}, bf16[12,64,512]{2,1,0:T(8,128)(2,1)S(1)}, u32[]{:S(2)}, u32[]{:S(2)}) collective-permute-start(bf16[12,64,512]{2,1,0:T(8,128)(2,1)S(1)} %collective-permute-done.9.e0), channel_id=1, source_target_pairs={{0,32},{32,0},{64,96},{96,64},{1,33},{33,1},{65,97},{97,65},{2,34}... | collective-permute-start | bytes 2359304 | tf_op jit(solution)/shard_map/ppermute | solution.py:306
  21.4 6.8 %collective-permute-start.7 = (bf16[64,768]{1,0:T(8,128)(2,1)S(1)}, bf16[64,768]{1,0:T(8,128)(2,1)S(1)}, u32[]{:S(2)}, u32[]{:S(2)}) collective-permute-start(bf16[64,768]{1,0:T(8,128)(2,1)S(1)} %add_add_fusion.1), channel_id=1, source_target_pairs={{0,4},{1,5},{2,6},{3,7},{4,0},{5,1},{6,2},{7,3},{8,12},{9,13},{10,... | collective-permute-start | bytes 294920 | tf_op jit(solution)/shard_map/ppermute | solution.py:311
  24.5 6.1 %collective-permute-start.6 = (bf16[64,768]{1,0:T(8,128)(2,1)S(1)}, bf16[64,768]{1,0:T(8,128)(2,1)S(1)}, u32[]{:S(2)}, u32[]{:S(2)}) collective-permute-start(bf16[64,768]{1,0:T(8,128)(2,1)S(1)} %add_add_fusion.1), channel_id=1, source_target_pairs={{0,6},{1,7},{2,4},{3,5},{4,2},{5,3},{6,0},{7,1},{8,14},{9,15},{10,... | collective-permute-start | bytes 294920 | tf_op jit(solution)/shard_map/ppermute | solution.py:311
  25.6 5.0 %collective-permute-start.5 = (bf16[64,768]{1,0:T(8,128)(2,1)S(1)}, bf16[64,768]{1,0:T(8,128)(2,1)S(1)}, u32[]{:S(2)}, u32[]{:S(2)}) collective-permute-start(bf16[64,768]{1,0:T(8,128)(2,1)S(1)} %add_add_fusion.1), channel_id=1, source_target_pairs={{0,2},{1,3},{2,0},{3,1},{4,6},{5,7},{6,4},{7,5},{8,10},{9,11},{10,... | collective-permute-start | bytes 294920 | tf_op jit(solution)/shard_map/ppermute | solution.py:311
  30.6 5.9 %collective-permute-start.8 = (bf16[32,768]{1,0:T(8,128)(2,1)S(1)}, bf16[32,768]{1,0:T(8,128)(2,1)S(1)}, u32[]{:S(2)}, u32[]{:S(2)}) collective-permute-start(bf16[32,768]{1,0:T(8,128)(2,1)S(1)} %get-tuple-element.12.s0), channel_id=1, source_target_pairs={{0,1},{1,0},{2,3},{3,2},{4,5},{5,4},{6,7},{7,6},{8,9},{9,8},{10,11... | collective-permute-start | bytes 147464 | tf_op jit(solution)/shard_map/ppermute | solution.py:323
  33.0 5.9 %collective-permute-start.12 = (bf16[32,768]{1,0:T(8,128)(2,1)S(1)}, bf16[32,768]{1,0:T(8,128)(2,1)S(1)}, u32[]{:S(2)}, u32[]{:S(2)}) collective-permute-start(bf16[32,768]{1,0:T(8,128)(2,1)S(1)} %get-tuple-element.11), channel_id=1, source_target_pairs={{0,65},{1,64},{2,67},{3,66},{4,69},{5,68},{6,71},{7,70},{8,73},{9,... | collective-permute-start | bytes 147464 | tf_op jit(solution)/shard_map/ppermute | solution.py:323
  33.0 5.9 %collective-permute-start.11 = (bf16[32,768]{1,0:T(8,128)(2,1)S(1)}, bf16[32,768]{1,0:T(8,128)(2,1)S(1)}, u32[]{:S(2)}, u32[]{:S(2)}) collective-permute-start(bf16[32,768]{1,0:T(8,128)(2,1)S(1)} %get-tuple-element.11), channel_id=1, source_target_pairs={{0,64},{1,65},{2,66},{3,67},{4,68},{5,69},{6,70},{7,71},{8,72},{9,... | collective-permute-start | bytes 147464 | tf_op jit(solution)/shard_map/ppermute | solution.py:323
  68.3 5.0 %collective-permute-start.15 = (f32[96,128]{1,0:T(8,128)S(1)}, f32[96,128]{1,0:T(8,128)S(1)}, u32[]{:S(2)}, u32[]{:S(2)}) collective-permute-start(f32[96,128]{1,0:T(8,128)S(1)} %convert_reduce_fusion), channel_id=1, source_target_pairs={{0,64},{1,0},{2,96},{3,32},{4,68},{5,4},{6,100},{7,36},{8,72},{9,8... | collective-permute-start | bytes 147464 | tf_op jit(solution)/shard_map/ppermute | solution.py:359
  68.6 7.2 %collective-permute-start.13 = (f32[96,128]{1,0:T(8,128)S(1)}, f32[96,128]{1,0:T(8,128)S(1)}, u32[]{:S(2)}, u32[]{:S(2)}) collective-permute-start(f32[96,128]{1,0:T(8,128)S(1)} %convert_reduce_fusion), channel_id=1, source_target_pairs={{0,0},{1,64},{2,32},{3,96},{4,4},{5,68},{6,36},{7,100},{8,8},{9,72... | collective-permute-start | bytes 147464 | tf_op jit(solution)/shard_map/ppermute | solution.py:359
  73.3 2.6 %collective-permute-start.16 = (f32[96,128]{1,0:T(8,128)S(1)}, f32[96,128]{1,0:T(8,128)S(1)}, u32[]{:S(2)}, u32[]{:S(2)}) collective-permute-start(f32[96,128]{1,0:T(8,128)S(1)} %collective-permute-done.15.y2), channel_id=1, source_target_pairs={{0,32},{32,0},{64,96},{96,64},{1,33},{33,1},{65,97},{97,65},{2,34}... | collective-permute-start | bytes 147464 | tf_op jit(solution)/shard_map/ppermute | solution.py:306
  75.8 1.2 %collective-permute-start.14 = (f32[96,128]{1,0:T(8,128)S(1)}, f32[96,128]{1,0:T(8,128)S(1)}, u32[]{:S(2)}, u32[]{:S(2)}) collective-permute-start(f32[96,128]{1,0:T(8,128)S(1)} %collective-permute-done.13.y0), channel_id=1, source_target_pairs={{0,32},{32,0},{64,96},{96,64},{1,33},{33,1},{65,97},{97,65},{2,34}... | collective-permute-start | bytes 147464 | tf_op jit(solution)/shard_map/ppermute | solution.py:306

commit v9 on v8

--- a/solution.py
+++ b/solution.py
@@ -14,8 +14,9 @@
 KL = 16
 PART = 2 * SL
 HALF = EP * SB // 3
-BLOCKS = ((0, 0), (0, 1), (0, 2), (1, 1), (1, 2), (2, 2))
-QUARTER = len(BLOCKS) * HALF // GR
+UPPER = ((0, 1), (0, 2), (1, 2))
+TILES = len(UPPER) + 2
+QUARTER = TILES * HALF // GR
 VOX = 16384
 F32 = jnp.float32
 BF16 = jnp.bfloat16
@@ -213,32 +214,38 @@
                     tile = jnp.concatenate([tiles[0][e], tiles[1][e]], axis=0).astype(BF16)
                     z_ref[slot, h, at : at + SB, c : c + 128] = tile
 
+    down, across = iota((HALF, HALF), 0), iota((HALF, HALF), 1)
+
     def products(q, slot):
-        for h in range(2):
-            product = dot_nt(z_ref[slot, h], z_ref[slot, h])
-            for n, (low, high) in enumerate(BLOCKS):
-                line, column = ((m - h) % 3 * HALF for m in (low, high))
-                tile = product[line : line + HALF, column : column + HALF]
-                column = side(h, high) * HALF
-                for first in range(0, HALF, HALF // 2):
-                    r, line = divmod(n * HALF + first, QUARTER)
-                    to = (q // 2) * 8 + (slot * 2 + r % 2) * 2 + r // 2
-                    part = tile[first : first + HALF // 2]
-                    o_ref[to, line : line + HALF // 2, column : column + HALF] = part
-
-    def step(t, carry):
-        products(2 * t, 0)
-        scores(2 * t + 1, 1)
-        products(2 * t + 1, 1)
-        scores(2 * t + 2, 0)
-        return carry
-
-    last = KL // 2 - 1
+        whole = [dot_nt(z_ref[slot, h], z_ref[slot, h]) for h in range(2)]
+
+        def block(h, low, high):
+            line, column = ((m - h) % 3 * HALF for m in (low, high))
+            return whole[h][line : line + HALF, column : column + HALF]
+
+        tiles = []
+        for low, high in UPPER:
+            first = side(0, high)
+            tiles.append([block(first, low, high), block(1 - first, low, high)])
+        mixed, rest = [], jnp.zeros((HALF, HALF), F32)
+        for m in range(3):
+            second = block(1, m, m)
+            mixed.append(jnp.where(across <= down, block(0, m, m), second))
+            ends = jnp.sum(jnp.where(across == down, second, 0.0), axis=1, keepdims=True)
+            rest = jnp.where(across == m, ends, rest)
+        tiles += [mixed[0:2], [mixed[2], rest]]
+        for n, tile in enumerate(tiles):
+            tile = jnp.concatenate(tile, axis=1)
+            for first in range(0, HALF, SB):
+                r, line = divmod(n * HALF + first, QUARTER)
+                to = (q // 2) * 8 + (slot * 2 + r % 2) * 2 + r // 2
+                o_ref[to, line : line + SB, :] = tile[first : first + SB]
+
     scores(0, 0)
-    lax.fori_loop(0, last // 2, step, 0)
-    products(last - 1, 0)
-    scores(last, 1)
-    products(last, 1)
+    for q in range(1, KL // 2):
+        products(q - 1, (q - 1) % 2)
+        scores(q, q % 2)
+    products(KL // 2 - 1, 1)
 
 
 def partial_kernels(fa, fb, devices):
@@ -258,18 +265,29 @@
     j = lax.axis_index("subj")
     for r, y in enumerate((y0, y1, y2, y3)):
         b_ref[pl.ds(pl.multiple_of((j ^ r) * QUARTER, QUARTER), QUARTER), :] = y[...]
-    for n, (low, high) in enumerate(BLOCKS):
+
+    def put(h, low, high, block):
+        at = (high % 2) * HALF
+        k_ref[h, high // 2, low * HALF : (low + 1) * HALF, at : at + HALF] = block
+
+    down, across = iota((HALF, HALF), 0), iota((HALF, HALF), 1)
+    for n in range(TILES):
         tile = b_ref[n * HALF : (n + 1) * HALF, :]
         mirrored = tile.T
-        for h in range(2):
-            place = side(h, high) * HALF
-            block = tile[:, place : place + HALF]
-            at = (high % 2) * HALF
-            k_ref[h, high // 2, low * HALF : (low + 1) * HALF, at : at + HALF] = block
-            if low != high:
-                block = mirrored[place : place + HALF]
-                at = (low % 2) * HALF
-                k_ref[h, low // 2, high * HALF : (high + 1) * HALF, at : at + HALF] = block
+        if n < len(UPPER):
+            low, high = UPPER[n]
+            for h in range(2):
+                place = side(h, high) * HALF
+                put(h, low, high, tile[:, place : place + HALF])
+                put(h, high, low, mirrored[place : place + HALF])
+            continue
+        for m in range((n - len(UPPER)) * 2, min((n - len(UPPER)) * 2 + 2, 3)):
+            place = m % 2 * HALF
+            mixed, flipped = tile[:, place : place + HALF], mirrored[place : place + HALF]
+            ends = b_ref[(TILES - 1) * HALF : TILES * HALF, HALF + m : HALF + m + 1]
+            put(0, m, m, jnp.where(across <= down, mixed, flipped))
+            second = jnp.where(across > down, mixed, flipped)
+            put(1, m, m, jnp.where(across == down, ends, second))
     cols = EP * SB
     turn = lax.axis_index("vox") % 2
     source = iota((cols, cols), 0)
@@ -294,7 +312,7 @@
         in_specs=[pl.BlockSpec(memory_space=pltpu.VMEM)] * GR,
         out_specs=pl.BlockSpec(memory_space=pltpu.VMEM),
         scratch_shapes=[
-            pltpu.VMEM((len(BLOCKS) * HALF, 2 * HALF), F32),
+            pltpu.VMEM((TILES * HALF, 2 * HALF), F32),
             pltpu.VMEM((2, 2, EP * SB, 2 * HALF), F32),
         ],
         compiler_params=pltpu.CompilerParams(vmem_limit_bytes=4 << 20),

time: 79 us -> 77.8 us (0.985)
  blocking collectives: 24.5 us -> 23.1 us
    all_to_all x1, blocking collectives: 24.5 us -> 23.1 us  [body(): lax.all_to_all(tiles.astype(LINK), 'vox', split_axis=0, concat_axis=0, ti...]
where the time goes in v9:
time: 77.8 us; the launch traced here: 76.8 us
  blocking collectives  23.1 us (30%)
  waiting for transfers between devices  22.6 us (29%)
  starting transfers between devices  19.7 us (25%)
  Pallas kernels  11 us (14%)
    all_to_all x1, blocking collectives, body(): lax.all_to_all(tiles.astype(LINK), 'vox', split_axis=0, concat_axis=0, ti...  23.1 us
    ppermute x6, waiting for transfers between devices, swapped(): return lax.ppermute(x, 'subj', [(n, n ^ r) for n in range(GR)])  15 us
    ppermute x6, starting transfers between devices, summed(): lax.ppermute(x, 'vox', [(n, n ^ step * stride) for n in range(devices)])  9.41 us
    ppermute x6, waiting for transfers between devices, summed(): lax.ppermute(x, 'vox', [(n, n ^ step * stride) for n in range(devices)])  5 us
    ppermute x2, starting transfers between devices, turned(): return lax.ppermute(tile, ('subj', 'vox'), moves)  4.97 us
    ppermute x3, starting transfers between devices, along_y(): return lax.ppermute(x, ('subj', 'vox'), moves)  4.78 us
    pallas_call x2, Pallas kernels, fishers(): pl.pallas_call(fisher_kernel, out_shape=pltpu.VMEM((EP, KL * PART, width)...  3.27 us
    pallas_call x1, Pallas kernels, partial_kernels(): pl.pallas_call(kernel_kernel, out_shape=pltpu.VMEM((devices, QUARTER, 2 *...  3.17 us
  transfers between devices with their start and end apart: 17, of which 7 were waited for; matrix products, arithmetic and copies ran while one was open for 0% of the time, Pallas kernels for 4%

profile of v9, /device:TPU:8, one launch (start us, length us, event | category | flops | bytes accessed | tf_op | source)
XLA Modules:
  0.0 76.8 jit_solution(18411700810710544997)
XLA Ops:
  0.0 1.9 %windows.1 = (bf16[12,64,512]{2,1,0:T(8,128)(2,1)S(1)}, bf16[32,768]{1,0:T(8,128)(2,1)S(1)}, bf16[32,768]{1,0:T(8,128)(2,1)S(1)}) custom-call(s32[16,12]{1,0:T(8,128)} %off_ref.1, s32[64]{0:T(128)} %sel_ref.1, bf16[4,256,512]{2,1,0:T(8,128)(2,1)} %series_ref.1), custom_call_target="tpu_custom_call" | custom-call | tf_op jit(solution)/shard_map/windows/pallas_call | solution.py:95
  1.9 0.4 collective-permute-start.9
  2.3 1.2 %collective-permute-done.1 = bf16[32,768]{1,0:T(8,128)(2,1)S(1)} collective-permute-done((bf16[32,768]{1,0:T(8,128)(2,1)S(1)}, bf16[32,768]{1,0:T(8,128)(2,1)S(1)}, u32[]{:S(2)}, u32[]{:S(2)}) %collective-permute-start.1) | collective-permute-done | bytes 49184 | tf_op jit(solution)/shard_map/ppermute | solution.py:324
  3.6 4.2 %collective-permute-start.3 = (bf16[64,768]{1,0:T(8,128)(2,1)S(1)}, bf16[64,768]{1,0:T(8,128)(2,1)S(1)}, u32[]{:S(2)}, u32[]{:S(2)}) collective-permute-start(bf16[64,768]{1,0:T(8,128)(2,1)S(1)} %pad_maximum_fusion), channel_id=1, source_target_pairs={{0,24},{1,25},{2,26},{3,27},{4,28},{5,29},{6,30},{7,31},{8,16},{9,... | collective-permute-start | bytes 294920 | tf_op jit(solution)/shard_map/ppermute | solution.py:329
  7.8 0.9 %collective-permute-start.2 = (bf16[64,768]{1,0:T(8,128)(2,1)S(1)}, bf16[64,768]{1,0:T(8,128)(2,1)S(1)}, u32[]{:S(2)}, u32[]{:S(2)}) collective-permute-start(bf16[64,768]{1,0:T(8,128)(2,1)S(1)} %pad_maximum_fusion), channel_id=1, source_target_pairs={{0,8},{1,9},{2,10},{3,11},{4,12},{5,13},{6,14},{7,15},{8,0},{9,1},... | collective-permute-start | bytes 294920 | tf_op jit(solution)/shard_map/ppermute | solution.py:329
  8.8 0.0 collective-permute-start
  8.8 12.5 %collective-permute-done.9.e0 = bf16[12,64,512]{2,1,0:T(8,128)(2,1)S(1)} collective-permute-done((bf16[12,64,512]{2,1,0:T(8,128)(2,1)S(1)}, bf16[12,64,512]{2,1,0:T(8,128)(2,1)S(1)}, u32[]{:S(2)}, u32[]{:S(2)}) %collective-permute-start.9) | collective-permute-done | bytes 786464 | tf_op jit(solution)/shard_map/ppermute | solution.py:324
  21.3 0.0 collective-permute-start.10
  21.3 0.0 collective-permute-done.3
  21.3 0.1 add_add_fusion.1
  21.4 3.1 %collective-permute-start.7 = (bf16[64,768]{1,0:T(8,128)(2,1)S(1)}, bf16[64,768]{1,0:T(8,128)(2,1)S(1)}, u32[]{:S(2)}, u32[]{:S(2)}) collective-permute-start(bf16[64,768]{1,0:T(8,128)(2,1)S(1)} %add_add_fusion.1), channel_id=1, source_target_pairs={{0,4},{1,5},{2,6},{3,7},{4,0},{5,1},{6,2},{7,3},{8,12},{9,13},{10,... | collective-permute-start | bytes 294920 | tf_op jit(solution)/shard_map/ppermute | solution.py:329
  24.5 1.1 %collective-permute-start.6 = (bf16[64,768]{1,0:T(8,128)(2,1)S(1)}, bf16[64,768]{1,0:T(8,128)(2,1)S(1)}, u32[]{:S(2)}, u32[]{:S(2)}) collective-permute-start(bf16[64,768]{1,0:T(8,128)(2,1)S(1)} %add_add_fusion.1), channel_id=1, source_target_pairs={{0,6},{1,7},{2,4},{3,5},{4,2},{5,3},{6,0},{7,1},{8,14},{9,15},{10,... | collective-permute-start | bytes 294920 | tf_op jit(solution)/shard_map/ppermute | solution.py:329
  25.6 2.5 %collective-permute-done.7 = bf16[64,768]{1,0:T(8,128)(2,1)S(1)} collective-permute-done((bf16[64,768]{1,0:T(8,128)(2,1)S(1)}, bf16[64,768]{1,0:T(8,128)(2,1)S(1)}, u32[]{:S(2)}, u32[]{:S(2)}) %collective-permute-start.7) | collective-permute-done | bytes 98336 | tf_op jit(solution)/shard_map/ppermute | solution.py:329
  28.1 2.4 %collective-permute-done.6 = bf16[64,768]{1,0:T(8,128)(2,1)S(1)} collective-permute-done((bf16[64,768]{1,0:T(8,128)(2,1)S(1)}, bf16[64,768]{1,0:T(8,128)(2,1)S(1)}, u32[]{:S(2)}, u32[]{:S(2)}) %collective-permute-start.6) | collective-permute-done | bytes 98336 | tf_op jit(solution)/shard_map/ppermute | solution.py:329
  30.6 2.4 %collective-permute-start.8 = (bf16[32,768]{1,0:T(8,128)(2,1)S(1)}, bf16[32,768]{1,0:T(8,128)(2,1)S(1)}, u32[]{:S(2)}, u32[]{:S(2)}) collective-permute-start(bf16[32,768]{1,0:T(8,128)(2,1)S(1)} %get-tuple-element.12.s0), channel_id=1, source_target_pairs={{0,1},{1,0},{2,3},{3,2},{4,5},{5,4},{6,7},{7,6},{8,9},{9,8},{10,11... | collective-permute-start | bytes 147464 | tf_op jit(solution)/shard_map/ppermute | solution.py:341
  33.0 2.4 %collective-permute-start.11 = (bf16[32,768]{1,0:T(8,128)(2,1)S(1)}, bf16[32,768]{1,0:T(8,128)(2,1)S(1)}, u32[]{:S(2)}, u32[]{:S(2)}) collective-permute-start(bf16[32,768]{1,0:T(8,128)(2,1)S(1)} %get-tuple-element.11), channel_id=1, source_target_pairs={{0,64},{1,65},{2,66},{3,67},{4,68},{5,69},{6,70},{7,71},{8,72},{9,... | collective-permute-start | bytes 147464 | tf_op jit(solution)/shard_map/ppermute | solution.py:341
  35.4 0.8 norms.2.n_ref
  36.2 0.4 collective-permute-done.8.s1
  36.5 1.6 %fishers.2.fa = f32[12,128,512]{2,1,0:T(8,128)S(1)} custom-call(bf16[12,64,512]{2,1,0:T(8,128)(2,1)S(1)} %get-tuple-element.8.e0, bf16[12,64,512]{2,1,0:T(8,128)(2,1)S(1)} %collective-permute-done.e1, bf16[32,768]{1,0:T(8,128)(2,1)S(1)} %get-tuple-element.12.s0, bf16[32,768]{1,0:T(8,128)(2,1)S(1)} %collective-permute-done.8.s1, f32[12,8,512]{2,1,0:T(8,128)S(1)} %norms.2.n_ref), custom_call_target="tpu_custom_call" | custom-call | tf_op jit(solution)/shard_map/fishers/pallas_call | solution.py:184
  38.2 0.7 norms.3.n_ref
  39.0 0.0 collective-permute-done.11.s0
  39.0 1.6 %fishers.3.fb = f32[12,128,512]{2,1,0:T(8,128)S(1)} custom-call(bf16[12,64,512]{2,1,0:T(8,128)(2,1)S(1)} %collective-permute-done.9.e0, bf16[12,64,512]{2,1,0:T(8,128)(2,1)S(1)} %collective-permute-done.10.e1, bf16[32,768]{1,0:T(8,128)(2,1)S(1)} %collective-permute-done.11.s0, bf16[32,768]{1,0:T(8,128)(2,1)S(1)} %collective-permute-done.12.s1, ...), custom_call_target="tpu_custom_call" | custom-call | tf_op jit(solution)/shard_map/fishers/pallas_call | solution.py:184
  40.6 3.2 %partial_kernels.1 = f32[32,80,128]{2,1,0:T(8,128)S(1)} custom-call(f32[12,128,512]{2,1,0:T(8,128)S(1)} %fishers.2.fa, f32[12,128,512]{2,1,0:T(8,128)S(1)} %fishers.3.fb), custom_call_target="tpu_custom_call" | custom-call | tf_op jit(solution)/shard_map/partial_kernels/pallas_call | solution.py:253
  43.8 0.1 convert_element_type.6
  43.9 23.1 %all_to_all.5 = f16[32,80,128]{2,1,0:T(8,128)(2,1)S(1)} all-to-all(f16[32,80,128]{2,1,0:T(8,128)(2,1)S(1)} %convert_element_type.6), channel_id=1, replica_groups=mesh['subj'=4,'vox'=32] {'vox'}, dimensions={0} | all-to-all | bytes 1310720 | tf_op jit(solution)/shard_map/all_to_all | solution.py:363
  66.9 0.1 convert_reduce_fusion
  67.0 0.3 collective-permute-start.15
  67.4 4.6 %collective-permute-start.13 = (f32[80,128]{1,0:T(8,128)S(1)}, f32[80,128]{1,0:T(8,128)S(1)}, u32[]{:S(2)}, u32[]{:S(2)}) collective-permute-start(f32[80,128]{1,0:T(8,128)S(1)} %convert_reduce_fusion), channel_id=1, source_target_pairs={{0,0},{1,64},{2,32},{3,96},{4,4},{5,68},{6,36},{7,100},{8,8},{9,72... | collective-permute-start | bytes 122888 | tf_op jit(solution)/shard_map/ppermute | solution.py:377
  72.0 0.1 collective-permute-start.16
  72.1 2.3 %collective-permute-done.13.y0 = f32[80,128]{1,0:T(8,128)S(1)} collective-permute-done((f32[80,128]{1,0:T(8,128)S(1)}, f32[80,128]{1,0:T(8,128)S(1)}, u32[]{:S(2)}, u32[]{:S(2)}) %collective-permute-start.13) | collective-permute-done | bytes 40992 | tf_op jit(solution)/shard_map/ppermute | solution.py:377
  74.4 1.2 %collective-permute-done.14.y1 = f32[80,128]{1,0:T(8,128)S(1)} collective-permute-done((f32[80,128]{1,0:T(8,128)S(1)}, f32[80,128]{1,0:T(8,128)S(1)}, u32[]{:S(2)}, u32[]{:S(2)}) %collective-permute-start.14) | collective-permute-done | bytes 40992 | tf_op jit(solution)/shard_map/ppermute | solution.py:324
  75.6 1.2 %in_order.1 = f32[2,48,192]{2,1,0:T(8,128)} custom-call(f32[80,128]{1,0:T(8,128)S(1)} %collective-permute-done.13.y0, f32[80,128]{1,0:T(8,128)S(1)} %collective-permute-done.14.y1, f32[80,128]{1,0:T(8,128)S(1)} %collective-permute-done.15.y2, f32[80,128]{1,0:T(8,128)S(1)} %collective-permute-done.16.y3), custom_call_target="tpu_custom_call" | custom-call | tf_op jit(solution)/shard_map/in_order/pallas_call | solution.py:309
  (18 shorter events, 0.1 us)
Async XLA Ops:
  1.9 19.4 %collective-permute-start.9 = (bf16[12,64,512]{2,1,0:T(8,128)(2,1)S(1)}, bf16[12,64,512]{2,1,0:T(8,128)(2,1)S(1)}, u32[]{:S(2)}, u32[]{:S(2)}) collective-permute-start(bf16[12,64,512]{2,1,0:T(8,128)(2,1)S(1)} %get-tuple-element.8.e0), channel_id=1, source_target_pairs={{0,64},{32,96},{64,0},{96,32},{1,65},{33,97},{65,1},{97,33},{2,66}... | collective-permute-start | bytes 2359304 | tf_op jit(solution)/shard_map/ppermute | solution.py:324
  2.3 1.2 %collective-permute-start.1 = (bf16[32,768]{1,0:T(8,128)(2,1)S(1)}, bf16[32,768]{1,0:T(8,128)(2,1)S(1)}, u32[]{:S(2)}, u32[]{:S(2)}) collective-permute-start(bf16[32,768]{1,0:T(8,128)(2,1)S(1)} %get-tuple-element.10), channel_id=1, source_target_pairs={{0,32},{32,0},{64,96},{96,64},{1,33},{33,1},{65,97},{97,65},{2,34}... | collective-permute-start | bytes 147464 | tf_op jit(solution)/shard_map/ppermute | solution.py:324
  3.6 17.7 %collective-permute-start.3 = (bf16[64,768]{1,0:T(8,128)(2,1)S(1)}, bf16[64,768]{1,0:T(8,128)(2,1)S(1)}, u32[]{:S(2)}, u32[]{:S(2)}) collective-permute-start(bf16[64,768]{1,0:T(8,128)(2,1)S(1)} %pad_maximum_fusion), channel_id=1, source_target_pairs={{0,24},{1,25},{2,26},{3,27},{4,28},{5,29},{6,30},{7,31},{8,16},{9,... | collective-permute-start | bytes 294920 | tf_op jit(solution)/shard_map/ppermute | solution.py:329
  7.8 13.5 %collective-permute-start.4 = (bf16[64,768]{1,0:T(8,128)(2,1)S(1)}, bf16[64,768]{1,0:T(8,128)(2,1)S(1)}, u32[]{:S(2)}, u32[]{:S(2)}) collective-permute-start(bf16[64,768]{1,0:T(8,128)(2,1)S(1)} %pad_maximum_fusion), channel_id=1, source_target_pairs={{0,16},{1,17},{2,18},{3,19},{4,20},{5,21},{6,22},{7,23},{8,24},{9,... | collective-permute-start | bytes 294920 | tf_op jit(solution)/shard_map/ppermute | solution.py:329
  7.8 13.5 %collective-permute-start.2 = (bf16[64,768]{1,0:T(8,128)(2,1)S(1)}, bf16[64,768]{1,0:T(8,128)(2,1)S(1)}, u32[]{:S(2)}, u32[]{:S(2)}) collective-permute-start(bf16[64,768]{1,0:T(8,128)(2,1)S(1)} %pad_maximum_fusion), channel_id=1, source_target_pairs={{0,8},{1,9},{2,10},{3,11},{4,12},{5,13},{6,14},{7,15},{8,0},{9,1},... | collective-permute-start | bytes 294920 | tf_op jit(solution)/shard_map/ppermute | solution.py:329
  8.8 26.7 %collective-permute-start = (bf16[12,64,512]{2,1,0:T(8,128)(2,1)S(1)}, bf16[12,64,512]{2,1,0:T(8,128)(2,1)S(1)}, u32[]{:S(2)}, u32[]{:S(2)}) collective-permute-start(bf16[12,64,512]{2,1,0:T(8,128)(2,1)S(1)} %get-tuple-element.8.e0), channel_id=1, source_target_pairs={{0,32},{32,0},{64,96},{96,64},{1,33},{33,1},{65,97},{97,65},{2,34}... | collective-permute-start | bytes 2359304 | tf_op jit(solution)/shard_map/ppermute | solution.py:324
  21.3 16.9 %collective-permute-start.10 = (bf16[12,64,512]{2,1,0:T(8,128)(2,1)S(1)}, bf16[12,64,512]{2,1,0:T(8,128)(2,1)S(1)}, u32[]{:S(2)}, u32[]{:S(2)}) collective-permute-start(bf16[12,64,512]{2,1,0:T(8,128)(2,1)S(1)} %collective-permute-done.9.e0), channel_id=1, source_target_pairs={{0,32},{32,0},{64,96},{96,64},{1,33},{33,1},{65,97},{97,65},{2,34}... | collective-permute-start | bytes 2359304 | tf_op jit(solution)/shard_map/ppermute | solution.py:324
  21.4 6.8 %collective-permute-start.7 = (bf16[64,768]{1,0:T(8,128)(2,1)S(1)}, bf16[64,768]{1,0:T(8,128)(2,1)S(1)}, u32[]{:S(2)}, u32[]{:S(2)}) collective-permute-start(bf16[64,768]{1,0:T(8,128)(2,1)S(1)} %add_add_fusion.1), channel_id=1, source_target_pairs={{0,4},{1,5},{2,6},{3,7},{4,0},{5,1},{6,2},{7,3},{8,12},{9,13},{10,... | collective-permute-start | bytes 294920 | tf_op jit(solution)/shard_map/ppermute | solution.py:329
  24.5 6.1 %collective-permute-start.6 = (bf16[64,768]{1,0:T(8,128)(2,1)S(1)}, bf16[64,768]{1,0:T(8,128)(2,1)S(1)}, u32[]{:S(2)}, u32[]{:S(2)}) collective-permute-start(bf16[64,768]{1,0:T(8,128)(2,1)S(1)} %add_add_fusion.1), channel_id=1, source_target_pairs={{0,6},{1,7},{2,4},{3,5},{4,2},{5,3},{6,0},{7,1},{8,14},{9,15},{10,... | collective-permute-start | bytes 294920 | tf_op jit(solution)/shard_map/ppermute | solution.py:329
  25.6 5.0 %collective-permute-start.5 = (bf16[64,768]{1,0:T(8,128)(2,1)S(1)}, bf16[64,768]{1,0:T(8,128)(2,1)S(1)}, u32[]{:S(2)}, u32[]{:S(2)}) collective-permute-start(bf16[64,768]{1,0:T(8,128)(2,1)S(1)} %add_add_fusion.1), channel_id=1, source_target_pairs={{0,2},{1,3},{2,0},{3,1},{4,6},{5,7},{6,4},{7,5},{8,10},{9,11},{10,... | collective-permute-start | bytes 294920 | tf_op jit(solution)/shard_map/ppermute | solution.py:329
  30.6 5.9 %collective-permute-start.8 = (bf16[32,768]{1,0:T(8,128)(2,1)S(1)}, bf16[32,768]{1,0:T(8,128)(2,1)S(1)}, u32[]{:S(2)}, u32[]{:S(2)}) collective-permute-start(bf16[32,768]{1,0:T(8,128)(2,1)S(1)} %get-tuple-element.12.s0), channel_id=1, source_target_pairs={{0,1},{1,0},{2,3},{3,2},{4,5},{5,4},{6,7},{7,6},{8,9},{9,8},{10,11... | collective-permute-start | bytes 147464 | tf_op jit(solution)/shard_map/ppermute | solution.py:341
  33.0 5.9 %collective-permute-start.12 = (bf16[32,768]{1,0:T(8,128)(2,1)S(1)}, bf16[32,768]{1,0:T(8,128)(2,1)S(1)}, u32[]{:S(2)}, u32[]{:S(2)}) collective-permute-start(bf16[32,768]{1,0:T(8,128)(2,1)S(1)} %get-tuple-element.11), channel_id=1, source_target_pairs={{0,65},{1,64},{2,67},{3,66},{4,69},{5,68},{6,71},{7,70},{8,73},{9,... | collective-permute-start | bytes 147464 | tf_op jit(solution)/shard_map/ppermute | solution.py:341
  33.0 5.9 %collective-permute-start.11 = (bf16[32,768]{1,0:T(8,128)(2,1)S(1)}, bf16[32,768]{1,0:T(8,128)(2,1)S(1)}, u32[]{:S(2)}, u32[]{:S(2)}) collective-permute-start(bf16[32,768]{1,0:T(8,128)(2,1)S(1)} %get-tuple-element.11), channel_id=1, source_target_pairs={{0,64},{1,65},{2,66},{3,67},{4,68},{5,69},{6,70},{7,71},{8,72},{9,... | collective-permute-start | bytes 147464 | tf_op jit(solution)/shard_map/ppermute | solution.py:341
  67.0 5.0 %collective-permute-start.15 = (f32[80,128]{1,0:T(8,128)S(1)}, f32[80,128]{1,0:T(8,128)S(1)}, u32[]{:S(2)}, u32[]{:S(2)}) collective-permute-start(f32[80,128]{1,0:T(8,128)S(1)} %convert_reduce_fusion), channel_id=1, source_target_pairs={{0,64},{1,0},{2,96},{3,32},{4,68},{5,4},{6,100},{7,36},{8,72},{9,8... | collective-permute-start | bytes 122888 | tf_op jit(solution)/shard_map/ppermute | solution.py:377
  67.4 7.0 %collective-permute-start.13 = (f32[80,128]{1,0:T(8,128)S(1)}, f32[80,128]{1,0:T(8,128)S(1)}, u32[]{:S(2)}, u32[]{:S(2)}) collective-permute-start(f32[80,128]{1,0:T(8,128)S(1)} %convert_reduce_fusion), channel_id=1, source_target_pairs={{0,0},{1,64},{2,32},{3,96},{4,4},{5,68},{6,36},{7,100},{8,8},{9,72... | collective-permute-start | bytes 122888 | tf_op jit(solution)/shard_map/ppermute | solution.py:377
  72.0 2.4 %collective-permute-start.16 = (f32[80,128]{1,0:T(8,128)S(1)}, f32[80,128]{1,0:T(8,128)S(1)}, u32[]{:S(2)}, u32[]{:S(2)}) collective-permute-start(f32[80,128]{1,0:T(8,128)S(1)} %collective-permute-done.15.y2), channel_id=1, source_target_pairs={{0,32},{32,0},{64,96},{96,64},{1,33},{33,1},{65,97},{97,65},{2,34}... | collective-permute-start | bytes 122888 | tf_op jit(solution)/shard_map/ppermute | solution.py:324
  74.4 1.2 %collective-permute-start.14 = (f32[80,128]{1,0:T(8,128)S(1)}, f32[80,128]{1,0:T(8,128)S(1)}, u32[]{:S(2)}, u32[]{:S(2)}) collective-permute-start(f32[80,128]{1,0:T(8,128)S(1)} %collective-permute-done.13.y0), channel_id=1, source_target_pairs={{0,32},{32,0},{64,96},{96,64},{1,33},{33,1},{65,97},{97,65},{2,34}... | collective-permute-start | bytes 122888 | tf_op jit(solution)/shard_map/ppermute | solution.py:324

commit v10 on v9

--- a/solution.py
+++ b/solution.py
@@ -36,6 +36,12 @@
 
 def small(mib):
     return pltpu.CompilerParams(vmem_limit_bytes=mib << 20)
+
+
+ORDER = (
+    31, 23, 30, 22, 10, 21, 7, 24, 17, 0, 15, 14, 1, 19, 5, 13,
+    20, 27, 8, 4, 18, 9, 26, 11, 12, 6, 29, 3, 16, 28, 25, 2,
+)
 
 
 def side(h, high):
@@ -239,7 +245,7 @@
             for first in range(0, HALF, SB):
                 r, line = divmod(n * HALF + first, QUARTER)
                 to = (q // 2) * 8 + (slot * 2 + r % 2) * 2 + r // 2
-                o_ref[to, line : line + SB, :] = tile[first : first + SB]
+                o_ref[ORDER.index(to), line : line + SB, :] = tile[first : first + SB]
 
     scores(0, 0)
     for q in range(1, KL // 2):
@@ -360,7 +366,9 @@
     fa = fishers(own, beside, mine, ours, first)
     fb = fishers(across, beyond, left, right, second)
     tiles = partial_kernels(fa, fb, devices)
-    tiles = lax.all_to_all(tiles.astype(LINK), "vox", split_axis=0, concat_axis=0, tiled=True)
+    tiles = lax.all_to_all(
+        tiles.astype(LINK), "vox", 0, 0, axis_index_groups=[list(ORDER)], tiled=True
+    )
     tile = jnp.sum(tiles.astype(F32), axis=0)
 
     def turned(chips):

time: 77.8 us -> 74.9 us (0.963)
  blocking collectives: 23.1 us -> 19 us
  waiting for transfers between devices: 22.6 us -> 23.5 us
    all_to_all x1, blocking collectives: 23.1 us -> 19 us  [body(): lax.all_to_all(tiles.astype(LINK), 'vox', 0, 0, axis_index_groups=[list(O...]
    ppermute x2, waiting for transfers between devices: 2.3 us -> 3.53 us  [turned(): return lax.ppermute(tile, ('subj', 'vox'), moves)]
    ppermute x6, starting transfers between devices: 0.51 us -> 1.5 us  [swapped(): return lax.ppermute(x, 'subj', [(n, n ^ r) for n in range(GR)])]
where the time goes in v10:
time: 74.9 us; the launch traced here: 74.1 us
  waiting for transfers between devices  23.5 us (31%)
  starting transfers between devices  20.2 us (27%)
  blocking collectives  19 us (25%)
  Pallas kernels  11 us (15%)
    all_to_all x1, blocking collectives, body(): lax.all_to_all(tiles.astype(LINK), 'vox', 0, 0, axis_index_groups=[list(O...  19 us
    ppermute x6, waiting for transfers between devices, swapped(): return lax.ppermute(x, 'subj', [(n, n ^ r) for n in range(GR)])  14.6 us
    ppermute x6, starting transfers between devices, summed(): lax.ppermute(x, 'vox', [(n, n ^ step * stride) for n in range(devices)])  9.41 us
    ppermute x6, waiting for transfers between devices, summed(): lax.ppermute(x, 'vox', [(n, n ^ step * stride) for n in range(devices)])  5 us
    ppermute x3, starting transfers between devices, along_y(): return lax.ppermute(x, ('subj', 'vox'), moves)  4.78 us
    ppermute x2, starting transfers between devices, turned(): return lax.ppermute(tile, ('subj', 'vox'), moves)  4.52 us
    ppermute x2, waiting for transfers between devices, turned(): return lax.ppermute(tile, ('subj', 'vox'), moves)  3.53 us
    pallas_call x2, Pallas kernels, fishers(): pl.pallas_call(fisher_kernel, out_shape=pltpu.VMEM((EP, KL * PART, width)...  3.27 us
  transfers between devices with their start and end apart: 17, of which 7 were waited for; matrix products, arithmetic and copies ran while one was open for 0% of the time, Pallas kernels for 4%

profile of v10, /device:TPU:8, one launch (start us, length us, event | category | flops | bytes accessed | tf_op | source)
XLA Modules:
  0.0 74.1 jit_solution(6695511613681707052)
XLA Ops:
  0.0 1.9 %windows.1 = (bf16[12,64,512]{2,1,0:T(8,128)(2,1)S(1)}, bf16[32,768]{1,0:T(8,128)(2,1)S(1)}, bf16[32,768]{1,0:T(8,128)(2,1)S(1)}) custom-call(s32[16,12]{1,0:T(8,128)} %off_ref.1, s32[64]{0:T(128)} %sel_ref.1, bf16[4,256,512]{2,1,0:T(8,128)(2,1)} %series_ref.1), custom_call_target="tpu_custom_call" | custom-call | tf_op jit(solution)/shard_map/windows/pallas_call | solution.py:101
  1.9 0.4 collective-permute-start.9
  2.3 1.2 %collective-permute-done.1 = bf16[32,768]{1,0:T(8,128)(2,1)S(1)} collective-permute-done((bf16[32,768]{1,0:T(8,128)(2,1)S(1)}, bf16[32,768]{1,0:T(8,128)(2,1)S(1)}, u32[]{:S(2)}, u32[]{:S(2)}) %collective-permute-start.1) | collective-permute-done | bytes 49184 | tf_op jit(solution)/shard_map/ppermute | solution.py:330
  3.6 4.2 %collective-permute-start.3 = (bf16[64,768]{1,0:T(8,128)(2,1)S(1)}, bf16[64,768]{1,0:T(8,128)(2,1)S(1)}, u32[]{:S(2)}, u32[]{:S(2)}) collective-permute-start(bf16[64,768]{1,0:T(8,128)(2,1)S(1)} %pad_maximum_fusion), channel_id=1, source_target_pairs={{0,24},{1,25},{2,26},{3,27},{4,28},{5,29},{6,30},{7,31},{8,16},{9,... | collective-permute-start | bytes 294920 | tf_op jit(solution)/shard_map/ppermute | solution.py:335
  7.8 0.9 %collective-permute-start.2 = (bf16[64,768]{1,0:T(8,128)(2,1)S(1)}, bf16[64,768]{1,0:T(8,128)(2,1)S(1)}, u32[]{:S(2)}, u32[]{:S(2)}) collective-permute-start(bf16[64,768]{1,0:T(8,128)(2,1)S(1)} %pad_maximum_fusion), channel_id=1, source_target_pairs={{0,8},{1,9},{2,10},{3,11},{4,12},{5,13},{6,14},{7,15},{8,0},{9,1},... | collective-permute-start | bytes 294920 | tf_op jit(solution)/shard_map/ppermute | solution.py:335
  8.8 0.0 collective-permute-start
  8.8 12.5 %collective-permute-done.9.e0 = bf16[12,64,512]{2,1,0:T(8,128)(2,1)S(1)} collective-permute-done((bf16[12,64,512]{2,1,0:T(8,128)(2,1)S(1)}, bf16[12,64,512]{2,1,0:T(8,128)(2,1)S(1)}, u32[]{:S(2)}, u32[]{:S(2)}) %collective-permute-start.9) | collective-permute-done | bytes 786464 | tf_op jit(solution)/shard_map/ppermute | solution.py:330
  21.3 0.0 collective-permute-start.10
  21.3 0.1 add_add_fusion.1
  21.4 3.1 %collective-permute-start.7 = (bf16[64,768]{1,0:T(8,128)(2,1)S(1)}, bf16[64,768]{1,0:T(8,128)(2,1)S(1)}, u32[]{:S(2)}, u32[]{:S(2)}) collective-permute-start(bf16[64,768]{1,0:T(8,128)(2,1)S(1)} %add_add_fusion.1), channel_id=1, source_target_pairs={{0,4},{1,5},{2,6},{3,7},{4,0},{5,1},{6,2},{7,3},{8,12},{9,13},{10,... | collective-permute-start | bytes 294920 | tf_op jit(solution)/shard_map/ppermute | solution.py:335
  24.5 1.1 %collective-permute-start.6 = (bf16[64,768]{1,0:T(8,128)(2,1)S(1)}, bf16[64,768]{1,0:T(8,128)(2,1)S(1)}, u32[]{:S(2)}, u32[]{:S(2)}) collective-permute-start(bf16[64,768]{1,0:T(8,128)(2,1)S(1)} %add_add_fusion.1), channel_id=1, source_target_pairs={{0,6},{1,7},{2,4},{3,5},{4,2},{5,3},{6,0},{7,1},{8,14},{9,15},{10,... | collective-permute-start | bytes 294920 | tf_op jit(solution)/shard_map/ppermute | solution.py:335
  25.6 2.5 %collective-permute-done.7 = bf16[64,768]{1,0:T(8,128)(2,1)S(1)} collective-permute-done((bf16[64,768]{1,0:T(8,128)(2,1)S(1)}, bf16[64,768]{1,0:T(8,128)(2,1)S(1)}, u32[]{:S(2)}, u32[]{:S(2)}) %collective-permute-start.7) | collective-permute-done | bytes 98336 | tf_op jit(solution)/shard_map/ppermute | solution.py:335
  28.1 2.4 %collective-permute-done.6 = bf16[64,768]{1,0:T(8,128)(2,1)S(1)} collective-permute-done((bf16[64,768]{1,0:T(8,128)(2,1)S(1)}, bf16[64,768]{1,0:T(8,128)(2,1)S(1)}, u32[]{:S(2)}, u32[]{:S(2)}) %collective-permute-start.6) | collective-permute-done | bytes 98336 | tf_op jit(solution)/shard_map/ppermute | solution.py:335
  30.6 2.4 %collective-permute-start.8 = (bf16[32,768]{1,0:T(8,128)(2,1)S(1)}, bf16[32,768]{1,0:T(8,128)(2,1)S(1)}, u32[]{:S(2)}, u32[]{:S(2)}) collective-permute-start(bf16[32,768]{1,0:T(8,128)(2,1)S(1)} %get-tuple-element.12.s0), channel_id=1, source_target_pairs={{0,1},{1,0},{2,3},{3,2},{4,5},{5,4},{6,7},{7,6},{8,9},{9,8},{10,11... | collective-permute-start | bytes 147464 | tf_op jit(solution)/shard_map/ppermute | solution.py:347
  33.0 2.4 %collective-permute-start.11 = (bf16[32,768]{1,0:T(8,128)(2,1)S(1)}, bf16[32,768]{1,0:T(8,128)(2,1)S(1)}, u32[]{:S(2)}, u32[]{:S(2)}) collective-permute-start(bf16[32,768]{1,0:T(8,128)(2,1)S(1)} %get-tuple-element.11), channel_id=1, source_target_pairs={{0,64},{1,65},{2,66},{3,67},{4,68},{5,69},{6,70},{7,71},{8,72},{9,... | collective-permute-start | bytes 147464 | tf_op jit(solution)/shard_map/ppermute | solution.py:347
  35.4 0.8 %norms.2.n_ref = f32[12,8,512]{2,1,0:T(8,128)S(1)} custom-call(bf16[12,64,512]{2,1,0:T(8,128)(2,1)S(1)} %get-tuple-element.8.e0, bf16[12,64,512]{2,1,0:T(8,128)(2,1)S(1)} %collective-permute-done.e1), custom_call_target="tpu_custom_call" | custom-call | tf_op jit(solution)/shard_map/norms/pallas_call | solution.py:142
  36.2 0.4 collective-permute-done.8.s1
  36.5 1.6 %fishers.2.fa = f32[12,128,512]{2,1,0:T(8,128)S(1)} custom-call(bf16[12,64,512]{2,1,0:T(8,128)(2,1)S(1)} %get-tuple-element.8.e0, bf16[12,64,512]{2,1,0:T(8,128)(2,1)S(1)} %collective-permute-done.e1, bf16[32,768]{1,0:T(8,128)(2,1)S(1)} %get-tuple-element.12.s0, bf16[32,768]{1,0:T(8,128)(2,1)S(1)} %collective-permute-done.8.s1, f32[12,8,512]{2,1,0:T(8,128)S(1)} %norms.2.n_ref), custom_call_target="tpu_custom_call" | custom-call | tf_op jit(solution)/shard_map/fishers/pallas_call | solution.py:190
  38.2 0.7 %norms.3.n_ref = f32[12,8,512]{2,1,0:T(8,128)S(1)} custom-call(bf16[12,64,512]{2,1,0:T(8,128)(2,1)S(1)} %collective-permute-done.9.e0, bf16[12,64,512]{2,1,0:T(8,128)(2,1)S(1)} %collective-permute-done.10.e1), custom_call_target="tpu_custom_call" | custom-call | tf_op jit(solution)/shard_map/norms/pallas_call | solution.py:142
  39.0 0.0 collective-permute-done.11.s0
  39.0 1.6 %fishers.3.fb = f32[12,128,512]{2,1,0:T(8,128)S(1)} custom-call(bf16[12,64,512]{2,1,0:T(8,128)(2,1)S(1)} %collective-permute-done.9.e0, bf16[12,64,512]{2,1,0:T(8,128)(2,1)S(1)} %collective-permute-done.10.e1, bf16[32,768]{1,0:T(8,128)(2,1)S(1)} %collective-permute-done.11.s0, bf16[32,768]{1,0:T(8,128)(2,1)S(1)} %collective-permute-done.12.s1, ...), custom_call_target="tpu_custom_call" | custom-call | tf_op jit(solution)/shard_map/fishers/pallas_call | solution.py:190
  40.6 3.2 %partial_kernels.1 = f32[32,80,128]{2,1,0:T(8,128)S(1)} custom-call(f32[12,128,512]{2,1,0:T(8,128)S(1)} %fishers.2.fa, f32[12,128,512]{2,1,0:T(8,128)S(1)} %fishers.3.fb), custom_call_target="tpu_custom_call" | custom-call | tf_op jit(solution)/shard_map/partial_kernels/pallas_call | solution.py:259
  43.8 0.1 convert_element_type.6
  43.9 19.0 %all_to_all.5 = f16[32,80,128]{2,1,0:T(8,128)(2,1)S(1)} all-to-all(f16[32,80,128]{2,1,0:T(8,128)(2,1)S(1)} %convert_element_type.6), channel_id=1, replica_groups={{31,23,30,22,10,21,7,24,17,0,15,14,1,19,5,13,20,27,8,4,18,9,26,11,12,6,..., dimensions={0} | all-to-all | bytes 1310720 | tf_op jit(solution)/shard_map/all_to_all | solution.py:369
  62.8 0.1 convert_reduce_fusion
  62.9 2.6 %collective-permute-start.15 = (f32[80,128]{1,0:T(8,128)S(1)}, f32[80,128]{1,0:T(8,128)S(1)}, u32[]{:S(2)}, u32[]{:S(2)}) collective-permute-start(f32[80,128]{1,0:T(8,128)S(1)} %convert_reduce_fusion), channel_id=1, source_target_pairs={{0,64},{1,0},{2,96},{3,32},{4,68},{5,4},{6,100},{7,36},{8,72},{9,8... | collective-permute-start | bytes 122888 | tf_op jit(solution)/shard_map/ppermute | solution.py:385
  65.5 1.9 %collective-permute-start.13 = (f32[80,128]{1,0:T(8,128)S(1)}, f32[80,128]{1,0:T(8,128)S(1)}, u32[]{:S(2)}, u32[]{:S(2)}) collective-permute-start(f32[80,128]{1,0:T(8,128)S(1)} %convert_reduce_fusion), channel_id=1, source_target_pairs={{0,0},{1,64},{2,32},{3,96},{4,4},{5,68},{6,36},{7,100},{8,8},{9,72... | collective-permute-start | bytes 122888 | tf_op jit(solution)/shard_map/ppermute | solution.py:385
  67.5 0.4 collective-permute-start.16
  67.9 3.5 %collective-permute-done.13.y0 = f32[80,128]{1,0:T(8,128)S(1)} collective-permute-done((f32[80,128]{1,0:T(8,128)S(1)}, f32[80,128]{1,0:T(8,128)S(1)}, u32[]{:S(2)}, u32[]{:S(2)}) %collective-permute-start.13) | collective-permute-done | bytes 40992 | tf_op jit(solution)/shard_map/ppermute | solution.py:385
  71.4 0.7 collective-permute-start.14
  72.1 0.9 %collective-permute-done.14.y1 = f32[80,128]{1,0:T(8,128)S(1)} collective-permute-done((f32[80,128]{1,0:T(8,128)S(1)}, f32[80,128]{1,0:T(8,128)S(1)}, u32[]{:S(2)}, u32[]{:S(2)}) %collective-permute-start.14) | collective-permute-done | bytes 40992 | tf_op jit(solution)/shard_map/ppermute | solution.py:330
  72.9 1.2 %in_order.1 = f32[2,48,192]{2,1,0:T(8,128)} custom-call(f32[80,128]{1,0:T(8,128)S(1)} %collective-permute-done.13.y0, f32[80,128]{1,0:T(8,128)S(1)} %collective-permute-done.14.y1, f32[80,128]{1,0:T(8,128)S(1)} %collective-permute-done.15.y2, f32[80,128]{1,0:T(8,128)S(1)} %collective-permute-done.16.y3), custom_call_target="tpu_custom_call" | custom-call | tf_op jit(solution)/shard_map/in_order/pallas_call | solution.py:315
  (18 shorter events, 0.1 us)
Async XLA Ops:
  1.9 19.4 %collective-permute-start.9 = (bf16[12,64,512]{2,1,0:T(8,128)(2,1)S(1)}, bf16[12,64,512]{2,1,0:T(8,128)(2,1)S(1)}, u32[]{:S(2)}, u32[]{:S(2)}) collective-permute-start(bf16[12,64,512]{2,1,0:T(8,128)(2,1)S(1)} %get-tuple-element.8.e0), channel_id=1, source_target_pairs={{0,64},{32,96},{64,0},{96,32},{1,65},{33,97},{65,1},{97,33},{2,66}... | collective-permute-start | bytes 2359304 | tf_op jit(solution)/shard_map/ppermute | solution.py:330
  2.3 1.2 %collective-permute-start.1 = (bf16[32,768]{1,0:T(8,128)(2,1)S(1)}, bf16[32,768]{1,0:T(8,128)(2,1)S(1)}, u32[]{:S(2)}, u32[]{:S(2)}) collective-permute-start(bf16[32,768]{1,0:T(8,128)(2,1)S(1)} %get-tuple-element.10), channel_id=1, source_target_pairs={{0,32},{32,0},{64,96},{96,64},{1,33},{33,1},{65,97},{97,65},{2,34}... | collective-permute-start | bytes 147464 | tf_op jit(solution)/shard_map/ppermute | solution.py:330
  3.6 17.7 %collective-permute-start.3 = (bf16[64,768]{1,0:T(8,128)(2,1)S(1)}, bf16[64,768]{1,0:T(8,128)(2,1)S(1)}, u32[]{:S(2)}, u32[]{:S(2)}) collective-permute-start(bf16[64,768]{1,0:T(8,128)(2,1)S(1)} %pad_maximum_fusion), channel_id=1, source_target_pairs={{0,24},{1,25},{2,26},{3,27},{4,28},{5,29},{6,30},{7,31},{8,16},{9,... | collective-permute-start | bytes 294920 | tf_op jit(solution)/shard_map/ppermute | solution.py:335
  7.8 13.5 %collective-permute-start.4 = (bf16[64,768]{1,0:T(8,128)(2,1)S(1)}, bf16[64,768]{1,0:T(8,128)(2,1)S(1)}, u32[]{:S(2)}, u32[]{:S(2)}) collective-permute-start(bf16[64,768]{1,0:T(8,128)(2,1)S(1)} %pad_maximum_fusion), channel_id=1, source_target_pairs={{0,16},{1,17},{2,18},{3,19},{4,20},{5,21},{6,22},{7,23},{8,24},{9,... | collective-permute-start | bytes 294920 | tf_op jit(solution)/shard_map/ppermute | solution.py:335
  7.8 13.5 %collective-permute-start.2 = (bf16[64,768]{1,0:T(8,128)(2,1)S(1)}, bf16[64,768]{1,0:T(8,128)(2,1)S(1)}, u32[]{:S(2)}, u32[]{:S(2)}) collective-permute-start(bf16[64,768]{1,0:T(8,128)(2,1)S(1)} %pad_maximum_fusion), channel_id=1, source_target_pairs={{0,8},{1,9},{2,10},{3,11},{4,12},{5,13},{6,14},{7,15},{8,0},{9,1},... | collective-permute-start | bytes 294920 | tf_op jit(solution)/shard_map/ppermute | solution.py:335
  8.8 26.7 %collective-permute-start = (bf16[12,64,512]{2,1,0:T(8,128)(2,1)S(1)}, bf16[12,64,512]{2,1,0:T(8,128)(2,1)S(1)}, u32[]{:S(2)}, u32[]{:S(2)}) collective-permute-start(bf16[12,64,512]{2,1,0:T(8,128)(2,1)S(1)} %get-tuple-element.8.e0), channel_id=1, source_target_pairs={{0,32},{32,0},{64,96},{96,64},{1,33},{33,1},{65,97},{97,65},{2,34}... | collective-permute-start | bytes 2359304 | tf_op jit(solution)/shard_map/ppermute | solution.py:330
  21.3 16.9 %collective-permute-start.10 = (bf16[12,64,512]{2,1,0:T(8,128)(2,1)S(1)}, bf16[12,64,512]{2,1,0:T(8,128)(2,1)S(1)}, u32[]{:S(2)}, u32[]{:S(2)}) collective-permute-start(bf16[12,64,512]{2,1,0:T(8,128)(2,1)S(1)} %collective-permute-done.9.e0), channel_id=1, source_target_pairs={{0,32},{32,0},{64,96},{96,64},{1,33},{33,1},{65,97},{97,65},{2,34}... | collective-permute-start | bytes 2359304 | tf_op jit(solution)/shard_map/ppermute | solution.py:330
  21.4 6.8 %collective-permute-start.7 = (bf16[64,768]{1,0:T(8,128)(2,1)S(1)}, bf16[64,768]{1,0:T(8,128)(2,1)S(1)}, u32[]{:S(2)}, u32[]{:S(2)}) collective-permute-start(bf16[64,768]{1,0:T(8,128)(2,1)S(1)} %add_add_fusion.1), channel_id=1, source_target_pairs={{0,4},{1,5},{2,6},{3,7},{4,0},{5,1},{6,2},{7,3},{8,12},{9,13},{10,... | collective-permute-start | bytes 294920 | tf_op jit(solution)/shard_map/ppermute | solution.py:335
  24.5 6.1 %collective-permute-start.6 = (bf16[64,768]{1,0:T(8,128)(2,1)S(1)}, bf16[64,768]{1,0:T(8,128)(2,1)S(1)}, u32[]{:S(2)}, u32[]{:S(2)}) collective-permute-start(bf16[64,768]{1,0:T(8,128)(2,1)S(1)} %add_add_fusion.1), channel_id=1, source_target_pairs={{0,6},{1,7},{2,4},{3,5},{4,2},{5,3},{6,0},{7,1},{8,14},{9,15},{10,... | collective-permute-start | bytes 294920 | tf_op jit(solution)/shard_map/ppermute | solution.py:335
  25.6 5.0 %collective-permute-start.5 = (bf16[64,768]{1,0:T(8,128)(2,1)S(1)}, bf16[64,768]{1,0:T(8,128)(2,1)S(1)}, u32[]{:S(2)}, u32[]{:S(2)}) collective-permute-start(bf16[64,768]{1,0:T(8,128)(2,1)S(1)} %add_add_fusion.1), channel_id=1, source_target_pairs={{0,2},{1,3},{2,0},{3,1},{4,6},{5,7},{6,4},{7,5},{8,10},{9,11},{10,... | collective-permute-start | bytes 294920 | tf_op jit(solution)/shard_map/ppermute | solution.py:335
  30.6 5.9 %collective-permute-start.8 = (bf16[32,768]{1,0:T(8,128)(2,1)S(1)}, bf16[32,768]{1,0:T(8,128)(2,1)S(1)}, u32[]{:S(2)}, u32[]{:S(2)}) collective-permute-start(bf16[32,768]{1,0:T(8,128)(2,1)S(1)} %get-tuple-element.12.s0), channel_id=1, source_target_pairs={{0,1},{1,0},{2,3},{3,2},{4,5},{5,4},{6,7},{7,6},{8,9},{9,8},{10,11... | collective-permute-start | bytes 147464 | tf_op jit(solution)/shard_map/ppermute | solution.py:347
  33.0 5.9 %collective-permute-start.12 = (bf16[32,768]{1,0:T(8,128)(2,1)S(1)}, bf16[32,768]{1,0:T(8,128)(2,1)S(1)}, u32[]{:S(2)}, u32[]{:S(2)}) collective-permute-start(bf16[32,768]{1,0:T(8,128)(2,1)S(1)} %get-tuple-element.11), channel_id=1, source_target_pairs={{0,65},{1,64},{2,67},{3,66},{4,69},{5,68},{6,71},{7,70},{8,73},{9,... | collective-permute-start | bytes 147464 | tf_op jit(solution)/shard_map/ppermute | solution.py:347
  33.0 5.9 %collective-permute-start.11 = (bf16[32,768]{1,0:T(8,128)(2,1)S(1)}, bf16[32,768]{1,0:T(8,128)(2,1)S(1)}, u32[]{:S(2)}, u32[]{:S(2)}) collective-permute-start(bf16[32,768]{1,0:T(8,128)(2,1)S(1)} %get-tuple-element.11), channel_id=1, source_target_pairs={{0,64},{1,65},{2,66},{3,67},{4,68},{5,69},{6,70},{7,71},{8,72},{9,... | collective-permute-start | bytes 147464 | tf_op jit(solution)/shard_map/ppermute | solution.py:347
  62.9 4.5 %collective-permute-start.15 = (f32[80,128]{1,0:T(8,128)S(1)}, f32[80,128]{1,0:T(8,128)S(1)}, u32[]{:S(2)}, u32[]{:S(2)}) collective-permute-start(f32[80,128]{1,0:T(8,128)S(1)} %convert_reduce_fusion), channel_id=1, source_target_pairs={{0,64},{1,0},{2,96},{3,32},{4,68},{5,4},{6,100},{7,36},{8,72},{9,8... | collective-permute-start | bytes 122888 | tf_op jit(solution)/shard_map/ppermute | solution.py:385
  65.5 5.9 %collective-permute-start.13 = (f32[80,128]{1,0:T(8,128)S(1)}, f32[80,128]{1,0:T(8,128)S(1)}, u32[]{:S(2)}, u32[]{:S(2)}) collective-permute-start(f32[80,128]{1,0:T(8,128)S(1)} %convert_reduce_fusion), channel_id=1, source_target_pairs={{0,0},{1,64},{2,32},{3,96},{4,4},{5,68},{6,36},{7,100},{8,8},{9,72... | collective-permute-start | bytes 122888 | tf_op jit(solution)/shard_map/ppermute | solution.py:385
  67.5 4.6 %collective-permute-start.16 = (f32[80,128]{1,0:T(8,128)S(1)}, f32[80,128]{1,0:T(8,128)S(1)}, u32[]{:S(2)}, u32[]{:S(2)}) collective-permute-start(f32[80,128]{1,0:T(8,128)S(1)} %collective-permute-done.15.y2), channel_id=1, source_target_pairs={{0,32},{32,0},{64,96},{96,64},{1,33},{33,1},{65,97},{97,65},{2,34}... | collective-permute-start | bytes 122888 | tf_op jit(solution)/shard_map/ppermute | solution.py:330
  71.4 1.5 %collective-permute-start.14 = (f32[80,128]{1,0:T(8,128)S(1)}, f32[80,128]{1,0:T(8,128)S(1)}, u32[]{:S(2)}, u32[]{:S(2)}) collective-permute-start(f32[80,128]{1,0:T(8,128)S(1)} %collective-permute-done.13.y0), channel_id=1, source_target_pairs={{0,32},{32,0},{64,96},{96,64},{1,33},{33,1},{65,97},{97,65},{2,34}... | collective-permute-start | bytes 122888 | tf_op jit(solution)/shard_map/ppermute | solution.py:330

commit v11 on v10

--- a/solution.py
+++ b/solution.py
@@ -41,6 +41,12 @@
 ORDER = (
     31, 23, 30, 22, 10, 21, 7, 24, 17, 0, 15, 14, 1, 19, 5, 13,
     20, 27, 8, 4, 18, 9, 26, 11, 12, 6, 29, 3, 16, 28, 25, 2,
+)
+
+
+OTHER_ORDER = (
+    20, 10, 29, 18, 9, 24, 22, 8, 2, 31, 0, 14, 3, 23, 11, 26,
+    7, 28, 5, 16, 27, 30, 25, 15, 4, 1, 17, 19, 13, 6, 21, 12,
 )
 
 
@@ -221,6 +227,11 @@
                     z_ref[slot, h, at : at + SB, c : c + 128] = tile
 
     down, across = iota((HALF, HALF), 0), iota((HALF, HALF), 1)
+    other_core = lax.axis_index("subj") % 2
+
+    def place_of(to):
+        place = ORDER.index(to)
+        return place + other_core * (OTHER_ORDER.index(to) - place)
 
     def products(q, slot):
         whole = [dot_nt(z_ref[slot, h], z_ref[slot, h]) for h in range(2)]
@@ -245,7 +256,7 @@
             for first in range(0, HALF, SB):
                 r, line = divmod(n * HALF + first, QUARTER)
                 to = (q // 2) * 8 + (slot * 2 + r % 2) * 2 + r // 2
-                o_ref[ORDER.index(to), line : line + SB, :] = tile[first : first + SB]
+                o_ref[place_of(to), line : line + SB, :] = tile[first : first + SB]
 
     scores(0, 0)
     for q in range(1, KL // 2):
@@ -366,8 +377,9 @@
     fa = fishers(own, beside, mine, ours, first)
     fb = fishers(across, beyond, left, right, second)
     tiles = partial_kernels(fa, fb, devices)
+    groups = [[j * devices + i for i in (ORDER, OTHER_ORDER)[j % 2]] for j in range(GR)]
     tiles = lax.all_to_all(
-        tiles.astype(LINK), "vox", 0, 0, axis_index_groups=[list(ORDER)], tiled=True
+        tiles.astype(LINK), ("subj", "vox"), 0, 0, axis_index_groups=groups, tiled=True
     )
     tile = jnp.sum(tiles.astype(F32), axis=0)
 

time: 74.9 us -> 74.9 us (level)
  waiting for transfers between devices: 23.5 us -> 22.2 us
  blocking collectives: 19 us -> 20.1 us
    ppermute x2, waiting for transfers between devices: 3.53 us -> 2.25 us  [turned(): return lax.ppermute(tile, ('subj', 'vox'), moves)]
    all_to_all x1, blocking collectives: 19 us -> 20.1 us  [body(): lax.all_to_all(tiles.astype(LINK), ('subj', 'vox'), 0, 0, axis_index_grou...]
where the time goes in v11:
time: 74.9 us; the launch traced here: 73.7 us
  waiting for transfers between devices  22.2 us (30%)
  blocking collectives  20.1 us (27%)
  starting transfers between devices  19.9 us (27%)
  Pallas kernels  11 us (15%)
    all_to_all x1, blocking collectives, body(): lax.all_to_all(tiles.astype(LINK), ('subj', 'vox'), 0, 0, axis_index_grou...  20.1 us
    ppermute x6, waiting for transfers between devices, swapped(): return lax.ppermute(x, 'subj', [(n, n ^ r) for n in range(GR)])  14.6 us
    ppermute x6, starting transfers between devices, summed(): lax.ppermute(x, 'vox', [(n, n ^ step * stride) for n in range(devices)])  9.41 us
    ppermute x6, waiting for transfers between devices, summed(): lax.ppermute(x, 'vox', [(n, n ^ step * stride) for n in range(devices)])  5 us
    ppermute x2, starting transfers between devices, turned(): return lax.ppermute(tile, ('subj', 'vox'), moves)  4.8 us
    ppermute x3, starting transfers between devices, along_y(): return lax.ppermute(x, ('subj', 'vox'), moves)  4.78 us
    pallas_call x2, Pallas kernels, fishers(): pl.pallas_call(fisher_kernel, out_shape=pltpu.VMEM((EP, KL * PART, width)...  3.27 us
    pallas_call x1, Pallas kernels, partial_kernels(): pl.pallas_call(kernel_kernel, out_shape=pltpu.VMEM((devices, QUARTER, 2 *...  3.16 us
  transfers between devices with their start and end apart: 17, of which 7 were waited for; matrix products, arithmetic and copies ran while one was open for 0% of the time, Pallas kernels for 4%

profile of v11, /device:TPU:8, one launch (start us, length us, event | category | flops | bytes accessed | tf_op | source)
XLA Modules:
  0.0 73.7 jit_solution(7240585078310543261)
XLA Ops:
  0.0 1.9 %windows.1 = (bf16[12,64,512]{2,1,0:T(8,128)(2,1)S(1)}, bf16[32,768]{1,0:T(8,128)(2,1)S(1)}, bf16[32,768]{1,0:T(8,128)(2,1)S(1)}) custom-call(s32[16,12]{1,0:T(8,128)} %off_ref.1, s32[64]{0:T(128)} %sel_ref.1, bf16[4,256,512]{2,1,0:T(8,128)(2,1)} %series_ref.1), custom_call_target="tpu_custom_call" | custom-call | tf_op jit(solution)/shard_map/windows/pallas_call | solution.py:107
  1.9 0.4 collective-permute-start.9
  2.3 1.2 %collective-permute-done.1 = bf16[32,768]{1,0:T(8,128)(2,1)S(1)} collective-permute-done((bf16[32,768]{1,0:T(8,128)(2,1)S(1)}, bf16[32,768]{1,0:T(8,128)(2,1)S(1)}, u32[]{:S(2)}, u32[]{:S(2)}) %collective-permute-start.1) | collective-permute-done | bytes 49184 | tf_op jit(solution)/shard_map/ppermute | solution.py:341
  3.6 4.2 %collective-permute-start.3 = (bf16[64,768]{1,0:T(8,128)(2,1)S(1)}, bf16[64,768]{1,0:T(8,128)(2,1)S(1)}, u32[]{:S(2)}, u32[]{:S(2)}) collective-permute-start(bf16[64,768]{1,0:T(8,128)(2,1)S(1)} %pad_maximum_fusion), channel_id=1, source_target_pairs={{0,24},{1,25},{2,26},{3,27},{4,28},{5,29},{6,30},{7,31},{8,16},{9,... | collective-permute-start | bytes 294920 | tf_op jit(solution)/shard_map/ppermute | solution.py:346
  7.8 0.9 %collective-permute-start.2 = (bf16[64,768]{1,0:T(8,128)(2,1)S(1)}, bf16[64,768]{1,0:T(8,128)(2,1)S(1)}, u32[]{:S(2)}, u32[]{:S(2)}) collective-permute-start(bf16[64,768]{1,0:T(8,128)(2,1)S(1)} %pad_maximum_fusion), channel_id=1, source_target_pairs={{0,8},{1,9},{2,10},{3,11},{4,12},{5,13},{6,14},{7,15},{8,0},{9,1},... | collective-permute-start | bytes 294920 | tf_op jit(solution)/shard_map/ppermute | solution.py:346
  8.8 0.0 collective-permute-start
  8.8 12.5 %collective-permute-done.9.e0 = bf16[12,64,512]{2,1,0:T(8,128)(2,1)S(1)} collective-permute-done((bf16[12,64,512]{2,1,0:T(8,128)(2,1)S(1)}, bf16[12,64,512]{2,1,0:T(8,128)(2,1)S(1)}, u32[]{:S(2)}, u32[]{:S(2)}) %collective-permute-start.9) | collective-permute-done | bytes 786464 | tf_op jit(solution)/shard_map/ppermute | solution.py:341
  21.3 0.0 collective-permute-start.10
  21.3 0.1 add_add_fusion.1
  21.4 3.1 %collective-permute-start.7 = (bf16[64,768]{1,0:T(8,128)(2,1)S(1)}, bf16[64,768]{1,0:T(8,128)(2,1)S(1)}, u32[]{:S(2)}, u32[]{:S(2)}) collective-permute-start(bf16[64,768]{1,0:T(8,128)(2,1)S(1)} %add_add_fusion.1), channel_id=1, source_target_pairs={{0,4},{1,5},{2,6},{3,7},{4,0},{5,1},{6,2},{7,3},{8,12},{9,13},{10,... | collective-permute-start | bytes 294920 | tf_op jit(solution)/shard_map/ppermute | solution.py:346
  24.5 1.1 %collective-permute-start.6 = (bf16[64,768]{1,0:T(8,128)(2,1)S(1)}, bf16[64,768]{1,0:T(8,128)(2,1)S(1)}, u32[]{:S(2)}, u32[]{:S(2)}) collective-permute-start(bf16[64,768]{1,0:T(8,128)(2,1)S(1)} %add_add_fusion.1), channel_id=1, source_target_pairs={{0,6},{1,7},{2,4},{3,5},{4,2},{5,3},{6,0},{7,1},{8,14},{9,15},{10,... | collective-permute-start | bytes 294920 | tf_op jit(solution)/shard_map/ppermute | solution.py:346
  25.6 2.5 %collective-permute-done.7 = bf16[64,768]{1,0:T(8,128)(2,1)S(1)} collective-permute-done((bf16[64,768]{1,0:T(8,128)(2,1)S(1)}, bf16[64,768]{1,0:T(8,128)(2,1)S(1)}, u32[]{:S(2)}, u32[]{:S(2)}) %collective-permute-start.7) | collective-permute-done | bytes 98336 | tf_op jit(solution)/shard_map/ppermute | solution.py:346
  28.1 2.4 %collective-permute-done.6 = bf16[64,768]{1,0:T(8,128)(2,1)S(1)} collective-permute-done((bf16[64,768]{1,0:T(8,128)(2,1)S(1)}, bf16[64,768]{1,0:T(8,128)(2,1)S(1)}, u32[]{:S(2)}, u32[]{:S(2)}) %collective-permute-start.6) | collective-permute-done | bytes 98336 | tf_op jit(solution)/shard_map/ppermute | solution.py:346
  30.6 2.4 %collective-permute-start.8 = (bf16[32,768]{1,0:T(8,128)(2,1)S(1)}, bf16[32,768]{1,0:T(8,128)(2,1)S(1)}, u32[]{:S(2)}, u32[]{:S(2)}) collective-permute-start(bf16[32,768]{1,0:T(8,128)(2,1)S(1)} %get-tuple-element.12.s0), channel_id=1, source_target_pairs={{0,1},{1,0},{2,3},{3,2},{4,5},{5,4},{6,7},{7,6},{8,9},{9,8},{10,11... | collective-permute-start | bytes 147464 | tf_op jit(solution)/shard_map/ppermute | solution.py:358
  33.0 2.4 %collective-permute-start.11 = (bf16[32,768]{1,0:T(8,128)(2,1)S(1)}, bf16[32,768]{1,0:T(8,128)(2,1)S(1)}, u32[]{:S(2)}, u32[]{:S(2)}) collective-permute-start(bf16[32,768]{1,0:T(8,128)(2,1)S(1)} %get-tuple-element.11), channel_id=1, source_target_pairs={{0,64},{1,65},{2,66},{3,67},{4,68},{5,69},{6,70},{7,71},{8,72},{9,... | collective-permute-start | bytes 147464 | tf_op jit(solution)/shard_map/ppermute | solution.py:358
  35.4 0.8 %norms.2.n_ref = f32[12,8,512]{2,1,0:T(8,128)S(1)} custom-call(bf16[12,64,512]{2,1,0:T(8,128)(2,1)S(1)} %get-tuple-element.8.e0, bf16[12,64,512]{2,1,0:T(8,128)(2,1)S(1)} %collective-permute-done.e1), custom_call_target="tpu_custom_call" | custom-call | tf_op jit(solution)/shard_map/norms/pallas_call | solution.py:148
  36.2 0.4 collective-permute-done.8.s1
  36.5 1.6 %fishers.2.fa = f32[12,128,512]{2,1,0:T(8,128)S(1)} custom-call(bf16[12,64,512]{2,1,0:T(8,128)(2,1)S(1)} %get-tuple-element.8.e0, bf16[12,64,512]{2,1,0:T(8,128)(2,1)S(1)} %collective-permute-done.e1, bf16[32,768]{1,0:T(8,128)(2,1)S(1)} %get-tuple-element.12.s0, bf16[32,768]{1,0:T(8,128)(2,1)S(1)} %collective-permute-done.8.s1, f32[12,8,512]{2,1,0:T(8,128)S(1)} %norms.2.n_ref), custom_call_target="tpu_custom_call" | custom-call | tf_op jit(solution)/shard_map/fishers/pallas_call | solution.py:196
  38.2 0.7 %norms.3.n_ref = f32[12,8,512]{2,1,0:T(8,128)S(1)} custom-call(bf16[12,64,512]{2,1,0:T(8,128)(2,1)S(1)} %collective-permute-done.9.e0, bf16[12,64,512]{2,1,0:T(8,128)(2,1)S(1)} %collective-permute-done.10.e1), custom_call_target="tpu_custom_call" | custom-call | tf_op jit(solution)/shard_map/norms/pallas_call | solution.py:148
  39.0 0.0 collective-permute-done.11.s0
  39.0 1.6 %fishers.3.fb = f32[12,128,512]{2,1,0:T(8,128)S(1)} custom-call(bf16[12,64,512]{2,1,0:T(8,128)(2,1)S(1)} %collective-permute-done.9.e0, bf16[12,64,512]{2,1,0:T(8,128)(2,1)S(1)} %collective-permute-done.10.e1, bf16[32,768]{1,0:T(8,128)(2,1)S(1)} %collective-permute-done.11.s0, bf16[32,768]{1,0:T(8,128)(2,1)S(1)} %collective-permute-done.12.s1, ...), custom_call_target="tpu_custom_call" | custom-call | tf_op jit(solution)/shard_map/fishers/pallas_call | solution.py:196
  40.6 3.2 %partial_kernels.1 = f32[32,80,128]{2,1,0:T(8,128)S(1)} custom-call(f32[12,128,512]{2,1,0:T(8,128)S(1)} %fishers.2.fa, f32[12,128,512]{2,1,0:T(8,128)S(1)} %fishers.3.fb), custom_call_target="tpu_custom_call" | custom-call | tf_op jit(solution)/shard_map/partial_kernels/pallas_call | solution.py:270
  43.8 0.1 convert_element_type.6
  43.9 20.1 %all_to_all.5 = f16[32,80,128]{2,1,0:T(8,128)(2,1)S(1)} all-to-all(f16[32,80,128]{2,1,0:T(8,128)(2,1)S(1)} %convert_element_type.6), channel_id=1, replica_groups={{31,23,30,22,10,21,7,24,17,0,15,14,1,19,5,13,20,27,8,4,18,9,26,11,12,6,..., dimensions={0} | all-to-all | bytes 1310720 | tf_op jit(solution)/shard_map/all_to_all | solution.py:381
  63.9 0.1 convert_reduce_fusion
  64.0 1.3 %collective-permute-start.15 = (f32[80,128]{1,0:T(8,128)S(1)}, f32[80,128]{1,0:T(8,128)S(1)}, u32[]{:S(2)}, u32[]{:S(2)}) collective-permute-start(f32[80,128]{1,0:T(8,128)S(1)} %convert_reduce_fusion), channel_id=1, source_target_pairs={{0,64},{1,0},{2,96},{3,32},{4,68},{5,4},{6,100},{7,36},{8,72},{9,8... | collective-permute-start | bytes 122888 | tf_op jit(solution)/shard_map/ppermute | solution.py:397
  65.3 3.5 %collective-permute-start.13 = (f32[80,128]{1,0:T(8,128)S(1)}, f32[80,128]{1,0:T(8,128)S(1)}, u32[]{:S(2)}, u32[]{:S(2)}) collective-permute-start(f32[80,128]{1,0:T(8,128)S(1)} %convert_reduce_fusion), channel_id=1, source_target_pairs={{0,0},{1,64},{2,32},{3,96},{4,4},{5,68},{6,36},{7,100},{8,8},{9,72... | collective-permute-start | bytes 122888 | tf_op jit(solution)/shard_map/ppermute | solution.py:397
  68.9 0.1 collective-permute-start.16
  68.9 2.2 %collective-permute-done.13.y0 = f32[80,128]{1,0:T(8,128)S(1)} collective-permute-done((f32[80,128]{1,0:T(8,128)S(1)}, f32[80,128]{1,0:T(8,128)S(1)}, u32[]{:S(2)}, u32[]{:S(2)}) %collective-permute-start.13) | collective-permute-done | bytes 40992 | tf_op jit(solution)/shard_map/ppermute | solution.py:397
  71.2 0.4 collective-permute-start.14
  71.6 0.9 %collective-permute-done.14.y1 = f32[80,128]{1,0:T(8,128)S(1)} collective-permute-done((f32[80,128]{1,0:T(8,128)S(1)}, f32[80,128]{1,0:T(8,128)S(1)}, u32[]{:S(2)}, u32[]{:S(2)}) %collective-permute-start.14) | collective-permute-done | bytes 40992 | tf_op jit(solution)/shard_map/ppermute | solution.py:341
  72.5 1.2 %in_order.1 = f32[2,48,192]{2,1,0:T(8,128)} custom-call(f32[80,128]{1,0:T(8,128)S(1)} %collective-permute-done.13.y0, f32[80,128]{1,0:T(8,128)S(1)} %collective-permute-done.14.y1, f32[80,128]{1,0:T(8,128)S(1)} %collective-permute-done.15.y2, f32[80,128]{1,0:T(8,128)S(1)} %collective-permute-done.16.y3), custom_call_target="tpu_custom_call" | custom-call | tf_op jit(solution)/shard_map/in_order/pallas_call | solution.py:326
  (18 shorter events, 0.1 us)
Async XLA Ops:
  1.9 19.4 %collective-permute-start.9 = (bf16[12,64,512]{2,1,0:T(8,128)(2,1)S(1)}, bf16[12,64,512]{2,1,0:T(8,128)(2,1)S(1)}, u32[]{:S(2)}, u32[]{:S(2)}) collective-permute-start(bf16[12,64,512]{2,1,0:T(8,128)(2,1)S(1)} %get-tuple-element.8.e0), channel_id=1, source_target_pairs={{0,64},{32,96},{64,0},{96,32},{1,65},{33,97},{65,1},{97,33},{2,66}... | collective-permute-start | bytes 2359304 | tf_op jit(solution)/shard_map/ppermute | solution.py:341
  2.3 1.2 %collective-permute-start.1 = (bf16[32,768]{1,0:T(8,128)(2,1)S(1)}, bf16[32,768]{1,0:T(8,128)(2,1)S(1)}, u32[]{:S(2)}, u32[]{:S(2)}) collective-permute-start(bf16[32,768]{1,0:T(8,128)(2,1)S(1)} %get-tuple-element.10), channel_id=1, source_target_pairs={{0,32},{32,0},{64,96},{96,64},{1,33},{33,1},{65,97},{97,65},{2,34}... | collective-permute-start | bytes 147464 | tf_op jit(solution)/shard_map/ppermute | solution.py:341
  3.6 17.7 %collective-permute-start.3 = (bf16[64,768]{1,0:T(8,128)(2,1)S(1)}, bf16[64,768]{1,0:T(8,128)(2,1)S(1)}, u32[]{:S(2)}, u32[]{:S(2)}) collective-permute-start(bf16[64,768]{1,0:T(8,128)(2,1)S(1)} %pad_maximum_fusion), channel_id=1, source_target_pairs={{0,24},{1,25},{2,26},{3,27},{4,28},{5,29},{6,30},{7,31},{8,16},{9,... | collective-permute-start | bytes 294920 | tf_op jit(solution)/shard_map/ppermute | solution.py:346
  7.8 13.5 %collective-permute-start.4 = (bf16[64,768]{1,0:T(8,128)(2,1)S(1)}, bf16[64,768]{1,0:T(8,128)(2,1)S(1)}, u32[]{:S(2)}, u32[]{:S(2)}) collective-permute-start(bf16[64,768]{1,0:T(8,128)(2,1)S(1)} %pad_maximum_fusion), channel_id=1, source_target_pairs={{0,16},{1,17},{2,18},{3,19},{4,20},{5,21},{6,22},{7,23},{8,24},{9,... | collective-permute-start | bytes 294920 | tf_op jit(solution)/shard_map/ppermute | solution.py:346
  7.8 13.5 %collective-permute-start.2 = (bf16[64,768]{1,0:T(8,128)(2,1)S(1)}, bf16[64,768]{1,0:T(8,128)(2,1)S(1)}, u32[]{:S(2)}, u32[]{:S(2)}) collective-permute-start(bf16[64,768]{1,0:T(8,128)(2,1)S(1)} %pad_maximum_fusion), channel_id=1, source_target_pairs={{0,8},{1,9},{2,10},{3,11},{4,12},{5,13},{6,14},{7,15},{8,0},{9,1},... | collective-permute-start | bytes 294920 | tf_op jit(solution)/shard_map/ppermute | solution.py:346
  8.8 26.7 %collective-permute-start = (bf16[12,64,512]{2,1,0:T(8,128)(2,1)S(1)}, bf16[12,64,512]{2,1,0:T(8,128)(2,1)S(1)}, u32[]{:S(2)}, u32[]{:S(2)}) collective-permute-start(bf16[12,64,512]{2,1,0:T(8,128)(2,1)S(1)} %get-tuple-element.8.e0), channel_id=1, source_target_pairs={{0,32},{32,0},{64,96},{96,64},{1,33},{33,1},{65,97},{97,65},{2,34}... | collective-permute-start | bytes 2359304 | tf_op jit(solution)/shard_map/ppermute | solution.py:341
  21.3 16.9 %collective-permute-start.10 = (bf16[12,64,512]{2,1,0:T(8,128)(2,1)S(1)}, bf16[12,64,512]{2,1,0:T(8,128)(2,1)S(1)}, u32[]{:S(2)}, u32[]{:S(2)}) collective-permute-start(bf16[12,64,512]{2,1,0:T(8,128)(2,1)S(1)} %collective-permute-done.9.e0), channel_id=1, source_target_pairs={{0,32},{32,0},{64,96},{96,64},{1,33},{33,1},{65,97},{97,65},{2,34}... | collective-permute-start | bytes 2359304 | tf_op jit(solution)/shard_map/ppermute | solution.py:341
  21.4 6.8 %collective-permute-start.7 = (bf16[64,768]{1,0:T(8,128)(2,1)S(1)}, bf16[64,768]{1,0:T(8,128)(2,1)S(1)}, u32[]{:S(2)}, u32[]{:S(2)}) collective-permute-start(bf16[64,768]{1,0:T(8,128)(2,1)S(1)} %add_add_fusion.1), channel_id=1, source_target_pairs={{0,4},{1,5},{2,6},{3,7},{4,0},{5,1},{6,2},{7,3},{8,12},{9,13},{10,... | collective-permute-start | bytes 294920 | tf_op jit(solution)/shard_map/ppermute | solution.py:346
  24.5 6.1 %collective-permute-start.6 = (bf16[64,768]{1,0:T(8,128)(2,1)S(1)}, bf16[64,768]{1,0:T(8,128)(2,1)S(1)}, u32[]{:S(2)}, u32[]{:S(2)}) collective-permute-start(bf16[64,768]{1,0:T(8,128)(2,1)S(1)} %add_add_fusion.1), channel_id=1, source_target_pairs={{0,6},{1,7},{2,4},{3,5},{4,2},{5,3},{6,0},{7,1},{8,14},{9,15},{10,... | collective-permute-start | bytes 294920 | tf_op jit(solution)/shard_map/ppermute | solution.py:346
  25.6 5.0 %collective-permute-start.5 = (bf16[64,768]{1,0:T(8,128)(2,1)S(1)}, bf16[64,768]{1,0:T(8,128)(2,1)S(1)}, u32[]{:S(2)}, u32[]{:S(2)}) collective-permute-start(bf16[64,768]{1,0:T(8,128)(2,1)S(1)} %add_add_fusion.1), channel_id=1, source_target_pairs={{0,2},{1,3},{2,0},{3,1},{4,6},{5,7},{6,4},{7,5},{8,10},{9,11},{10,... | collective-permute-start | bytes 294920 | tf_op jit(solution)/shard_map/ppermute | solution.py:346
  30.6 5.9 %collective-permute-start.8 = (bf16[32,768]{1,0:T(8,128)(2,1)S(1)}, bf16[32,768]{1,0:T(8,128)(2,1)S(1)}, u32[]{:S(2)}, u32[]{:S(2)}) collective-permute-start(bf16[32,768]{1,0:T(8,128)(2,1)S(1)} %get-tuple-element.12.s0), channel_id=1, source_target_pairs={{0,1},{1,0},{2,3},{3,2},{4,5},{5,4},{6,7},{7,6},{8,9},{9,8},{10,11... | collective-permute-start | bytes 147464 | tf_op jit(solution)/shard_map/ppermute | solution.py:358
  33.0 5.9 %collective-permute-start.12 = (bf16[32,768]{1,0:T(8,128)(2,1)S(1)}, bf16[32,768]{1,0:T(8,128)(2,1)S(1)}, u32[]{:S(2)}, u32[]{:S(2)}) collective-permute-start(bf16[32,768]{1,0:T(8,128)(2,1)S(1)} %get-tuple-element.11), channel_id=1, source_target_pairs={{0,65},{1,64},{2,67},{3,66},{4,69},{5,68},{6,71},{7,70},{8,73},{9,... | collective-permute-start | bytes 147464 | tf_op jit(solution)/shard_map/ppermute | solution.py:358
  33.0 5.9 %collective-permute-start.11 = (bf16[32,768]{1,0:T(8,128)(2,1)S(1)}, bf16[32,768]{1,0:T(8,128)(2,1)S(1)}, u32[]{:S(2)}, u32[]{:S(2)}) collective-permute-start(bf16[32,768]{1,0:T(8,128)(2,1)S(1)} %get-tuple-element.11), channel_id=1, source_target_pairs={{0,64},{1,65},{2,66},{3,67},{4,68},{5,69},{6,70},{7,71},{8,72},{9,... | collective-permute-start | bytes 147464 | tf_op jit(solution)/shard_map/ppermute | solution.py:358
  64.0 4.8 %collective-permute-start.15 = (f32[80,128]{1,0:T(8,128)S(1)}, f32[80,128]{1,0:T(8,128)S(1)}, u32[]{:S(2)}, u32[]{:S(2)}) collective-permute-start(f32[80,128]{1,0:T(8,128)S(1)} %convert_reduce_fusion), channel_id=1, source_target_pairs={{0,64},{1,0},{2,96},{3,32},{4,68},{5,4},{6,100},{7,36},{8,72},{9,8... | collective-permute-start | bytes 122888 | tf_op jit(solution)/shard_map/ppermute | solution.py:397
  65.3 5.9 %collective-permute-start.13 = (f32[80,128]{1,0:T(8,128)S(1)}, f32[80,128]{1,0:T(8,128)S(1)}, u32[]{:S(2)}, u32[]{:S(2)}) collective-permute-start(f32[80,128]{1,0:T(8,128)S(1)} %convert_reduce_fusion), channel_id=1, source_target_pairs={{0,0},{1,64},{2,32},{3,96},{4,4},{5,68},{6,36},{7,100},{8,8},{9,72... | collective-permute-start | bytes 122888 | tf_op jit(solution)/shard_map/ppermute | solution.py:397
  68.9 2.8 %collective-permute-start.16 = (f32[80,128]{1,0:T(8,128)S(1)}, f32[80,128]{1,0:T(8,128)S(1)}, u32[]{:S(2)}, u32[]{:S(2)}) collective-permute-start(f32[80,128]{1,0:T(8,128)S(1)} %collective-permute-done.15.y2), channel_id=1, source_target_pairs={{0,32},{32,0},{64,96},{96,64},{1,33},{33,1},{65,97},{97,65},{2,34}... | collective-permute-start | bytes 122888 | tf_op jit(solution)/shard_map/ppermute | solution.py:341
  71.2 1.3 %collective-permute-start.14 = (f32[80,128]{1,0:T(8,128)S(1)}, f32[80,128]{1,0:T(8,128)S(1)}, u32[]{:S(2)}, u32[]{:S(2)}) collective-permute-start(f32[80,128]{1,0:T(8,128)S(1)} %collective-permute-done.13.y0), channel_id=1, source_target_pairs={{0,32},{32,0},{64,96},{96,64},{1,33},{33,1},{65,97},{97,65},{2,34}... | collective-permute-start | bytes 122888 | tf_op jit(solution)/shard_map/ppermute | solution.py:341

commit v12 on v11

--- a/solution.py
+++ b/solution.py
@@ -75,18 +75,16 @@
     return (p // 2) * 8 + ((p % 2) * 2 + g % 2) * 2 + g // 2
 
 
-def window_kernel(off_ref, sel_ref, series_ref, e_ref, keep_ref, give_ref, w_ref):
+def window_kernel(off_ref, sel_ref, series_hbm, e_ref, keep_ref, give_ref, w_ref, series_ref, sems):
     j = lax.axis_index("subj")
     i = lax.axis_index("vox")
     width = series_ref.shape[2]
     lead = iota((TR, series_ref.shape[1]), 1) - iota((TR, series_ref.shape[1]), 0)
-    for s in range(SL):
-        for e in range(EP):
-            chosen = lead == off_ref[j * SL + s, e]
-            w_ref[e * TR : (e + 1) * TR, :] = jnp.where(chosen, 1.0, 0.0).astype(BF16)
-        rows = dot(w_ref[...], series_ref[s]).astype(BF16)
-        for e in range(EP):
-            e_ref[e, s * TR : (s + 1) * TR, :] = rows[e * TR : (e + 1) * TR]
+    copies = [
+        pltpu.make_async_copy(series_hbm.at[s], series_ref.at[s], sems.at[s]) for s in range(SL)
+    ]
+    for copy in copies:
+        copy.start()
     row = iota((GR * KL, 128), 0)
     column = jnp.zeros((GR * KL, 128), jnp.int32)
     for b, r in enumerate((0, 2, 1, 3)):
@@ -97,6 +95,14 @@
     picker = jnp.concatenate(
         [jnp.where(column == lane + c, 1.0, 0.0).astype(BF16) for c in range(0, width, 128)], axis=1
     )
+    for s in range(SL):
+        for e in range(EP):
+            chosen = lead == off_ref[j * SL + s, e]
+            w_ref[s % 2, e * TR : (e + 1) * TR, :] = jnp.where(chosen, 1.0, 0.0).astype(BF16)
+        copies[s].wait()
+        rows = dot(w_ref[s % 2], series_ref[s]).astype(BF16)
+        for e in range(EP):
+            e_ref[e, s * TR : (s + 1) * TR, :] = rows[e * TR : (e + 1) * TR]
     picked = dot_nt(picker, e_ref[...].reshape(EP * SL * TR, width)).astype(BF16)
     keep_ref[...] = picked[0 : 2 * KL]
     give_ref[...] = picked[2 * KL :]
@@ -114,10 +120,14 @@
         in_specs=[
             pl.BlockSpec(memory_space=pltpu.SMEM),
             pl.BlockSpec(memory_space=pltpu.SMEM),
-            pl.BlockSpec(memory_space=pltpu.VMEM),
+            pl.BlockSpec(memory_space=pltpu.HBM),
         ],
         out_specs=(pl.BlockSpec(memory_space=pltpu.VMEM),) * 3,
-        scratch_shapes=[pltpu.VMEM((EP * TR, series.shape[1]), BF16)],
+        scratch_shapes=[
+            pltpu.VMEM((2, EP * TR, series.shape[1]), BF16),
+            pltpu.VMEM(series.shape, BF16),
+            pltpu.SemaphoreType.DMA((SL,)),
+        ],
         compiler_params=pltpu.CompilerParams(vmem_limit_bytes=8 << 20),
         name="windows",
     )(

time: 74.9 us -> 75.9 us (1.013)
  Pallas kernels: 11 us -> 12 us
    pallas_call x1, Pallas kernels: 1.91 us -> 2.94 us  [take_windows(): pl.pallas_call(window_kernel, out_shape=(pltpu.VMEM((EP, SL * TR, width),...]
where the time goes in v12:
time: 75.9 us; the launch traced here: 74.7 us
  waiting for transfers between devices  22.2 us (29%)
  blocking collectives  20.1 us (26%)
  starting transfers between devices  19.9 us (26%)
  Pallas kernels  12 us (16%)
    all_to_all x1, blocking collectives, body(): lax.all_to_all(tiles.astype(LINK), ('subj', 'vox'), 0, 0, axis_index_grou...  20.1 us
    ppermute x6, waiting for transfers between devices, swapped(): return lax.ppermute(x, 'subj', [(n, n ^ r) for n in range(GR)])  14.6 us
    ppermute x6, starting transfers between devices, summed(): lax.ppermute(x, 'vox', [(n, n ^ step * stride) for n in range(devices)])  9.42 us
    ppermute x6, waiting for transfers between devices, summed(): lax.ppermute(x, 'vox', [(n, n ^ step * stride) for n in range(devices)])  5 us
    ppermute x2, starting transfers between devices, turned(): return lax.ppermute(tile, ('subj', 'vox'), moves)  4.78 us
    ppermute x3, starting transfers between devices, along_y(): return lax.ppermute(x, ('subj', 'vox'), moves)  4.78 us
    pallas_call x2, Pallas kernels, fishers(): pl.pallas_call(fisher_kernel, out_shape=pltpu.VMEM((EP, KL * PART, width)...  3.27 us
    pallas_call x1, Pallas kernels, partial_kernels(): pl.pallas_call(kernel_kernel, out_shape=pltpu.VMEM((devices, QUARTER, 2 *...  3.16 us
  transfers between devices with their start and end apart: 17, of which 7 were waited for; matrix products, arithmetic and copies ran while one was open for 0% of the time, Pallas kernels for 4%

profile of v12, /device:TPU:8, one launch (start us, length us, event | category | flops | bytes accessed | tf_op | source)
XLA Modules:
  0.0 74.7 jit_solution(13022618544387469948)
XLA Ops:
  0.0 2.9 %windows.1 = (bf16[12,64,512]{2,1,0:T(8,128)(2,1)S(1)}, bf16[32,768]{1,0:T(8,128)(2,1)S(1)}, bf16[32,768]{1,0:T(8,128)(2,1)S(1)}) custom-call(s32[16,12]{1,0:T(8,128)} %off_ref.1, s32[64]{0:T(128)} %sel_ref.1, bf16[4,256,512]{2,1,0:T(8,128)(2,1)} %series_hbm.1), custom_call_target="tpu_custom_call" | custom-call | tf_op jit(solution)/shard_map/windows/pallas_call | solution.py:113
  2.9 0.4 collective-permute-start.9
  3.4 0.0 collective-permute-start.1
  3.4 1.2 %collective-permute-done.1 = bf16[32,768]{1,0:T(8,128)(2,1)S(1)} collective-permute-done((bf16[32,768]{1,0:T(8,128)(2,1)S(1)}, bf16[32,768]{1,0:T(8,128)(2,1)S(1)}, u32[]{:S(2)}, u32[]{:S(2)}) %collective-permute-start.1) | collective-permute-done | bytes 49184 | tf_op jit(solution)/shard_map/ppermute | solution.py:351
  4.6 4.2 %collective-permute-start.3 = (bf16[64,768]{1,0:T(8,128)(2,1)S(1)}, bf16[64,768]{1,0:T(8,128)(2,1)S(1)}, u32[]{:S(2)}, u32[]{:S(2)}) collective-permute-start(bf16[64,768]{1,0:T(8,128)(2,1)S(1)} %pad_maximum_fusion), channel_id=1, source_target_pairs={{0,24},{1,25},{2,26},{3,27},{4,28},{5,29},{6,30},{7,31},{8,16},{9,... | collective-permute-start | bytes 294920 | tf_op jit(solution)/shard_map/ppermute | solution.py:356
  8.9 0.0 collective-permute-start.4
  8.9 0.9 %collective-permute-start.2 = (bf16[64,768]{1,0:T(8,128)(2,1)S(1)}, bf16[64,768]{1,0:T(8,128)(2,1)S(1)}, u32[]{:S(2)}, u32[]{:S(2)}) collective-permute-start(bf16[64,768]{1,0:T(8,128)(2,1)S(1)} %pad_maximum_fusion), channel_id=1, source_target_pairs={{0,8},{1,9},{2,10},{3,11},{4,12},{5,13},{6,14},{7,15},{8,0},{9,1},... | collective-permute-start | bytes 294920 | tf_op jit(solution)/shard_map/ppermute | solution.py:356
  9.8 12.5 %collective-permute-done.9.e0 = bf16[12,64,512]{2,1,0:T(8,128)(2,1)S(1)} collective-permute-done((bf16[12,64,512]{2,1,0:T(8,128)(2,1)S(1)}, bf16[12,64,512]{2,1,0:T(8,128)(2,1)S(1)}, u32[]{:S(2)}, u32[]{:S(2)}) %collective-permute-start.9) | collective-permute-done | bytes 786464 | tf_op jit(solution)/shard_map/ppermute | solution.py:351
  22.3 0.1 add_add_fusion.1
  22.4 3.1 %collective-permute-start.7 = (bf16[64,768]{1,0:T(8,128)(2,1)S(1)}, bf16[64,768]{1,0:T(8,128)(2,1)S(1)}, u32[]{:S(2)}, u32[]{:S(2)}) collective-permute-start(bf16[64,768]{1,0:T(8,128)(2,1)S(1)} %add_add_fusion.1), channel_id=1, source_target_pairs={{0,4},{1,5},{2,6},{3,7},{4,0},{5,1},{6,2},{7,3},{8,12},{9,13},{10,... | collective-permute-start | bytes 294920 | tf_op jit(solution)/shard_map/ppermute | solution.py:356
  25.5 1.1 %collective-permute-start.6 = (bf16[64,768]{1,0:T(8,128)(2,1)S(1)}, bf16[64,768]{1,0:T(8,128)(2,1)S(1)}, u32[]{:S(2)}, u32[]{:S(2)}) collective-permute-start(bf16[64,768]{1,0:T(8,128)(2,1)S(1)} %add_add_fusion.1), channel_id=1, source_target_pairs={{0,6},{1,7},{2,4},{3,5},{4,2},{5,3},{6,0},{7,1},{8,14},{9,15},{10,... | collective-permute-start | bytes 294920 | tf_op jit(solution)/shard_map/ppermute | solution.py:356
  26.6 2.5 %collective-permute-done.7 = bf16[64,768]{1,0:T(8,128)(2,1)S(1)} collective-permute-done((bf16[64,768]{1,0:T(8,128)(2,1)S(1)}, bf16[64,768]{1,0:T(8,128)(2,1)S(1)}, u32[]{:S(2)}, u32[]{:S(2)}) %collective-permute-start.7) | collective-permute-done | bytes 98336 | tf_op jit(solution)/shard_map/ppermute | solution.py:356
  29.2 2.4 %collective-permute-done.6 = bf16[64,768]{1,0:T(8,128)(2,1)S(1)} collective-permute-done((bf16[64,768]{1,0:T(8,128)(2,1)S(1)}, bf16[64,768]{1,0:T(8,128)(2,1)S(1)}, u32[]{:S(2)}, u32[]{:S(2)}) %collective-permute-start.6) | collective-permute-done | bytes 98336 | tf_op jit(solution)/shard_map/ppermute | solution.py:356
  31.7 2.4 %collective-permute-start.8 = (bf16[32,768]{1,0:T(8,128)(2,1)S(1)}, bf16[32,768]{1,0:T(8,128)(2,1)S(1)}, u32[]{:S(2)}, u32[]{:S(2)}) collective-permute-start(bf16[32,768]{1,0:T(8,128)(2,1)S(1)} %get-tuple-element.12.s0), channel_id=1, source_target_pairs={{0,1},{1,0},{2,3},{3,2},{4,5},{5,4},{6,7},{7,6},{8,9},{9,8},{10,11... | collective-permute-start | bytes 147464 | tf_op jit(solution)/shard_map/ppermute | solution.py:368
  34.1 2.4 %collective-permute-start.11 = (bf16[32,768]{1,0:T(8,128)(2,1)S(1)}, bf16[32,768]{1,0:T(8,128)(2,1)S(1)}, u32[]{:S(2)}, u32[]{:S(2)}) collective-permute-start(bf16[32,768]{1,0:T(8,128)(2,1)S(1)} %get-tuple-element.11), channel_id=1, source_target_pairs={{0,64},{1,65},{2,66},{3,67},{4,68},{5,69},{6,70},{7,71},{8,72},{9,... | collective-permute-start | bytes 147464 | tf_op jit(solution)/shard_map/ppermute | solution.py:368
  36.5 0.8 %norms.2.n_ref = f32[12,8,512]{2,1,0:T(8,128)S(1)} custom-call(bf16[12,64,512]{2,1,0:T(8,128)(2,1)S(1)} %get-tuple-element.8.e0, bf16[12,64,512]{2,1,0:T(8,128)(2,1)S(1)} %collective-permute-done.e1), custom_call_target="tpu_custom_call" | custom-call | tf_op jit(solution)/shard_map/norms/pallas_call | solution.py:158
  37.2 0.4 collective-permute-done.8.s1
  37.6 1.6 %fishers.2.fa = f32[12,128,512]{2,1,0:T(8,128)S(1)} custom-call(bf16[12,64,512]{2,1,0:T(8,128)(2,1)S(1)} %get-tuple-element.8.e0, bf16[12,64,512]{2,1,0:T(8,128)(2,1)S(1)} %collective-permute-done.e1, bf16[32,768]{1,0:T(8,128)(2,1)S(1)} %get-tuple-element.12.s0, bf16[32,768]{1,0:T(8,128)(2,1)S(1)} %collective-permute-done.8.s1, f32[12,8,512]{2,1,0:T(8,128)S(1)} %norms.2.n_ref), custom_call_target="tpu_custom_call" | custom-call | tf_op jit(solution)/shard_map/fishers/pallas_call | solution.py:206
  39.2 0.7 %norms.3.n_ref = f32[12,8,512]{2,1,0:T(8,128)S(1)} custom-call(bf16[12,64,512]{2,1,0:T(8,128)(2,1)S(1)} %collective-permute-done.9.e0, bf16[12,64,512]{2,1,0:T(8,128)(2,1)S(1)} %collective-permute-done.10.e1), custom_call_target="tpu_custom_call" | custom-call | tf_op jit(solution)/shard_map/norms/pallas_call | solution.py:158
  40.0 0.0 collective-permute-done.11.s0
  40.0 1.6 %fishers.3.fb = f32[12,128,512]{2,1,0:T(8,128)S(1)} custom-call(bf16[12,64,512]{2,1,0:T(8,128)(2,1)S(1)} %collective-permute-done.9.e0, bf16[12,64,512]{2,1,0:T(8,128)(2,1)S(1)} %collective-permute-done.10.e1, bf16[32,768]{1,0:T(8,128)(2,1)S(1)} %collective-permute-done.11.s0, bf16[32,768]{1,0:T(8,128)(2,1)S(1)} %collective-permute-done.12.s1, ...), custom_call_target="tpu_custom_call" | custom-call | tf_op jit(solution)/shard_map/fishers/pallas_call | solution.py:206
  41.6 3.2 %partial_kernels.1 = f32[32,80,128]{2,1,0:T(8,128)S(1)} custom-call(f32[12,128,512]{2,1,0:T(8,128)S(1)} %fishers.2.fa, f32[12,128,512]{2,1,0:T(8,128)S(1)} %fishers.3.fb), custom_call_target="tpu_custom_call" | custom-call | tf_op jit(solution)/shard_map/partial_kernels/pallas_call | solution.py:280
  44.8 0.1 convert_element_type.6
  44.9 20.1 %all_to_all.5 = f16[32,80,128]{2,1,0:T(8,128)(2,1)S(1)} all-to-all(f16[32,80,128]{2,1,0:T(8,128)(2,1)S(1)} %convert_element_type.6), channel_id=1, replica_groups={{31,23,30,22,10,21,7,24,17,0,15,14,1,19,5,13,20,27,8,4,18,9,26,11,12,6,..., dimensions={0} | all-to-all | bytes 1310720 | tf_op jit(solution)/shard_map/all_to_all | solution.py:391
  65.0 0.1 convert_reduce_fusion
  65.1 1.3 %collective-permute-start.15 = (f32[80,128]{1,0:T(8,128)S(1)}, f32[80,128]{1,0:T(8,128)S(1)}, u32[]{:S(2)}, u32[]{:S(2)}) collective-permute-start(f32[80,128]{1,0:T(8,128)S(1)} %convert_reduce_fusion), channel_id=1, source_target_pairs={{0,64},{1,0},{2,96},{3,32},{4,68},{5,4},{6,100},{7,36},{8,72},{9,8... | collective-permute-start | bytes 122888 | tf_op jit(solution)/shard_map/ppermute | solution.py:407
  66.4 3.5 %collective-permute-start.13 = (f32[80,128]{1,0:T(8,128)S(1)}, f32[80,128]{1,0:T(8,128)S(1)}, u32[]{:S(2)}, u32[]{:S(2)}) collective-permute-start(f32[80,128]{1,0:T(8,128)S(1)} %convert_reduce_fusion), channel_id=1, source_target_pairs={{0,0},{1,64},{2,32},{3,96},{4,4},{5,68},{6,36},{7,100},{8,8},{9,72... | collective-permute-start | bytes 122888 | tf_op jit(solution)/shard_map/ppermute | solution.py:407
  69.9 0.1 collective-permute-start.16
  70.0 2.3 %collective-permute-done.13.y0 = f32[80,128]{1,0:T(8,128)S(1)} collective-permute-done((f32[80,128]{1,0:T(8,128)S(1)}, f32[80,128]{1,0:T(8,128)S(1)}, u32[]{:S(2)}, u32[]{:S(2)}) %collective-permute-start.13) | collective-permute-done | bytes 40992 | tf_op jit(solution)/shard_map/ppermute | solution.py:407
  72.2 0.4 collective-permute-start.14
  72.7 0.9 %collective-permute-done.14.y1 = f32[80,128]{1,0:T(8,128)S(1)} collective-permute-done((f32[80,128]{1,0:T(8,128)S(1)}, f32[80,128]{1,0:T(8,128)S(1)}, u32[]{:S(2)}, u32[]{:S(2)}) %collective-permute-start.14) | collective-permute-done | bytes 40992 | tf_op jit(solution)/shard_map/ppermute | solution.py:351
  73.5 1.2 %in_order.1 = f32[2,48,192]{2,1,0:T(8,128)} custom-call(f32[80,128]{1,0:T(8,128)S(1)} %collective-permute-done.13.y0, f32[80,128]{1,0:T(8,128)S(1)} %collective-permute-done.14.y1, f32[80,128]{1,0:T(8,128)S(1)} %collective-permute-done.15.y2, f32[80,128]{1,0:T(8,128)S(1)} %collective-permute-done.16.y3), custom_call_target="tpu_custom_call" | custom-call | tf_op jit(solution)/shard_map/in_order/pallas_call | solution.py:336
  (18 shorter events, 0.1 us)
Async XLA Ops:
  2.9 19.4 %collective-permute-start.9 = (bf16[12,64,512]{2,1,0:T(8,128)(2,1)S(1)}, bf16[12,64,512]{2,1,0:T(8,128)(2,1)S(1)}, u32[]{:S(2)}, u32[]{:S(2)}) collective-permute-start(bf16[12,64,512]{2,1,0:T(8,128)(2,1)S(1)} %get-tuple-element.8.e0), channel_id=1, source_target_pairs={{0,64},{32,96},{64,0},{96,32},{1,65},{33,97},{65,1},{97,33},{2,66}... | collective-permute-start | bytes 2359304 | tf_op jit(solution)/shard_map/ppermute | solution.py:351
  3.4 1.2 %collective-permute-start.1 = (bf16[32,768]{1,0:T(8,128)(2,1)S(1)}, bf16[32,768]{1,0:T(8,128)(2,1)S(1)}, u32[]{:S(2)}, u32[]{:S(2)}) collective-permute-start(bf16[32,768]{1,0:T(8,128)(2,1)S(1)} %get-tuple-element.10), channel_id=1, source_target_pairs={{0,32},{32,0},{64,96},{96,64},{1,33},{33,1},{65,97},{97,65},{2,34}... | collective-permute-start | bytes 147464 | tf_op jit(solution)/shard_map/ppermute | solution.py:351
  4.6 17.7 %collective-permute-start.3 = (bf16[64,768]{1,0:T(8,128)(2,1)S(1)}, bf16[64,768]{1,0:T(8,128)(2,1)S(1)}, u32[]{:S(2)}, u32[]{:S(2)}) collective-permute-start(bf16[64,768]{1,0:T(8,128)(2,1)S(1)} %pad_maximum_fusion), channel_id=1, source_target_pairs={{0,24},{1,25},{2,26},{3,27},{4,28},{5,29},{6,30},{7,31},{8,16},{9,... | collective-permute-start | bytes 294920 | tf_op jit(solution)/shard_map/ppermute | solution.py:356
  8.9 13.5 %collective-permute-start.4 = (bf16[64,768]{1,0:T(8,128)(2,1)S(1)}, bf16[64,768]{1,0:T(8,128)(2,1)S(1)}, u32[]{:S(2)}, u32[]{:S(2)}) collective-permute-start(bf16[64,768]{1,0:T(8,128)(2,1)S(1)} %pad_maximum_fusion), channel_id=1, source_target_pairs={{0,16},{1,17},{2,18},{3,19},{4,20},{5,21},{6,22},{7,23},{8,24},{9,... | collective-permute-start | bytes 294920 | tf_op jit(solution)/shard_map/ppermute | solution.py:356
  8.9 13.5 %collective-permute-start.2 = (bf16[64,768]{1,0:T(8,128)(2,1)S(1)}, bf16[64,768]{1,0:T(8,128)(2,1)S(1)}, u32[]{:S(2)}, u32[]{:S(2)}) collective-permute-start(bf16[64,768]{1,0:T(8,128)(2,1)S(1)} %pad_maximum_fusion), channel_id=1, source_target_pairs={{0,8},{1,9},{2,10},{3,11},{4,12},{5,13},{6,14},{7,15},{8,0},{9,1},... | collective-permute-start | bytes 294920 | tf_op jit(solution)/shard_map/ppermute | solution.py:356
  9.8 26.7 %collective-permute-start = (bf16[12,64,512]{2,1,0:T(8,128)(2,1)S(1)}, bf16[12,64,512]{2,1,0:T(8,128)(2,1)S(1)}, u32[]{:S(2)}, u32[]{:S(2)}) collective-permute-start(bf16[12,64,512]{2,1,0:T(8,128)(2,1)S(1)} %get-tuple-element.8.e0), channel_id=1, source_target_pairs={{0,32},{32,0},{64,96},{96,64},{1,33},{33,1},{65,97},{97,65},{2,34}... | collective-permute-start | bytes 2359304 | tf_op jit(solution)/shard_map/ppermute | solution.py:351
  22.3 16.9 %collective-permute-start.10 = (bf16[12,64,512]{2,1,0:T(8,128)(2,1)S(1)}, bf16[12,64,512]{2,1,0:T(8,128)(2,1)S(1)}, u32[]{:S(2)}, u32[]{:S(2)}) collective-permute-start(bf16[12,64,512]{2,1,0:T(8,128)(2,1)S(1)} %collective-permute-done.9.e0), channel_id=1, source_target_pairs={{0,32},{32,0},{64,96},{96,64},{1,33},{33,1},{65,97},{97,65},{2,34}... | collective-permute-start | bytes 2359304 | tf_op jit(solution)/shard_map/ppermute | solution.py:351
  22.4 6.8 %collective-permute-start.7 = (bf16[64,768]{1,0:T(8,128)(2,1)S(1)}, bf16[64,768]{1,0:T(8,128)(2,1)S(1)}, u32[]{:S(2)}, u32[]{:S(2)}) collective-permute-start(bf16[64,768]{1,0:T(8,128)(2,1)S(1)} %add_add_fusion.1), channel_id=1, source_target_pairs={{0,4},{1,5},{2,6},{3,7},{4,0},{5,1},{6,2},{7,3},{8,12},{9,13},{10,... | collective-permute-start | bytes 294920 | tf_op jit(solution)/shard_map/ppermute | solution.py:356
  25.5 6.1 %collective-permute-start.6 = (bf16[64,768]{1,0:T(8,128)(2,1)S(1)}, bf16[64,768]{1,0:T(8,128)(2,1)S(1)}, u32[]{:S(2)}, u32[]{:S(2)}) collective-permute-start(bf16[64,768]{1,0:T(8,128)(2,1)S(1)} %add_add_fusion.1), channel_id=1, source_target_pairs={{0,6},{1,7},{2,4},{3,5},{4,2},{5,3},{6,0},{7,1},{8,14},{9,15},{10,... | collective-permute-start | bytes 294920 | tf_op jit(solution)/shard_map/ppermute | solution.py:356
  26.6 5.0 %collective-permute-start.5 = (bf16[64,768]{1,0:T(8,128)(2,1)S(1)}, bf16[64,768]{1,0:T(8,128)(2,1)S(1)}, u32[]{:S(2)}, u32[]{:S(2)}) collective-permute-start(bf16[64,768]{1,0:T(8,128)(2,1)S(1)} %add_add_fusion.1), channel_id=1, source_target_pairs={{0,2},{1,3},{2,0},{3,1},{4,6},{5,7},{6,4},{7,5},{8,10},{9,11},{10,... | collective-permute-start | bytes 294920 | tf_op jit(solution)/shard_map/ppermute | solution.py:356
  31.7 5.9 %collective-permute-start.8 = (bf16[32,768]{1,0:T(8,128)(2,1)S(1)}, bf16[32,768]{1,0:T(8,128)(2,1)S(1)}, u32[]{:S(2)}, u32[]{:S(2)}) collective-permute-start(bf16[32,768]{1,0:T(8,128)(2,1)S(1)} %get-tuple-element.12.s0), channel_id=1, source_target_pairs={{0,1},{1,0},{2,3},{3,2},{4,5},{5,4},{6,7},{7,6},{8,9},{9,8},{10,11... | collective-permute-start | bytes 147464 | tf_op jit(solution)/shard_map/ppermute | solution.py:368
  34.1 5.9 %collective-permute-start.12 = (bf16[32,768]{1,0:T(8,128)(2,1)S(1)}, bf16[32,768]{1,0:T(8,128)(2,1)S(1)}, u32[]{:S(2)}, u32[]{:S(2)}) collective-permute-start(bf16[32,768]{1,0:T(8,128)(2,1)S(1)} %get-tuple-element.11), channel_id=1, source_target_pairs={{0,65},{1,64},{2,67},{3,66},{4,69},{5,68},{6,71},{7,70},{8,73},{9,... | collective-permute-start | bytes 147464 | tf_op jit(solution)/shard_map/ppermute | solution.py:368
  34.1 5.9 %collective-permute-start.11 = (bf16[32,768]{1,0:T(8,128)(2,1)S(1)}, bf16[32,768]{1,0:T(8,128)(2,1)S(1)}, u32[]{:S(2)}, u32[]{:S(2)}) collective-permute-start(bf16[32,768]{1,0:T(8,128)(2,1)S(1)} %get-tuple-element.11), channel_id=1, source_target_pairs={{0,64},{1,65},{2,66},{3,67},{4,68},{5,69},{6,70},{7,71},{8,72},{9,... | collective-permute-start | bytes 147464 | tf_op jit(solution)/shard_map/ppermute | solution.py:368
  65.1 4.8 %collective-permute-start.15 = (f32[80,128]{1,0:T(8,128)S(1)}, f32[80,128]{1,0:T(8,128)S(1)}, u32[]{:S(2)}, u32[]{:S(2)}) collective-permute-start(f32[80,128]{1,0:T(8,128)S(1)} %convert_reduce_fusion), channel_id=1, source_target_pairs={{0,64},{1,0},{2,96},{3,32},{4,68},{5,4},{6,100},{7,36},{8,72},{9,8... | collective-permute-start | bytes 122888 | tf_op jit(solution)/shard_map/ppermute | solution.py:407
  66.4 5.9 %collective-permute-start.13 = (f32[80,128]{1,0:T(8,128)S(1)}, f32[80,128]{1,0:T(8,128)S(1)}, u32[]{:S(2)}, u32[]{:S(2)}) collective-permute-start(f32[80,128]{1,0:T(8,128)S(1)} %convert_reduce_fusion), channel_id=1, source_target_pairs={{0,0},{1,64},{2,32},{3,96},{4,4},{5,68},{6,36},{7,100},{8,8},{9,72... | collective-permute-start | bytes 122888 | tf_op jit(solution)/shard_map/ppermute | solution.py:407
  69.9 2.8 %collective-permute-start.16 = (f32[80,128]{1,0:T(8,128)S(1)}, f32[80,128]{1,0:T(8,128)S(1)}, u32[]{:S(2)}, u32[]{:S(2)}) collective-permute-start(f32[80,128]{1,0:T(8,128)S(1)} %collective-permute-done.15.y2), channel_id=1, source_target_pairs={{0,32},{32,0},{64,96},{96,64},{1,33},{33,1},{65,97},{97,65},{2,34}... | collective-permute-start | bytes 122888 | tf_op jit(solution)/shard_map/ppermute | solution.py:351
  72.2 1.3 %collective-permute-start.14 = (f32[80,128]{1,0:T(8,128)S(1)}, f32[80,128]{1,0:T(8,128)S(1)}, u32[]{:S(2)}, u32[]{:S(2)}) collective-permute-start(f32[80,128]{1,0:T(8,128)S(1)} %collective-permute-done.13.y0), channel_id=1, source_target_pairs={{0,32},{32,0},{64,96},{96,64},{1,33},{33,1},{65,97},{97,65},{2,34}... | collective-permute-start | bytes 122888 | tf_op jit(solution)/shard_map/ppermute | solution.py:351
